TPU v7x, 128 devices: a whole 4x4x4 slice. The times are simulated.
128 devices in a mesh: ctx: 8 (over z_lo, y), tp: 16 (over z_hi, x, core).
Axes of the slice: x: 4, y: 4, z: 4 (z_hi: 2, z_lo: 2; z = z_hi * 2 + z_lo), core: 2. Of those that a mesh axis runs over, the one named last changes fastest.
Arguments:
- queries: bfloat16 [8192, 8192], P('ctx', 'tp'), may hold values from -64 to 64
- context_keys: bfloat16 [8192, 1024], P('ctx'), may hold values from -6 to 6
- context_values: bfloat16 [8192, 1024], P('ctx'), may hold values from -6 to 6
- positions: int32 [8192], P('ctx'), may hold values from 0 to 8191, as said below
- out_weight: bfloat16 [8192, 8192], P('tp'), may hold values from -0.5 to 0.5
- residual_in: bfloat16 [8192, 8192], P(('ctx', 'tp')), may hold values from -3 to 3
- norm_gain: float32 [8192], replicated, may hold values from 0.5 to 1.5
- static_scale: float32 [1], replicated, may hold values from 0.004 to 0.009
Outputs:
- hidden_out: bfloat16 [8192, 8192], P(('ctx', 'tp'))
- clipped: bfloat16 [8192, 8192], P(('ctx', 'tp'))
Inputs may be any that keep to these rules, and one draw needn't show every extreme that they name: Rows fall into aligned runs of 512 rows that hold consecutive positions in increasing order; all positions together are a permutation of 0 to 8191.
All inputs are finite; a program needn't handle non-finite values.
Results may differ from a plain program's by a relative error of at most 0.017.
Values may be sent and summed in bfloat16 or wider, within the bound.
No kernel may reach another device: no remote copies, remote signals or barrier semaphores. Data moves between devices by JAX's collectives and lax.ppermute only.
A program may use at most 128 MiB of HBM per device.

v0:
```python
import functools
import math

import jax
import jax.numpy as jnp
from jax import lax
from jax.experimental import pallas as pl
from jax.experimental.pallas import tpu as pltpu
from jax.sharding import PartitionSpec as P


HD = 128
SPAN = 512
GW = 256
MASKED = -1e30
LOG2_SCALE = math.log2(math.e) / math.sqrt(HD)
PARTS = 2
Y_COUNT = 4
X_COUNT = 4
ANY = pl.ANY


def attend_kernel(
    own_ref, loc_ref, core_ref, q_ref, first_ref, second_ref, out_ref,
    k_ref, v_ref, vt_ref, qt_ref, acc_ref, max_ref, sum_ref, top_ref, factor_ref, sems, *tile_refs,
    rows, part, heads, run,
):
    span = pl.program_id(0)
    slots = first_ref.shape[0]
    block_rows = k_ref.shape[0] // slots
    nrow = q_ref.shape[0] * rows
    groups = nrow * heads // GW
    score_refs, weight_refs = tile_refs[:groups], tile_refs[groups:]

    @pl.when(span == 0)
    def _():
        def fetch(k_src, v_src):
            copies = []
            for s in range(slots):
                dst = pl.ds(s * block_rows, block_rows)
                copies.append(pltpu.make_async_copy(k_src.at[s, pl.ds(0, block_rows)], k_ref.at[dst], sems.at[s]))
                copies.append(pltpu.make_async_copy(v_src.at[s, pl.ds(0, block_rows)], v_ref.at[dst], sems.at[slots + s]))
            for c in copies:
                c.start()
            for c in copies:
                c.wait()

        @pl.when(core_ref[0] == 0)
        def _():
            fetch(first_ref, second_ref)

        @pl.when(core_ref[0] != 0)
        def _():
            fetch(second_ref, first_ref)

        for b in range(k_ref.shape[0] // SPAN):
            vt_ref[b] = v_ref[b * SPAN:(b + 1) * SPAN, :].T

    own = own_ref[span]
    q_all = q_ref[...].reshape(nrow, heads * HD)
    for h in range(heads):
        qt_ref[:, h * nrow:(h + 1) * nrow] = q_all[:, h * HD:(h + 1) * HD].T

    def score(blk, g):
        keys = k_ref[pl.ds(pl.multiple_of(blk * SPAN, SPAN), SPAN), :]
        s = jnp.dot(keys, qt_ref[:, g * GW:(g + 1) * GW], preferred_element_type=jnp.float32)
        score_refs[g][...] = s
        top_ref[g] = jnp.max(s.reshape(SPAN // 8, 8, GW), axis=0)

    def weigh(s, top, g):
        old = max_ref[g]
        new = jnp.maximum(old, jnp.broadcast_to(jnp.max(top, axis=0, keepdims=True), old.shape))
        max_ref[g] = new
        p = jnp.exp2(s.reshape(SPAN // 8, 8, GW) * LOG2_SCALE - (new * LOG2_SCALE)[None])
        factor = jnp.exp2((old - new) * LOG2_SCALE)
        factor_ref[g] = factor
        sum_ref[g] = sum_ref[g] * factor + jnp.sum(p, axis=0)
        weight_refs[g][...] = p.reshape(SPAN, GW).astype(jnp.bfloat16)

    def apply(blk, g):
        pv = jnp.dot(vt_ref[blk], weight_refs[g][...], preferred_element_type=jnp.float32)
        acc_ref[g] = acc_ref[g] * factor_ref[g][None] + pv.reshape(HD // 8, 8, GW)

    max_ref[...] = jnp.full_like(max_ref, MASKED)
    sum_ref[...] = jnp.zeros_like(sum_ref)
    acc_ref[...] = jnp.zeros_like(acc_ref)
    factor_ref[...] = jnp.zeros_like(factor_ref)
    for g in range(groups):
        weight_refs[g][...] = jnp.zeros_like(weight_refs[g])
        score(loc_ref[0], g)

    def body(t, carry):
        prev = loc_ref[jnp.maximum(t - 1, 0)]
        for g in range(groups):
            apply(prev, g)
            weigh(score_refs[g][...], top_ref[g], g)
            score(loc_ref[t + 1], g)
        return carry

    lax.fori_loop(0, own, body, 0)
    prev = loc_ref[jnp.maximum(own - 1, 0)]
    key_i = lax.broadcasted_iota(jnp.int32, (SPAN, GW), 0)
    col_i = lax.broadcasted_iota(jnp.int32, (SPAN, GW), 1)
    for g in range(groups):
        apply(prev, g)
        r = (col_i + g * GW) & (nrow - 1)
        row_i = (r >> (rows.bit_length() - 1)) * run + part * rows + (r & (rows - 1))
        s = jnp.where(key_i <= row_i, score_refs[g][...], MASKED)
        weigh(s, jnp.max(s.reshape(SPAN // 8, 8, GW), axis=0), g)
    for g in range(groups):
        apply(loc_ref[own], g)
    for g in range(groups):
        total = jnp.sum(sum_ref[g], axis=0, keepdims=True)
        done = (acc_ref[g].reshape(HD, GW) * (1.0 / total)).T.astype(jnp.bfloat16)
        n = min(nrow, GW)
        for c in range(0, GW, n):
            h, r0 = divmod(g * GW + c, nrow)
            out_ref[r0 // rows:(r0 + n) // rows, :, h * HD:(h + 1) * HD] = done[c:c + n].reshape(n // rows, rows, HD)


def attend(own, loc, core, queries, first, second, part, tp_count):
    tok, width = queries.shape
    heads = width // HD
    run = tok // tp_count
    rows = run // PARTS
    spans = tok // SPAN
    per = tp_count // spans
    slots = first.shape[0]
    keys = slots * tok
    groups = per * rows * heads // GW
    pairs = heads * rows * per * spans * keys
    return pl.pallas_call(
        functools.partial(attend_kernel, rows=rows, part=part, heads=heads, run=run),
        out_shape=jax.ShapeDtypeStruct((tp_count, rows, width), jnp.bfloat16),
        grid_spec=pltpu.PrefetchScalarGridSpec(
            num_scalar_prefetch=3,
            grid=(spans,),
            in_specs=[
                pl.BlockSpec((per, rows, width), lambda s, *_: (s, part, 0)),
                pl.BlockSpec(memory_space=ANY),
                pl.BlockSpec(memory_space=ANY),
            ],
            out_specs=pl.BlockSpec((per, rows, width), lambda s, *_: (s, 0, 0)),
            scratch_shapes=[
                pltpu.VMEM((keys, HD), jnp.bfloat16),
                pltpu.VMEM((keys, HD), jnp.bfloat16),
                pltpu.VMEM((keys // SPAN, HD, SPAN), jnp.bfloat16),
                pltpu.VMEM((HD, per * rows * heads), jnp.bfloat16),
                pltpu.VMEM((groups, HD // 8, 8, GW), jnp.float32),
                pltpu.VMEM((groups, 8, GW), jnp.float32),
                pltpu.VMEM((groups, 8, GW), jnp.float32),
                pltpu.VMEM((groups, 8, GW), jnp.float32),
                pltpu.VMEM((groups, 8, GW), jnp.float32),
                pltpu.SemaphoreType.DMA((2 * slots,)),
            ]
            + [pltpu.VMEM((SPAN, GW), jnp.float32)] * groups
            + [pltpu.VMEM((SPAN, GW), jnp.bfloat16)] * groups,
        ),
        compiler_params=pltpu.CompilerParams(dimension_semantics=("arbitrary",), vmem_limit_bytes=40 * 2**20),
        cost_estimate=pl.CostEstimate(flops=8 * HD * pairs, bytes_accessed=4 * keys * HD, transcendentals=pairs),
    )(own, loc, core, queries.reshape(tp_count, run, width), first, second)


def project_kernel(x_ref, *refs):
    att_refs, w_refs, out_refs = refs[:4], refs[4:8], refs[8:]
    step = pl.program_id(0)
    rows = out_refs[0].shape[0]
    total = None
    for a, w in zip(att_refs, w_refs):
        term = jnp.dot(a[...].reshape(rows, a.shape[-1]), w[...], preferred_element_type=jnp.float32)
        total = term if total is None else total + term
    for i, o in enumerate(out_refs):
        @pl.when(step == i)
        def _(o=o):
            o[...] = total.astype(jnp.bfloat16)


def project(x_rank, atts, ws):
    tps, r, k = atts[0].shape
    cores = tps // (2 * X_COUNT)
    n = ws[0].shape[1]
    rows = 2 * cores * r
    views = [a.reshape(2, X_COUNT, cores * r, k) for a in atts]
    pick = lambda i, x: (0, (x[0] + i) % X_COUNT, 0, 0)
    return pl.pallas_call(
        project_kernel,
        out_shape=[jax.ShapeDtypeStruct((rows, n), jnp.bfloat16)] * X_COUNT,
        grid_spec=pltpu.PrefetchScalarGridSpec(
            num_scalar_prefetch=1,
            grid=(X_COUNT,),
            in_specs=[pl.BlockSpec((2, 1, cores * r, k), pick)] * 4 + [pl.BlockSpec((k, n), lambda i, x: (0, 0))] * 4,
            out_specs=[pl.BlockSpec((rows, n), lambda i, x: (0, 0))] * X_COUNT,
        ),
        compiler_params=pltpu.CompilerParams(dimension_semantics=("arbitrary",), vmem_limit_bytes=56 * 2**20),
        cost_estimate=pl.CostEstimate(flops=2 * rows * X_COUNT * 4 * k * n, bytes_accessed=8 * k * n, transcendentals=0),
        name="project",
    )(x_rank, *views, *ws)


def gather_kernel(m_ref, *refs):
    ins, outs = refs[:4], refs[4:]
    step = pl.program_id(0)
    total = ins[0][...].astype(jnp.float32)
    for i in ins[1:]:
        total = total + i[...].astype(jnp.float32)
    for i, o in enumerate(outs):
        @pl.when(step == i)
        def _(o=o):
            o[...] = total.astype(jnp.bfloat16)


def add_parts(member, parts):
    rows, n = parts[0].shape
    r = rows // 4
    return pl.pallas_call(
        gather_kernel,
        out_shape=[jax.ShapeDtypeStruct((r, n), jnp.bfloat16)] * 4,
        grid_spec=pltpu.PrefetchScalarGridSpec(
            num_scalar_prefetch=1,
            grid=(4,),
            in_specs=[pl.BlockSpec((r, n), lambda i, m: (m[0] ^ i, 0))] * 4,
            out_specs=[pl.BlockSpec((r, n), lambda i, m: (0, 0))] * 4,
        ),
        compiler_params=pltpu.CompilerParams(dimension_semantics=("arbitrary",)),
        cost_estimate=pl.CostEstimate(flops=4 * rows * n, bytes_accessed=10 * rows * n, transcendentals=0),
        name="add_parts",
    )(member, *parts)


def finish_kernel(m_ref, scale_ref, res_ref, gain_ref, *refs):
    parts, (hidden_ref, clipped_ref, tmp_ref) = refs[:4], refs[4:]
    n = parts[0].shape[1]
    square = None
    for i, part in enumerate(parts):
        cols = pl.ds(pl.multiple_of((m_ref[0] ^ i) * n, n), n)
        s = res_ref[:, cols].astype(jnp.float32) + part[...].astype(jnp.float32)
        tmp_ref[:, cols] = s
        hidden_ref[:, cols] = s.astype(jnp.bfloat16)
        t = jnp.sum(s * s, axis=1, keepdims=True)
        square = t if square is None else square + t
    inv = lax.rsqrt(square / (4 * n) + 1e-05)
    limit = 448.0 * scale_ref[0]
    clipped_ref[...] = jnp.clip(tmp_ref[...] * inv * gain_ref[...], -limit, limit).astype(jnp.bfloat16)


def finish(member, static_scale, residual, gain, parts, part, before):
    rows, width = residual.shape
    r = rows // PARTS
    whole = pl.BlockSpec((r, width), lambda i, *_: (part, 0))
    small = pl.BlockSpec(parts[0].shape, lambda i, *_: (0, 0))
    kernel = finish_kernel
    if before:
        kernel = lambda m, s, res, g, a, b, c, d, e, f, *rest: finish_kernel(m, s, res, g, a, b, c, d, *rest)
    return pl.pallas_call(
        kernel,
        out_shape=[jax.ShapeDtypeStruct((rows, width), jnp.bfloat16)] * 2,
        grid_spec=pltpu.PrefetchScalarGridSpec(
            num_scalar_prefetch=2,
            grid=(1,),
            in_specs=[whole, pl.BlockSpec((1, width), lambda i, *_: (0, 0))]
            + [small] * 4
            + [pl.BlockSpec(memory_space=ANY)] * len(before),
            out_specs=[whole] * 2,
            scratch_shapes=[pltpu.VMEM((r, width), jnp.float32)],
        ),
        input_output_aliases={8 + i: i for i in range(len(before))},
        cost_estimate=pl.CostEstimate(flops=8 * r * width, bytes_accessed=10 * r * width, transcendentals=0),
    )(member, static_scale, residual, gain, *parts, *before)


def swapped(value, mask, count):
    return lax.ppermute(value, "tp", [(i, i ^ mask) for i in range(count)])


def shards(
    queries,
    context_keys,
    context_values,
    positions,
    out_weight,
    residual_in,
    norm_gain,
    static_scale,
):
    ctx_count = lax.axis_size("ctx")
    tp_count = lax.axis_size("tp")
    tp_rank = lax.axis_index("tp").astype(jnp.int32)
    tok, _ = queries.shape
    core = tp_rank & 1
    x_rank = (tp_rank >> 1) & (X_COUNT - 1)
    far = tp_count // 2
    member = (tp_rank // far) * 2 + core
    masks = (0, 1, far, far + 1)

    kv_col = (tp_rank >> 1) * HD
    mine = jnp.where(
        core == 0,
        lax.dynamic_slice_in_dim(context_keys, kv_col, HD, 1),
        lax.dynamic_slice_in_dim(context_values, kv_col, HD, 1),
    )
    spans = tok // SPAN
    own = positions[::SPAN] // SPAN
    tag = jnp.pad(own.astype(jnp.bfloat16)[:, None] * jnp.ones((1, HD), jnp.bfloat16), ((0, 16 - spans), (0, 0)))
    mine = jnp.concatenate([mine, tag], axis=0)
    pieces = [mine]
    for dz in range(ctx_count // Y_COUNT):
        for dy in (0, 2, 1, 3):
            if dz or dy:
                pairs = [
                    (c, (c // Y_COUNT ^ dz) * Y_COUNT + (c + dy) % Y_COUNT) for c in range(ctx_count)
                ]
                pieces.append(lax.ppermute(mine, "ctx", pairs))
    first = jnp.stack(pieces)
    second = swapped(first, 1, tp_count)
    order = first[:, tok:tok + spans, 0].reshape(ctx_count * spans).astype(jnp.int32)
    blocks = jnp.arange(ctx_count * spans, dtype=jnp.int32)
    loc = jnp.sum(jnp.where(order[None, :] == blocks[:, None], blocks[None, :], 0), axis=1)

    quarter = out_weight.shape[1] // 4
    ws = []
    for i, mask in enumerate(masks):
        w = lax.dynamic_slice_in_dim(out_weight, (member ^ i) * quarter, quarter, 1)
        ws.append(swapped(w, mask, tp_count) if mask else w)

    outs = ()
    for part in range(PARTS):
        att = attend(own, loc, core[None], queries, first, second, part, tp_count)
        atts = []
        for mask in masks:
            atts.append(swapped(att, mask, tp_count) if mask else att)
        sent = project(x_rank[None], atts, ws)
        got = [sent[0]]
        for dx in (2, 1, 3):
            pairs = []
            for t in range(tp_count):
                x = (t >> 1) & (X_COUNT - 1)
                pairs.append((t, t - 2 * x + 2 * ((x + dx) % X_COUNT)))
            got.append(lax.ppermute(sent[dx], "tp", pairs))
        cols = list(add_parts(member[None], got))
        for i, mask in enumerate(masks):
            if mask:
                cols[i] = swapped(cols[i], mask, tp_count)
        outs = finish(member[None], static_scale, residual_in, norm_gain[None, :], cols, part, outs)
    return tuple(outs)


def solution(mesh):
    return jax.shard_map(
        shards,
        mesh=mesh,
        in_specs=(
            P("ctx", "tp"),
            P("ctx", None),
            P("ctx", None),
            P("ctx"),
            P("tp", None),
            P(("ctx", "tp"), None),
            P(),
            P(),
        ),
        out_specs=(P(("ctx", "tp"), None), P(("ctx", "tp"), None)),
        check_vma=False,
    )
```

profile of v0, /device:TPU:0, one launch (start us, length us, event | category | flops | bytes accessed | tf_op | source)
XLA Modules:
  0.0 249.6 jit_solution(12468371076464534136)
XLA Ops:
  2.8 3.1 %collective-permute-start.5 = (bf16[1040,128]{1,0:T(8,128)(2,1)S(1)}, bf16[1040,128]{1,0:T(8,128)(2,1)S(1)}, u32[]{:S(2)}, u32[]{:S(2)}) collective-permute-start(bf16[1040,128]{1,0:T(8,128)(2,1)S(1)} %pad_maximum_fusion), channel_id=1, source_target_pairs={{0,80},{16,96},{32,112},{48,64},{64,16},{80,32},{96,48},{112,0},{1... | collective-permute-start | bytes 798728 | tf_op jit(solution)/shard_map/ppermute | solution.py:312
  12.1 17.9 %collective-permute-done = bf16[1040,128]{1,0:T(8,128)(2,1)S(1)} collective-permute-done((bf16[1040,128]{1,0:T(8,128)(2,1)S(1)}, bf16[1040,128]{1,0:T(8,128)(2,1)S(1)}, u32[]{:S(2)}, u32[]{:S(2)}) %collective-permute-start) | collective-permute-done | bytes 266272 | tf_op jit(solution)/shard_map/ppermute | solution.py:312
  30.0 8.4 %collective-permute-done.1 = bf16[1040,128]{1,0:T(8,128)(2,1)S(1)} collective-permute-done((bf16[1040,128]{1,0:T(8,128)(2,1)S(1)}, bf16[1040,128]{1,0:T(8,128)(2,1)S(1)}, u32[]{:S(2)}, u32[]{:S(2)}) %collective-permute-start.1) | collective-permute-done | bytes 266272 | tf_op jit(solution)/shard_map/ppermute | solution.py:312
  38.7 7.1 %collective-permute-done.6 = bf16[1040,128]{1,0:T(8,128)(2,1)S(1)} collective-permute-done((bf16[1040,128]{1,0:T(8,128)(2,1)S(1)}, bf16[1040,128]{1,0:T(8,128)(2,1)S(1)}, u32[]{:S(2)}, u32[]{:S(2)}) %collective-permute-start.6) | collective-permute-done | bytes 266272 | tf_op jit(solution)/shard_map/ppermute | solution.py:312
  45.9 7.5 %constant_dynamic-slice_fusion.3 = (bf16[512,2048]{1,0:T(8,128)(2,1)}, bf16[512,2048]{1,0:T(8,128)(2,1)}, bf16[512,2048]{1,0:T(8,128)(2,1)}, bf16[512,2048]{1,0:T(8,128)(2,1)}) fusion(bf16[512,8192]{1,0:T(8,128)(2,1)} %param.12, s32[]{:T(128)S(6)} %select_n.47, s32[]{:T(128)S(6)} %select_n.45, s32[]{:T(128)S(6)} %select_n.44, s32[]{:T(128)S(6)} %select_n.46), kind=kLoop, calls=%fused_computation.19 | loop fusion | bytes 16777232 | tf_op jit(solution)/shard_map/dynamic_slice | solution.py:322
  53.5 3.6 %collective-permute-start.13 = (bf16[512,2048]{1,0:T(8,128)(2,1)}, bf16[512,2048]{1,0:T(8,128)(2,1)}, u32[]{:S(2)}, u32[]{:S(2)}) collective-permute-start(bf16[512,2048]{1,0:T(8,128)(2,1)} %get-tuple-element.40), channel_id=1, source_target_pairs={{0,9},{1,8},{2,11},{3,10},{4,13},{5,12},{6,15},{7,14},{8,1},{9,0},... | collective-permute-start | bytes 6291464 | tf_op jit(solution)/shard_map/ppermute | solution.py:272
  57.9 16.3 %shard_map.96 = bf16[16,32,512]{2,1,0:T(8,128)(2,1)S(1)} custom-call(s32[2]{0:T(128)S(1)} %get-tuple-element.39.own_ref, s32[16]{0:T(128)S(1)} %select_reduce_fusion.loc_ref, s32[1]{0:T(128)} %bitcast.11.core_ref, bf16[16,64,512]{2,1,0:T(8,128)(2,1)S(1)} %bitcast.29, bf16[8,1040,128]{2,1,0:T(8,128)(2,1)S(1)} %bitcast_dynamic-update-slice_fusion.first_ref, ...), custom_call_target="tpu_custom_call" | custom-call | flops 17179869184 | bytes 4194304 | tf_op jit(solution)/shard_map/pallas_call | solution.py:132
  74.2 3.0 %collective-permute-start.22 = (bf16[16,32,512]{2,1,0:T(8,128)(2,1)S(1)}, bf16[16,32,512]{2,1,0:T(8,128)(2,1)S(1)}, u32[]{:S(2)}, u32[]{:S(2)}) collective-permute-start(bf16[16,32,512]{2,1,0:T(8,128)(2,1)S(1)} %shard_map.96), channel_id=1, source_target_pairs={{0,9},{1,8},{2,11},{3,10},{4,13},{5,12},{6,15},{7,14},{8,1},{9,0},... | collective-permute-start | bytes 1572872 | tf_op jit(solution)/shard_map/ppermute | solution.py:272
  77.6 25.8 %collective-permute-done.13.refs_7_ = bf16[512,2048]{1,0:T(8,128)(2,1)} collective-permute-done((bf16[512,2048]{1,0:T(8,128)(2,1)}, bf16[512,2048]{1,0:T(8,128)(2,1)}, u32[]{:S(2)}, u32[]{:S(2)}) %collective-permute-start.13) | collective-permute-done | bytes 2097184 | tf_op jit(solution)/shard_map/ppermute | solution.py:272
  103.7 16.3 %shard_map.95 = bf16[16,32,512]{2,1,0:T(8,128)(2,1)S(1)} custom-call(s32[2]{0:T(128)S(1)} %get-tuple-element.39.own_ref, s32[16]{0:T(128)S(1)} %select_reduce_fusion.loc_ref, s32[1]{0:T(128)} %bitcast.11.core_ref, bf16[16,64,512]{2,1,0:T(8,128)(2,1)S(1)} %bitcast.30, bf16[8,1040,128]{2,1,0:T(8,128)(2,1)S(1)} %bitcast_dynamic-update-slice_fusion.first_ref, ...), custom_call_target="tpu_custom_call" | custom-call | flops 17179869184 | bytes 4194304 | tf_op jit(solution)/shard_map/pallas_call | solution.py:132
  120.0 3.3 %collective-permute-start.10 = (bf16[16,32,512]{2,1,0:T(8,128)(2,1)S(1)}, bf16[16,32,512]{2,1,0:T(8,128)(2,1)S(1)}, u32[]{:S(2)}, u32[]{:S(2)}) collective-permute-start(bf16[16,32,512]{2,1,0:T(8,128)(2,1)S(1)} %shard_map.95), channel_id=1, source_target_pairs={{0,9},{1,8},{2,11},{3,10},{4,13},{5,12},{6,15},{7,14},{8,1},{9,0},... | collective-permute-start | bytes 1572872 | tf_op jit(solution)/shard_map/ppermute | solution.py:272
  123.3 25.5 %collective-permute-done.12.refs_6_ = bf16[512,2048]{1,0:T(8,128)(2,1)} collective-permute-done((bf16[512,2048]{1,0:T(8,128)(2,1)}, bf16[512,2048]{1,0:T(8,128)(2,1)}, u32[]{:S(2)}, u32[]{:S(2)}) %collective-permute-start.12) | collective-permute-done | bytes 2097184 | tf_op jit(solution)/shard_map/ppermute | solution.py:272
  148.8 3.6 %collective-permute-start.9 = (bf16[16,32,512]{2,1,0:T(8,128)(2,1)S(1)}, bf16[16,32,512]{2,1,0:T(8,128)(2,1)S(1)}, u32[]{:S(2)}, u32[]{:S(2)}) collective-permute-start(bf16[16,32,512]{2,1,0:T(8,128)(2,1)S(1)} %shard_map.95), channel_id=1, source_target_pairs={{0,8},{1,9},{2,10},{3,11},{4,12},{5,13},{6,14},{7,15},{8,0},{9,1},... | collective-permute-start | bytes 1572872 | tf_op jit(solution)/shard_map/ppermute | solution.py:272
  152.4 7.1 %collective-permute-done.22 = bf16[16,32,512]{2,1,0:T(8,128)(2,1)S(1)} collective-permute-done((bf16[16,32,512]{2,1,0:T(8,128)(2,1)S(1)}, bf16[16,32,512]{2,1,0:T(8,128)(2,1)S(1)}, u32[]{:S(2)}, u32[]{:S(2)}) %collective-permute-start.22) | collective-permute-done | bytes 524320 | tf_op jit(solution)/shard_map/ppermute | solution.py:272
  159.7 11.4 %collective-permute-done.21 = bf16[16,32,512]{2,1,0:T(8,128)(2,1)S(1)} collective-permute-done((bf16[16,32,512]{2,1,0:T(8,128)(2,1)S(1)}, bf16[16,32,512]{2,1,0:T(8,128)(2,1)S(1)}, u32[]{:S(2)}, u32[]{:S(2)}) %collective-permute-start.21) | collective-permute-done | bytes 524320 | tf_op jit(solution)/shard_map/ppermute | solution.py:272
  172.1 10.8 %project.3 = (bf16[128,2048]{1,0:T(8,128)(2,1)}, bf16[128,2048]{1,0:T(8,128)(2,1)}, bf16[128,2048]{1,0:T(8,128)(2,1)}, bf16[128,2048]{1,0:T(8,128)(2,1)}) custom-call(s32[1]{0:T(128)} %bitcast.2.x_ref, bf16[2,4,64,512]{3,2,1,0:T(8,128)(2,1)} %bitcast.32, bf16[2,4,64,512]{3,2,1,0:T(8,128)(2,1)} %bitcast.40, bf16[2,4,64,512]{3,2,1,0:T(8,128)(2,1)} %bitcast.38, ...), custom_call_target="tpu_custom_call" | custom-call | flops 4294967296 | bytes 8388608 | tf_op jit(solution)/shard_map/project/pallas_call | solution.py:185
  182.9 3.1 %collective-permute-start.23 = (bf16[128,2048]{1,0:T(8,128)(2,1)}, bf16[128,2048]{1,0:T(8,128)(2,1)S(1)}, u32[]{:S(2)}, u32[]{:S(2)}) collective-permute-start(bf16[128,2048]{1,0:T(8,128)(2,1)} %get-tuple-element.29), channel_id=1, source_target_pairs={{0,4},{1,5},{2,6},{3,7},{4,0},{5,1},{6,2},{7,3},{8,12},{9,13},{10,... | collective-permute-start | bytes 1572872 | tf_op jit(solution)/shard_map/ppermute | solution.py:338
  189.2 4.1 %collective-permute-done.9 = bf16[16,32,512]{2,1,0:T(8,128)(2,1)S(1)} collective-permute-done((bf16[16,32,512]{2,1,0:T(8,128)(2,1)S(1)}, bf16[16,32,512]{2,1,0:T(8,128)(2,1)S(1)}, u32[]{:S(2)}, u32[]{:S(2)}) %collective-permute-start.9) | collective-permute-done | bytes 524320 | tf_op jit(solution)/shard_map/ppermute | solution.py:272
  194.3 10.7 %project.2 = (bf16[128,2048]{1,0:T(8,128)(2,1)}, bf16[128,2048]{1,0:T(8,128)(2,1)}, bf16[128,2048]{1,0:T(8,128)(2,1)}, bf16[128,2048]{1,0:T(8,128)(2,1)}) custom-call(s32[1]{0:T(128)} %bitcast.2.x_ref, bf16[2,4,64,512]{3,2,1,0:T(8,128)(2,1)} %bitcast.31, bf16[2,4,64,512]{3,2,1,0:T(8,128)(2,1)} %bitcast.39, bf16[2,4,64,512]{3,2,1,0:T(8,128)(2,1)} %bitcast.36, ...), custom_call_target="tpu_custom_call" | custom-call | flops 4294967296 | bytes 8388608 | tf_op jit(solution)/shard_map/project/pallas_call | solution.py:185
  205.0 3.0 %collective-permute-start.14 = (bf16[128,2048]{1,0:T(8,128)(2,1)}, bf16[128,2048]{1,0:T(8,128)(2,1)S(1)}, u32[]{:S(2)}, u32[]{:S(2)}) collective-permute-start(bf16[128,2048]{1,0:T(8,128)(2,1)} %get-tuple-element.21), channel_id=1, source_target_pairs={{0,4},{1,5},{2,6},{3,7},{4,0},{5,1},{6,2},{7,3},{8,12},{9,13},{10,... | collective-permute-start | bytes 1572872 | tf_op jit(solution)/shard_map/ppermute | solution.py:338
  212.3 3.4 %add_parts.3 = (bf16[32,2048]{1,0:T(8,128)(2,1)}, bf16[32,2048]{1,0:T(8,128)(2,1)}, bf16[32,2048]{1,0:T(8,128)(2,1)}, bf16[32,2048]{1,0:T(8,128)(2,1)}) custom-call(s32[1]{0:T(128)} %bitcast.m_ref.m, bf16[128,2048]{1,0:T(8,128)(2,1)} %get-tuple-element.28.refs_0_, bf16[128,2048]{1,0:T(8,128)(2,1)} %copy-done.3, bf16[128,2048]{1,0:T(8,128)(2,1)} %copy-done.5, ...), custom_call_target="tpu_custom_call" | custom-call | flops 1048576 | bytes 2621440 | tf_op jit(solution)/shard_map/add_parts/pallas_call | solution.py:215
  215.7 3.3 %collective-permute-start.27 = (bf16[32,2048]{1,0:T(8,128)(2,1)}, bf16[32,2048]{1,0:T(8,128)(2,1)S(1)}, u32[]{:S(2)}, u32[]{:S(2)}) collective-permute-start(bf16[32,2048]{1,0:T(8,128)(2,1)} %get-tuple-element.34), channel_id=1, source_target_pairs={{0,8},{1,9},{2,10},{3,11},{4,12},{5,13},{6,14},{7,15},{8,0},{9,1},... | collective-permute-start | bytes 393224 | tf_op jit(solution)/shard_map/ppermute | solution.py:272
  222.0 9.9 %collective-permute-done.15.refs_2_ = bf16[128,2048]{1,0:T(8,128)(2,1)S(1)} collective-permute-done((bf16[128,2048]{1,0:T(8,128)(2,1)}, bf16[128,2048]{1,0:T(8,128)(2,1)S(1)}, u32[]{:S(2)}, u32[]{:S(2)}) %collective-permute-start.15) | collective-permute-done | bytes 524320 | tf_op jit(solution)/shard_map/ppermute | solution.py:338
  232.9 3.4 %add_parts.2 = (bf16[32,2048]{1,0:T(8,128)(2,1)}, bf16[32,2048]{1,0:T(8,128)(2,1)}, bf16[32,2048]{1,0:T(8,128)(2,1)}, bf16[32,2048]{1,0:T(8,128)(2,1)}) custom-call(s32[1]{0:T(128)} %bitcast.m_ref.m, bf16[128,2048]{1,0:T(8,128)(2,1)} %get-tuple-element.20.refs_0_, bf16[128,2048]{1,0:T(8,128)(2,1)} %copy-done.4, bf16[128,2048]{1,0:T(8,128)(2,1)} %copy-done.6, ...), custom_call_target="tpu_custom_call" | custom-call | flops 1048576 | bytes 2621440 | tf_op jit(solution)/shard_map/add_parts/pallas_call | solution.py:215
  (101 shorter events, 36.4 us)
Async XLA Ops:
  2.8 35.9 %collective-permute-start.5 = (bf16[1040,128]{1,0:T(8,128)(2,1)S(1)}, bf16[1040,128]{1,0:T(8,128)(2,1)S(1)}, u32[]{:S(2)}, u32[]{:S(2)}) collective-permute-start(bf16[1040,128]{1,0:T(8,128)(2,1)S(1)} %pad_maximum_fusion), channel_id=1, source_target_pairs={{0,80},{16,96},{32,112},{48,64},{64,16},{80,32},{96,48},{112,0},{1... | collective-permute-start | bytes 798728 | tf_op jit(solution)/shard_map/ppermute | solution.py:312
  5.9 32.7 %collective-permute-start.4 = (bf16[1040,128]{1,0:T(8,128)(2,1)S(1)}, bf16[1040,128]{1,0:T(8,128)(2,1)S(1)}, u32[]{:S(2)}, u32[]{:S(2)}) collective-permute-start(bf16[1040,128]{1,0:T(8,128)(2,1)S(1)} %pad_maximum_fusion), channel_id=1, source_target_pairs={{0,96},{16,112},{32,64},{48,80},{64,32},{80,48},{96,0},{112,16},{1... | collective-permute-start | bytes 798728 | tf_op jit(solution)/shard_map/ppermute | solution.py:312
  8.3 30.2 %collective-permute-start.3 = (bf16[1040,128]{1,0:T(8,128)(2,1)S(1)}, bf16[1040,128]{1,0:T(8,128)(2,1)S(1)}, u32[]{:S(2)}, u32[]{:S(2)}) collective-permute-start(bf16[1040,128]{1,0:T(8,128)(2,1)S(1)} %pad_maximum_fusion), channel_id=1, source_target_pairs={{0,64},{16,80},{32,96},{48,112},{64,0},{80,16},{96,32},{112,48},{1... | collective-permute-start | bytes 798728 | tf_op jit(solution)/shard_map/ppermute | solution.py:312
  10.2 28.2 %collective-permute-start.2 = (bf16[1040,128]{1,0:T(8,128)(2,1)S(1)}, bf16[1040,128]{1,0:T(8,128)(2,1)S(1)}, u32[]{:S(2)}, u32[]{:S(2)}) collective-permute-start(bf16[1040,128]{1,0:T(8,128)(2,1)S(1)} %pad_maximum_fusion), channel_id=1, source_target_pairs={{0,48},{16,0},{32,16},{48,32},{64,112},{80,64},{96,80},{112,96},{1... | collective-permute-start | bytes 798728 | tf_op jit(solution)/shard_map/ppermute | solution.py:312
  11.6 18.4 %collective-permute-start = (bf16[1040,128]{1,0:T(8,128)(2,1)S(1)}, bf16[1040,128]{1,0:T(8,128)(2,1)S(1)}, u32[]{:S(2)}, u32[]{:S(2)}) collective-permute-start(bf16[1040,128]{1,0:T(8,128)(2,1)S(1)} %pad_maximum_fusion), channel_id=1, source_target_pairs={{0,32},{16,48},{32,0},{48,16},{64,96},{80,112},{96,64},{112,80},{1... | collective-permute-start | bytes 798728 | tf_op jit(solution)/shard_map/ppermute | solution.py:312
  45.8 12.1 %collective-permute-start.7 = (bf16[8,1040,128]{2,1,0:T(8,128)(2,1)S(1)}, bf16[8,1040,128]{2,1,0:T(8,128)(2,1)}, u32[]{:S(2)}, u32[]{:S(2)}) collective-permute-start(bf16[8,1040,128]{2,1,0:T(8,128)(2,1)S(1)} %bitcast_dynamic-update-slice_fusion.first_ref), channel_id=1, source_target_pairs={{0,1},{1,0},{2,3},{3,2},{4,5},{5,4},{6,7},{7,6},{8,9},{9,8},{10,11... | collective-permute-start | bytes 6389768 | tf_op jit(solution)/shard_map/ppermute | solution.py:272
  53.5 50.0 %collective-permute-start.13 = (bf16[512,2048]{1,0:T(8,128)(2,1)}, bf16[512,2048]{1,0:T(8,128)(2,1)}, u32[]{:S(2)}, u32[]{:S(2)}) collective-permute-start(bf16[512,2048]{1,0:T(8,128)(2,1)} %get-tuple-element.40), channel_id=1, source_target_pairs={{0,9},{1,8},{2,11},{3,10},{4,13},{5,12},{6,15},{7,14},{8,1},{9,0},... | collective-permute-start | bytes 6291464 | tf_op jit(solution)/shard_map/ppermute | solution.py:272
  57.1 62.9 %collective-permute-start.11 = (bf16[512,2048]{1,0:T(8,128)(2,1)}, bf16[512,2048]{1,0:T(8,128)(2,1)}, u32[]{:S(2)}, u32[]{:S(2)}) collective-permute-start(bf16[512,2048]{1,0:T(8,128)(2,1)} %get-tuple-element.41), channel_id=1, source_target_pairs={{0,1},{1,0},{2,3},{3,2},{4,5},{5,4},{6,7},{7,6},{8,9},{9,8},{10,11... | collective-permute-start | bytes 6291464 | tf_op jit(solution)/shard_map/ppermute | solution.py:272
  57.2 91.6 %collective-permute-start.12 = (bf16[512,2048]{1,0:T(8,128)(2,1)}, bf16[512,2048]{1,0:T(8,128)(2,1)}, u32[]{:S(2)}, u32[]{:S(2)}) collective-permute-start(bf16[512,2048]{1,0:T(8,128)(2,1)} %get-tuple-element.43), channel_id=1, source_target_pairs={{0,8},{1,9},{2,10},{3,11},{4,12},{5,13},{6,14},{7,15},{8,0},{9,1},... | collective-permute-start | bytes 6291464 | tf_op jit(solution)/shard_map/ppermute | solution.py:272
  74.2 85.3 %collective-permute-start.22 = (bf16[16,32,512]{2,1,0:T(8,128)(2,1)S(1)}, bf16[16,32,512]{2,1,0:T(8,128)(2,1)S(1)}, u32[]{:S(2)}, u32[]{:S(2)}) collective-permute-start(bf16[16,32,512]{2,1,0:T(8,128)(2,1)S(1)} %shard_map.96), channel_id=1, source_target_pairs={{0,9},{1,8},{2,11},{3,10},{4,13},{5,12},{6,15},{7,14},{8,1},{9,0},... | collective-permute-start | bytes 1572872 | tf_op jit(solution)/shard_map/ppermute | solution.py:272
  77.2 93.9 %collective-permute-start.21 = (bf16[16,32,512]{2,1,0:T(8,128)(2,1)S(1)}, bf16[16,32,512]{2,1,0:T(8,128)(2,1)S(1)}, u32[]{:S(2)}, u32[]{:S(2)}) collective-permute-start(bf16[16,32,512]{2,1,0:T(8,128)(2,1)S(1)} %shard_map.96), channel_id=1, source_target_pairs={{0,8},{1,9},{2,10},{3,11},{4,12},{5,13},{6,14},{7,15},{8,0},{9,1},... | collective-permute-start | bytes 1572872 | tf_op jit(solution)/shard_map/ppermute | solution.py:272
  103.4 67.7 %collective-permute-start.20 = (bf16[16,32,512]{2,1,0:T(8,128)(2,1)S(1)}, bf16[16,32,512]{2,1,0:T(8,128)(2,1)S(1)}, u32[]{:S(2)}, u32[]{:S(2)}) collective-permute-start(bf16[16,32,512]{2,1,0:T(8,128)(2,1)S(1)} %shard_map.96), channel_id=1, source_target_pairs={{0,1},{1,0},{2,3},{3,2},{4,5},{5,4},{6,7},{7,6},{8,9},{9,8},{10,11... | collective-permute-start | bytes 1572872 | tf_op jit(solution)/shard_map/ppermute | solution.py:272
  120.0 66.6 %collective-permute-start.10 = (bf16[16,32,512]{2,1,0:T(8,128)(2,1)S(1)}, bf16[16,32,512]{2,1,0:T(8,128)(2,1)S(1)}, u32[]{:S(2)}, u32[]{:S(2)}) collective-permute-start(bf16[16,32,512]{2,1,0:T(8,128)(2,1)S(1)} %shard_map.95), channel_id=1, source_target_pairs={{0,9},{1,8},{2,11},{3,10},{4,13},{5,12},{6,15},{7,14},{8,1},{9,0},... | collective-permute-start | bytes 1572872 | tf_op jit(solution)/shard_map/ppermute | solution.py:272
  148.8 44.6 %collective-permute-start.9 = (bf16[16,32,512]{2,1,0:T(8,128)(2,1)S(1)}, bf16[16,32,512]{2,1,0:T(8,128)(2,1)S(1)}, u32[]{:S(2)}, u32[]{:S(2)}) collective-permute-start(bf16[16,32,512]{2,1,0:T(8,128)(2,1)S(1)} %shard_map.95), channel_id=1, source_target_pairs={{0,8},{1,9},{2,10},{3,11},{4,12},{5,13},{6,14},{7,15},{8,0},{9,1},... | collective-permute-start | bytes 1572872 | tf_op jit(solution)/shard_map/ppermute | solution.py:272
  159.5 33.9 %collective-permute-start.8 = (bf16[16,32,512]{2,1,0:T(8,128)(2,1)S(1)}, bf16[16,32,512]{2,1,0:T(8,128)(2,1)S(1)}, u32[]{:S(2)}, u32[]{:S(2)}) collective-permute-start(bf16[16,32,512]{2,1,0:T(8,128)(2,1)S(1)} %shard_map.95), channel_id=1, source_target_pairs={{0,1},{1,0},{2,3},{3,2},{4,5},{5,4},{6,7},{7,6},{8,9},{9,8},{10,11... | collective-permute-start | bytes 1572872 | tf_op jit(solution)/shard_map/ppermute | solution.py:272
  182.9 25.7 %collective-permute-start.23 = (bf16[128,2048]{1,0:T(8,128)(2,1)}, bf16[128,2048]{1,0:T(8,128)(2,1)S(1)}, u32[]{:S(2)}, u32[]{:S(2)}) collective-permute-start(bf16[128,2048]{1,0:T(8,128)(2,1)} %get-tuple-element.29), channel_id=1, source_target_pairs={{0,4},{1,5},{2,6},{3,7},{4,0},{5,1},{6,2},{7,3},{8,12},{9,13},{10,... | collective-permute-start | bytes 1572872 | tf_op jit(solution)/shard_map/ppermute | solution.py:338
  186.0 25.3 %collective-permute-start.24 = (bf16[128,2048]{1,0:T(8,128)(2,1)}, bf16[128,2048]{1,0:T(8,128)(2,1)S(1)}, u32[]{:S(2)}, u32[]{:S(2)}) collective-permute-start(bf16[128,2048]{1,0:T(8,128)(2,1)} %get-tuple-element.30), channel_id=1, source_target_pairs={{0,2},{1,3},{2,4},{3,5},{4,6},{5,7},{6,0},{7,1},{8,10},{9,11},{10,... | collective-permute-start | bytes 1572872 | tf_op jit(solution)/shard_map/ppermute | solution.py:338
  186.6 24.7 %collective-permute-start.25 = (bf16[128,2048]{1,0:T(8,128)(2,1)}, bf16[128,2048]{1,0:T(8,128)(2,1)S(1)}, u32[]{:S(2)}, u32[]{:S(2)}) collective-permute-start(bf16[128,2048]{1,0:T(8,128)(2,1)} %get-tuple-element.31), channel_id=1, source_target_pairs={{0,6},{1,7},{2,0},{3,1},{4,2},{5,3},{6,4},{7,5},{8,14},{9,15},{10,... | collective-permute-start | bytes 1572872 | tf_op jit(solution)/shard_map/ppermute | solution.py:338
  205.0 16.6 %collective-permute-start.14 = (bf16[128,2048]{1,0:T(8,128)(2,1)}, bf16[128,2048]{1,0:T(8,128)(2,1)S(1)}, u32[]{:S(2)}, u32[]{:S(2)}) collective-permute-start(bf16[128,2048]{1,0:T(8,128)(2,1)} %get-tuple-element.21), channel_id=1, source_target_pairs={{0,4},{1,5},{2,6},{3,7},{4,0},{5,1},{6,2},{7,3},{8,12},{9,13},{10,... | collective-permute-start | bytes 1572872 | tf_op jit(solution)/shard_map/ppermute | solution.py:338
  208.1 23.8 %collective-permute-start.15 = (bf16[128,2048]{1,0:T(8,128)(2,1)}, bf16[128,2048]{1,0:T(8,128)(2,1)S(1)}, u32[]{:S(2)}, u32[]{:S(2)}) collective-permute-start(bf16[128,2048]{1,0:T(8,128)(2,1)} %get-tuple-element.22), channel_id=1, source_target_pairs={{0,2},{1,3},{2,4},{3,5},{4,6},{5,7},{6,0},{7,1},{8,10},{9,11},{10,... | collective-permute-start | bytes 1572872 | tf_op jit(solution)/shard_map/ppermute | solution.py:338
  208.7 23.4 %collective-permute-start.16 = (bf16[128,2048]{1,0:T(8,128)(2,1)}, bf16[128,2048]{1,0:T(8,128)(2,1)S(1)}, u32[]{:S(2)}, u32[]{:S(2)}) collective-permute-start(bf16[128,2048]{1,0:T(8,128)(2,1)} %get-tuple-element.23), channel_id=1, source_target_pairs={{0,6},{1,7},{2,0},{3,1},{4,2},{5,3},{6,4},{7,5},{8,14},{9,15},{10,... | collective-permute-start | bytes 1572872 | tf_op jit(solution)/shard_map/ppermute | solution.py:338
  215.7 23.5 %collective-permute-start.26 = (bf16[32,2048]{1,0:T(8,128)(2,1)}, bf16[32,2048]{1,0:T(8,128)(2,1)S(1)}, u32[]{:S(2)}, u32[]{:S(2)}) collective-permute-start(bf16[32,2048]{1,0:T(8,128)(2,1)} %get-tuple-element.33), channel_id=1, source_target_pairs={{0,1},{1,0},{2,3},{3,2},{4,5},{5,4},{6,7},{7,6},{8,9},{9,8},{10,11... | collective-permute-start | bytes 393224 | tf_op jit(solution)/shard_map/ppermute | solution.py:272
  215.7 24.6 %collective-permute-start.27 = (bf16[32,2048]{1,0:T(8,128)(2,1)}, bf16[32,2048]{1,0:T(8,128)(2,1)S(1)}, u32[]{:S(2)}, u32[]{:S(2)}) collective-permute-start(bf16[32,2048]{1,0:T(8,128)(2,1)} %get-tuple-element.34), channel_id=1, source_target_pairs={{0,8},{1,9},{2,10},{3,11},{4,12},{5,13},{6,14},{7,15},{8,0},{9,1},... | collective-permute-start | bytes 393224 | tf_op jit(solution)/shard_map/ppermute | solution.py:272
  221.6 18.7 %collective-permute-start.28 = (bf16[32,2048]{1,0:T(8,128)(2,1)}, bf16[32,2048]{1,0:T(8,128)(2,1)S(1)}, u32[]{:S(2)}, u32[]{:S(2)}) collective-permute-start(bf16[32,2048]{1,0:T(8,128)(2,1)} %get-tuple-element.35), channel_id=1, source_target_pairs={{0,9},{1,8},{2,11},{3,10},{4,13},{5,12},{6,15},{7,14},{8,1},{9,0},... | collective-permute-start | bytes 393224 | tf_op jit(solution)/shard_map/ppermute | solution.py:272
  (26 other events, 206.3 us)
where the time goes:
time: 251 us; the launch traced here: 250 us
  waiting for transfers between devices  123 us (49%)
  Pallas kernels  66 us (26%)
  starting transfers between devices  43.6 us (17%)
  local copies, waits for them, and re-layouts  13.7 us (5%)
    ppermute x16, waiting for transfers between devices, swapped(): return lax.ppermute(value, 'tp', [(i, i ^ mask) for i in range(count)])  76.8 us
    ppermute x7, waiting for transfers between devices, shards(): pieces.append(lax.ppermute(mine, 'ctx', pairs))  33.3 us
    pallas_call x2, Pallas kernels, attend(): pl.pallas_call(functools.partial(attend_kernel, rows=rows, part=part, hea...  32.6 us
    ppermute x16, starting transfers between devices, swapped(): return lax.ppermute(value, 'tp', [(i, i ^ mask) for i in range(count)])  21.8 us
    pallas_call x2, Pallas kernels, project(): pl.pallas_call(project_kernel, out_shape=[jax.ShapeDtypeStruct((rows, n),...  21.5 us
    ppermute x6, waiting for transfers between devices, shards(): got.append(lax.ppermute(sent[dx], 'tp', pairs))  12.7 us
    ppermute x6, starting transfers between devices, shards(): got.append(lax.ppermute(sent[dx], 'tp', pairs))  12.6 us
    ppermute x7, starting transfers between devices, shards(): pieces.append(lax.ppermute(mine, 'ctx', pairs))  9.16 us
  transfers between devices with their start and end apart: 29, of which 13 were waited for; matrix products, arithmetic and copies ran while one was open for 3% of the time, Pallas kernels for 25%

commit v1 on v0

--- a/solution.py
+++ b/solution.py
@@ -16,7 +16,6 @@
 LOG2_SCALE = math.log2(math.e) / math.sqrt(HD)
 PARTS = 2
 Y_COUNT = 4
-X_COUNT = 4
 ANY = pl.ANY
 
 
@@ -161,40 +160,66 @@
     )(own, loc, core, queries.reshape(tp_count, run, width), first, second)
 
 
-def project_kernel(x_ref, *refs):
-    att_refs, w_refs, out_refs = refs[:4], refs[4:8], refs[8:]
+def stack_kernel(*refs):
+    ins, out_ref, sems = refs[:-2], refs[-2], refs[-1]
+    copies = [pltpu.make_async_copy(x, out_ref.at[i], sems.at[i]) for i, x in enumerate(ins)]
+    for c in copies:
+        c.start()
+    for c in copies:
+        c.wait()
+
+
+def stacked(pieces):
+    shape = (len(pieces), *pieces[0].shape)
+    return pl.pallas_call(
+        stack_kernel,
+        out_shape=jax.ShapeDtypeStruct(shape, pieces[0].dtype),
+        in_specs=[pl.BlockSpec(memory_space=ANY)] * len(pieces),
+        out_specs=pl.BlockSpec(memory_space=ANY),
+        scratch_shapes=[pltpu.SemaphoreType.DMA((len(pieces),))],
+    )(*pieces)
+
+
+def project_kernel(place_ref, *refs):
+    atts, near, far, (acc_ref,), outs = refs[:4], refs[4:6], refs[6:10], refs[14:], refs[10:14]
     step = pl.program_id(0)
-    rows = out_refs[0].shape[0]
-    total = None
-    for a, w in zip(att_refs, w_refs):
-        term = jnp.dot(a[...].reshape(rows, a.shape[-1]), w[...], preferred_element_type=jnp.float32)
-        total = term if total is None else total + term
-    for i, o in enumerate(out_refs):
-        @pl.when(step == i)
-        def _(o=o):
-            o[...] = total.astype(jnp.bfloat16)
-
-
-def project(x_rank, atts, ws):
+    rows, k = acc_ref.shape[0], atts[0].shape[-1]
+    near_term = jnp.dot(atts[0][...].reshape(rows, k), near[0][...], preferred_element_type=jnp.float32)
+    near_term += jnp.dot(atts[1][...].reshape(rows, k), near[1][...], preferred_element_type=jnp.float32)
+    for j, w in enumerate(far):
+        @pl.when(step == j)
+        def _(w=w):
+            total = near_term + jnp.dot(atts[2][...].reshape(rows, k), w[0], preferred_element_type=jnp.float32)
+            acc_ref[...] = total + jnp.dot(atts[3][...].reshape(rows, k), w[1], preferred_element_type=jnp.float32)
+    n = outs[0].shape[0]
+    for i, o in enumerate(outs):
+        o[...] = acc_ref[pl.ds(pl.multiple_of((place_ref[1] ^ i) * n, n), n), :].astype(jnp.bfloat16)
+
+
+def project(place, atts, weight, paired, far):
     tps, r, k = atts[0].shape
-    cores = tps // (2 * X_COUNT)
-    n = ws[0].shape[1]
-    rows = 2 * cores * r
-    views = [a.reshape(2, X_COUNT, cores * r, k) for a in atts]
-    pick = lambda i, x: (0, (x[0] + i) % X_COUNT, 0, 0)
+    rows, cut = tps * r, far[0].shape[-1]
+    blocks = len(far)
+    col = lambda j, p: (p[2] - j) & (blocks - 1)
     return pl.pallas_call(
         project_kernel,
-        out_shape=[jax.ShapeDtypeStruct((rows, n), jnp.bfloat16)] * X_COUNT,
+        out_shape=[jax.ShapeDtypeStruct((rows // 4, cut * blocks), jnp.bfloat16)] * 4,
         grid_spec=pltpu.PrefetchScalarGridSpec(
             num_scalar_prefetch=1,
-            grid=(X_COUNT,),
-            in_specs=[pl.BlockSpec((2, 1, cores * r, k), pick)] * 4 + [pl.BlockSpec((k, n), lambda i, x: (0, 0))] * 4,
-            out_specs=[pl.BlockSpec((rows, n), lambda i, x: (0, 0))] * X_COUNT,
-        ),
-        compiler_params=pltpu.CompilerParams(dimension_semantics=("arbitrary",), vmem_limit_bytes=56 * 2**20),
-        cost_estimate=pl.CostEstimate(flops=2 * rows * X_COUNT * 4 * k * n, bytes_accessed=8 * k * n, transcendentals=0),
+            grid=(blocks,),
+            in_specs=[pl.BlockSpec((tps, r, k), lambda j, p: (0, 0, 0))] * 4
+            + [
+                pl.BlockSpec((k, cut), lambda j, p: (0, p[0] * blocks + col(j, p))),
+                pl.BlockSpec((k, cut), lambda j, p: (0, col(j, p))),
+            ]
+            + [pl.BlockSpec(far[0].shape, lambda j, p: (0, 0, 0))] * blocks,
+            out_specs=[pl.BlockSpec((rows // 4, cut), lambda j, p: (0, col(j, p)))] * 4,
+            scratch_shapes=[pltpu.VMEM((rows, cut), jnp.float32)],
+        ),
+        compiler_params=pltpu.CompilerParams(dimension_semantics=("arbitrary",), vmem_limit_bytes=40 * 2**20),
+        cost_estimate=pl.CostEstimate(flops=8 * rows * k * cut * blocks, bytes_accessed=8 * k * cut * blocks, transcendentals=0),
         name="project",
-    )(x_rank, *views, *ws)
+    )(place, *atts, weight, paired, *far)
 
 
 def gather_kernel(m_ref, *refs):
@@ -287,10 +312,9 @@
     tp_rank = lax.axis_index("tp").astype(jnp.int32)
     tok, _ = queries.shape
     core = tp_rank & 1
-    x_rank = (tp_rank >> 1) & (X_COUNT - 1)
-    far = tp_count // 2
-    member = (tp_rank // far) * 2 + core
-    masks = (0, 1, far, far + 1)
+    member = tp_rank & 3
+    group = tp_rank >> 2
+    y_rank = lax.axis_index("ctx").astype(jnp.int32) & (Y_COUNT - 1)
 
     kv_col = (tp_rank >> 1) * HD
     mine = jnp.where(
@@ -310,36 +334,40 @@
                     (c, (c // Y_COUNT ^ dz) * Y_COUNT + (c + dy) % Y_COUNT) for c in range(ctx_count)
                 ]
                 pieces.append(lax.ppermute(mine, "ctx", pairs))
-    first = jnp.stack(pieces)
+    first = stacked(pieces)
     second = swapped(first, 1, tp_count)
     order = first[:, tok:tok + spans, 0].reshape(ctx_count * spans).astype(jnp.int32)
     blocks = jnp.arange(ctx_count * spans, dtype=jnp.int32)
     loc = jnp.sum(jnp.where(order[None, :] == blocks[:, None], blocks[None, :], 0), axis=1)
 
     quarter = out_weight.shape[1] // 4
-    ws = []
-    for i, mask in enumerate(masks):
-        w = lax.dynamic_slice_in_dim(out_weight, (member ^ i) * quarter, quarter, 1)
-        ws.append(swapped(w, mask, tp_count) if mask else w)
+    cut = quarter // Y_COUNT
+    sides = []
+    for i in (2, 3):
+        w = lax.dynamic_slice_in_dim(out_weight, (member ^ i) * quarter + y_rank * cut, cut, 1)
+        sides.append(swapped(w, i, tp_count))
+    side = stacked(sides)
+    far = [side]
+    for dy in (1, 2, 3):
+        pairs = [(c, c - c % Y_COUNT + (c + dy) % Y_COUNT) for c in range(ctx_count)]
+        far.append(lax.ppermute(side, "ctx", pairs))
+    w = lax.dynamic_slice_in_dim(out_weight, (member ^ 1) * quarter, quarter, 1)
+    paired = swapped(w, 1, tp_count)
+    place = jnp.stack([member, group, y_rank])
 
     outs = ()
     for part in range(PARTS):
         att = attend(own, loc, core[None], queries, first, second, part, tp_count)
-        atts = []
-        for mask in masks:
-            atts.append(swapped(att, mask, tp_count) if mask else att)
-        sent = project(x_rank[None], atts, ws)
+        atts = [att]
+        for i in (1, 2, 3):
+            atts.append(swapped(att, i, tp_count))
+        sent = project(place, atts, out_weight, paired, far)
         got = [sent[0]]
-        for dx in (2, 1, 3):
-            pairs = []
-            for t in range(tp_count):
-                x = (t >> 1) & (X_COUNT - 1)
-                pairs.append((t, t - 2 * x + 2 * ((x + dx) % X_COUNT)))
-            got.append(lax.ppermute(sent[dx], "tp", pairs))
+        for i in (1, 2, 3):
+            got.append(swapped(sent[i], 4 * i, tp_count))
         cols = list(add_parts(member[None], got))
-        for i, mask in enumerate(masks):
-            if mask:
-                cols[i] = swapped(cols[i], mask, tp_count)
+        for i in (1, 2, 3):
+            cols[i] = swapped(cols[i], i, tp_count)
         outs = finish(member[None], static_scale, residual_in, norm_gain[None, :], cols, part, outs)
     return tuple(outs)
 

time: 251 us -> 326 us (1.30)
  the two profiles are of different devices: /device:TPU:0 before, /device:TPU:25 now
where the time goes in v1:
time: 326 us; the launch traced here: 325 us
  Pallas kernels  163 us (50%)
  waiting for transfers between devices  98.3 us (30%)
  starting transfers between devices  46.6 us (14%)
  local copies, waits for them, and re-layouts  13.1 us (4%)
    pallas_call x2, Pallas kernels, stacked(): pl.pallas_call(stack_kernel, out_shape=jax.ShapeDtypeStruct(shape, pieces...  98.6 us
    ppermute x22, waiting for transfers between devices, swapped(): return lax.ppermute(value, 'tp', [(i, i ^ mask) for i in range(count)])  50.6 us
    pallas_call x2, Pallas kernels, attend(): pl.pallas_call(functools.partial(attend_kernel, rows=rows, part=part, hea...  36.3 us
    ppermute x22, starting transfers between devices, swapped(): return lax.ppermute(value, 'tp', [(i, i ^ mask) for i in range(count)])  35.8 us
    ppermute x7, waiting for transfers between devices, shards(): pieces.append(lax.ppermute(mine, 'ctx', pairs))  25.7 us
    ppermute x3, waiting for transfers between devices, shards(): far.append(lax.ppermute(side, 'ctx', pairs))  22.1 us
    pallas_call x2, Pallas kernels, project(): pl.pallas_call(project_kernel, out_shape=[jax.ShapeDtypeStruct((rows // 4...  16.5 us
    pallas_call x2, Pallas kernels, add_parts(): pl.pallas_call(gather_kernel, out_shape=[jax.ShapeDtypeStruct((r, n), jnp...  6.81 us
  transfers between devices with their start and end apart: 32, of which 12 were waited for; matrix products, arithmetic and copies ran while one was open for 2% of the time, Pallas kernels for 29%

profile of v1, /device:TPU:25, one launch (start us, length us, event | category | flops | bytes accessed | tf_op | source)
XLA Modules:
  0.0 325.4 jit_solution(1173281057043311669)
XLA Ops:
  8.6 14.8 %collective-permute-done.6.refs_7_ = bf16[1040,128]{1,0:T(8,128)(2,1)S(1)} collective-permute-done((bf16[1040,128]{1,0:T(8,128)(2,1)S(1)}, bf16[1040,128]{1,0:T(8,128)(2,1)S(1)}, u32[]{:S(2)}, u32[]{:S(2)}) %collective-permute-start.6) | collective-permute-done | bytes 266272 | tf_op jit(solution)/shard_map/ppermute | solution.py:336
  23.6 6.8 %collective-permute-done.3.refs_4_ = bf16[1040,128]{1,0:T(8,128)(2,1)S(1)} collective-permute-done((bf16[1040,128]{1,0:T(8,128)(2,1)S(1)}, bf16[1040,128]{1,0:T(8,128)(2,1)S(1)}, u32[]{:S(2)}, u32[]{:S(2)}) %collective-permute-start.3) | collective-permute-done | bytes 266272 | tf_op jit(solution)/shard_map/ppermute | solution.py:336
  30.4 4.0 %collective-permute-done.2.refs_3_ = bf16[1040,128]{1,0:T(8,128)(2,1)S(1)} collective-permute-done((bf16[1040,128]{1,0:T(8,128)(2,1)S(1)}, bf16[1040,128]{1,0:T(8,128)(2,1)S(1)}, u32[]{:S(2)}, u32[]{:S(2)}) %collective-permute-start.2) | collective-permute-done | bytes 266272 | tf_op jit(solution)/shard_map/ppermute | solution.py:336
  35.9 65.7 %shard_map.95.first_ref = bf16[8,1040,128]{2,1,0:T(8,128)(2,1)} custom-call(bf16[1040,128]{1,0:T(8,128)(2,1)} %copy-done.6, bf16[1040,128]{1,0:T(8,128)(2,1)} %copy-done.19, bf16[1040,128]{1,0:T(8,128)(2,1)} %copy-done.18, bf16[1040,128]{1,0:T(8,128)(2,1)} %copy-done.17, bf16[1040,128]{1,0:T(8,128)(2,1)} %copy-done.16, bf16[1040,128]{1,0:T(8,128)(2,1)} %copy-done.15, ...), custom_call_target="tpu_custom_call" | custom-call | tf_op jit(solution)/shard_map/pallas_call | solution.py:174
  106.9 3.2 constant_dynamic-slice_fusion.2
  112.0 8.1 %collective-permute-done.13.refs_1_ = bf16[512,512]{1,0:T(8,128)(2,1)} collective-permute-done((bf16[512,512]{1,0:T(8,128)(2,1)}, bf16[512,512]{1,0:T(8,128)(2,1)}, u32[]{:S(2)}, u32[]{:S(2)}) %collective-permute-start.13) | collective-permute-done | bytes 524320 | tf_op jit(solution)/shard_map/ppermute | solution.py:297
  120.0 10.2 %collective-permute-done.12.refs_0_ = bf16[512,512]{1,0:T(8,128)(2,1)} collective-permute-done((bf16[512,512]{1,0:T(8,128)(2,1)}, bf16[512,512]{1,0:T(8,128)(2,1)}, u32[]{:S(2)}, u32[]{:S(2)}) %collective-permute-start.12) | collective-permute-done | bytes 524320 | tf_op jit(solution)/shard_map/ppermute | solution.py:297
  130.3 32.9 %shard_map.97.refs_6_ = bf16[2,512,512]{2,1,0:T(8,128)(2,1)} custom-call(bf16[512,512]{1,0:T(8,128)(2,1)} %collective-permute-done.12.refs_0_, bf16[512,512]{1,0:T(8,128)(2,1)} %collective-permute-done.13.refs_1_), custom_call_target="tpu_custom_call" | custom-call | tf_op jit(solution)/shard_map/pallas_call | solution.py:174
  163.7 4.3 %collective-permute-start.15 = (bf16[2,512,512]{2,1,0:T(8,128)(2,1)}, bf16[2,512,512]{2,1,0:T(8,128)(2,1)S(1)}, u32[]{:S(2)}, u32[]{:S(2)}) collective-permute-start(bf16[2,512,512]{2,1,0:T(8,128)(2,1)} %shard_map.97.refs_6_), channel_id=1, source_target_pairs={{0,32},{16,48},{32,0},{48,16},{64,96},{80,112},{96,64},{112,80},{1... | collective-permute-start | bytes 3145736 | tf_op jit(solution)/shard_map/ppermute | solution.py:353
  169.7 18.1 %shard_map.98.refs_0_ = bf16[16,32,512]{2,1,0:T(8,128)(2,1)S(1)} custom-call(s32[2]{0:T(128)S(1)} %get-tuple-element.39.own_ref, s32[16]{0:T(128)S(1)} %select_reduce_fusion.loc_ref, s32[1]{0:T(128)} %bitcast.4.core_ref, bf16[16,64,512]{2,1,0:T(8,128)(2,1)S(1)} %bitcast.6, bf16[8,1040,128]{2,1,0:T(8,128)(2,1)S(1)} %copy-done.1, ...), custom_call_target="tpu_custom_call" | custom-call | flops 17179869184 | bytes 4194304 | tf_op jit(solution)/shard_map/pallas_call | solution.py:131
  187.8 2.8 collective-permute-start.25
  190.9 22.1 %collective-permute-done.15.refs_8_ = bf16[2,512,512]{2,1,0:T(8,128)(2,1)S(1)} collective-permute-done((bf16[2,512,512]{2,1,0:T(8,128)(2,1)}, bf16[2,512,512]{2,1,0:T(8,128)(2,1)S(1)}, u32[]{:S(2)}, u32[]{:S(2)}) %collective-permute-start.15) | collective-permute-done | bytes 1048608 | tf_op jit(solution)/shard_map/ppermute | solution.py:353
  214.8 18.2 %shard_map.96.refs_0_ = bf16[16,32,512]{2,1,0:T(8,128)(2,1)S(1)} custom-call(s32[2]{0:T(128)S(1)} %get-tuple-element.39.own_ref, s32[16]{0:T(128)S(1)} %select_reduce_fusion.loc_ref, s32[1]{0:T(128)} %bitcast.4.core_ref, bf16[16,64,512]{2,1,0:T(8,128)(2,1)S(1)} %bitcast.7, bf16[8,1040,128]{2,1,0:T(8,128)(2,1)S(1)} %copy-done.2, ...), custom_call_target="tpu_custom_call" | custom-call | flops 17179869184 | bytes 4194304 | tf_op jit(solution)/shard_map/pallas_call | solution.py:131
  235.3 8.0 %project.3 = (bf16[128,2048]{1,0:T(8,128)(2,1)S(1)}, bf16[128,2048]{1,0:T(8,128)(2,1)S(1)}, bf16[128,2048]{1,0:T(8,128)(2,1)S(1)}, bf16[128,2048]{1,0:T(8,128)(2,1)S(1)}) custom-call(s32[3]{0:T(128)S(1)} %pad_add_fusion.place_ref, bf16[16,32,512]{2,1,0:T(8,128)(2,1)S(1)} %shard_map.98.refs_0_, bf16[16,32,512]{2,1,0:T(8,128)(2,1)S(1)} %collective-permute-done.23.refs_1_, ...), custom_call_target="tpu_custom_call" | custom-call | flops 4294967296 | bytes 8388608 | tf_op jit(solution)/shard_map/project/pallas_call | solution.py:204
  243.3 2.8 collective-permute-start.26
  246.1 3.6 %collective-permute-start.27 = (bf16[128,2048]{1,0:T(8,128)(2,1)S(1)}, bf16[128,2048]{1,0:T(8,128)(2,1)S(1)}, u32[]{:S(2)}, u32[]{:S(2)}) collective-permute-start(bf16[128,2048]{1,0:T(8,128)(2,1)S(1)} %get-tuple-element.30), channel_id=1, source_target_pairs={{0,8},{1,9},{2,10},{3,11},{4,12},{5,13},{6,14},{7,15},{8,0},{9,1},... | collective-permute-start | bytes 1572872 | tf_op jit(solution)/shard_map/ppermute | solution.py:297
  249.7 3.6 %collective-permute-start.28 = (bf16[128,2048]{1,0:T(8,128)(2,1)S(1)}, bf16[128,2048]{1,0:T(8,128)(2,1)S(1)}, u32[]{:S(2)}, u32[]{:S(2)}) collective-permute-start(bf16[128,2048]{1,0:T(8,128)(2,1)S(1)} %get-tuple-element.31), channel_id=1, source_target_pairs={{0,12},{1,13},{2,14},{3,15},{4,8},{5,9},{6,10},{7,11},{8,4},{9,5},... | collective-permute-start | bytes 1572872 | tf_op jit(solution)/shard_map/ppermute | solution.py:297
  253.4 4.1 %collective-permute-done.9.refs_2_ = bf16[16,32,512]{2,1,0:T(8,128)(2,1)S(1)} collective-permute-done((bf16[16,32,512]{2,1,0:T(8,128)(2,1)S(1)}, bf16[16,32,512]{2,1,0:T(8,128)(2,1)S(1)}, u32[]{:S(2)}, u32[]{:S(2)}) %collective-permute-start.9) | collective-permute-done | bytes 524320 | tf_op jit(solution)/shard_map/ppermute | solution.py:297
  257.5 8.5 %project.2 = (bf16[128,2048]{1,0:T(8,128)(2,1)S(1)}, bf16[128,2048]{1,0:T(8,128)(2,1)}, bf16[128,2048]{1,0:T(8,128)(2,1)S(1)}, bf16[128,2048]{1,0:T(8,128)(2,1)S(1)}) custom-call(s32[3]{0:T(128)S(1)} %pad_add_fusion.place_ref, bf16[16,32,512]{2,1,0:T(8,128)(2,1)S(1)} %shard_map.96.refs_0_, bf16[16,32,512]{2,1,0:T(8,128)(2,1)S(1)} %collective-permute-done.8.refs_1_, ...), custom_call_target="tpu_custom_call" | custom-call | flops 4294967296 | bytes 8388608 | tf_op jit(solution)/shard_map/project/pallas_call | solution.py:204
  269.6 3.6 %collective-permute-start.18 = (bf16[128,2048]{1,0:T(8,128)(2,1)S(1)}, bf16[128,2048]{1,0:T(8,128)(2,1)S(1)}, u32[]{:S(2)}, u32[]{:S(2)}) collective-permute-start(bf16[128,2048]{1,0:T(8,128)(2,1)S(1)} %get-tuple-element.22), channel_id=1, source_target_pairs={{0,8},{1,9},{2,10},{3,11},{4,12},{5,13},{6,14},{7,15},{8,0},{9,1},... | collective-permute-start | bytes 1572872 | tf_op jit(solution)/shard_map/ppermute | solution.py:297
  274.8 10.7 %collective-permute-done.28.refs_3_ = bf16[128,2048]{1,0:T(8,128)(2,1)S(1)} collective-permute-done((bf16[128,2048]{1,0:T(8,128)(2,1)S(1)}, bf16[128,2048]{1,0:T(8,128)(2,1)S(1)}, u32[]{:S(2)}, u32[]{:S(2)}) %collective-permute-start.28) | collective-permute-done | bytes 524320 | tf_op jit(solution)/shard_map/ppermute | solution.py:297
  286.3 3.4 %add_parts.3 = (bf16[32,2048]{1,0:T(8,128)(2,1)}, bf16[32,2048]{1,0:T(8,128)(2,1)}, bf16[32,2048]{1,0:T(8,128)(2,1)}, bf16[32,2048]{1,0:T(8,128)(2,1)}) custom-call(s32[1]{0:T(128)} %bitcast.m_ref.m, bf16[128,2048]{1,0:T(8,128)(2,1)} %copy-done.4, bf16[128,2048]{1,0:T(8,128)(2,1)} %copy-done.7, bf16[128,2048]{1,0:T(8,128)(2,1)} %copy-done.9, ...), custom_call_target="tpu_custom_call" | custom-call | flops 1048576 | bytes 2621440 | tf_op jit(solution)/shard_map/add_parts/pallas_call | solution.py:240
  296.1 11.8 %collective-permute-done.19.refs_3_ = bf16[128,2048]{1,0:T(8,128)(2,1)S(1)} collective-permute-done((bf16[128,2048]{1,0:T(8,128)(2,1)S(1)}, bf16[128,2048]{1,0:T(8,128)(2,1)S(1)}, u32[]{:S(2)}, u32[]{:S(2)}) %collective-permute-start.19) | collective-permute-done | bytes 524320 | tf_op jit(solution)/shard_map/ppermute | solution.py:297
  308.8 3.4 %add_parts.2 = (bf16[32,2048]{1,0:T(8,128)(2,1)}, bf16[32,2048]{1,0:T(8,128)(2,1)}, bf16[32,2048]{1,0:T(8,128)(2,1)}, bf16[32,2048]{1,0:T(8,128)(2,1)}) custom-call(s32[1]{0:T(128)} %bitcast.m_ref.m, bf16[128,2048]{1,0:T(8,128)(2,1)} %copy-done.3, bf16[128,2048]{1,0:T(8,128)(2,1)} %copy-done.8, bf16[128,2048]{1,0:T(8,128)(2,1)} %copy-done.10, ...), custom_call_target="tpu_custom_call" | custom-call | flops 1048576 | bytes 2621440 | tf_op jit(solution)/shard_map/add_parts/pallas_call | solution.py:240
  (113 shorter events, 49.0 us)
Async XLA Ops:
  2.8 20.7 %collective-permute-start.6 = (bf16[1040,128]{1,0:T(8,128)(2,1)S(1)}, bf16[1040,128]{1,0:T(8,128)(2,1)S(1)}, u32[]{:S(2)}, u32[]{:S(2)}) collective-permute-start(bf16[1040,128]{1,0:T(8,128)(2,1)S(1)} %pad_maximum_fusion.refs_0_), channel_id=1, source_target_pairs={{0,112},{16,64},{32,80},{48,96},{64,48},{80,0},{96,16},{112,32},{1... | collective-permute-start | bytes 798728 | tf_op jit(solution)/shard_map/ppermute | solution.py:336
  4.7 18.8 %collective-permute-start.5 = (bf16[1040,128]{1,0:T(8,128)(2,1)S(1)}, bf16[1040,128]{1,0:T(8,128)(2,1)S(1)}, u32[]{:S(2)}, u32[]{:S(2)}) collective-permute-start(bf16[1040,128]{1,0:T(8,128)(2,1)S(1)} %pad_maximum_fusion.refs_0_), channel_id=1, source_target_pairs={{0,80},{16,96},{32,112},{48,64},{64,16},{80,32},{96,48},{112,0},{1... | collective-permute-start | bytes 798728 | tf_op jit(solution)/shard_map/ppermute | solution.py:336
  7.5 22.9 %collective-permute-start.3 = (bf16[1040,128]{1,0:T(8,128)(2,1)S(1)}, bf16[1040,128]{1,0:T(8,128)(2,1)S(1)}, u32[]{:S(2)}, u32[]{:S(2)}) collective-permute-start(bf16[1040,128]{1,0:T(8,128)(2,1)S(1)} %pad_maximum_fusion.refs_0_), channel_id=1, source_target_pairs={{0,64},{16,80},{32,96},{48,112},{64,0},{80,16},{96,32},{112,48},{1... | collective-permute-start | bytes 798728 | tf_op jit(solution)/shard_map/ppermute | solution.py:336
  8.1 26.4 %collective-permute-start.2 = (bf16[1040,128]{1,0:T(8,128)(2,1)S(1)}, bf16[1040,128]{1,0:T(8,128)(2,1)S(1)}, u32[]{:S(2)}, u32[]{:S(2)}) collective-permute-start(bf16[1040,128]{1,0:T(8,128)(2,1)S(1)} %pad_maximum_fusion.refs_0_), channel_id=1, source_target_pairs={{0,48},{16,0},{32,16},{48,32},{64,112},{80,64},{96,80},{112,96},{1... | collective-permute-start | bytes 798728 | tf_op jit(solution)/shard_map/ppermute | solution.py:336
  101.6 66.4 %collective-permute-start.7 = (bf16[8,1040,128]{2,1,0:T(8,128)(2,1)}, bf16[8,1040,128]{2,1,0:T(8,128)(2,1)}, u32[]{:S(2)}, u32[]{:S(2)}) collective-permute-start(bf16[8,1040,128]{2,1,0:T(8,128)(2,1)} %shard_map.95.first_ref), channel_id=1, source_target_pairs={{0,1},{1,0},{2,3},{3,2},{4,5},{5,4},{6,7},{7,6},{8,9},{9,8},{10,11... | collective-permute-start | bytes 6389768 | tf_op jit(solution)/shard_map/ppermute | solution.py:297
  106.6 23.6 %collective-permute-start.12 = (bf16[512,512]{1,0:T(8,128)(2,1)}, bf16[512,512]{1,0:T(8,128)(2,1)}, u32[]{:S(2)}, u32[]{:S(2)}) collective-permute-start(bf16[512,512]{1,0:T(8,128)(2,1)} %get-tuple-element.41), channel_id=1, source_target_pairs={{0,2},{1,3},{2,0},{3,1},{4,6},{5,7},{6,4},{7,5},{8,10},{9,11},{10,... | collective-permute-start | bytes 1572872 | tf_op jit(solution)/shard_map/ppermute | solution.py:297
  110.1 124.1 %collective-permute-start.11 = (bf16[512,2048]{1,0:T(8,128)(2,1)}, bf16[512,2048]{1,0:T(8,128)(2,1)S(1)}, u32[]{:S(2)}, u32[]{:S(2)}) collective-permute-start(bf16[512,2048]{1,0:T(8,128)(2,1)} %constant_dynamic-slice_fusion.2), channel_id=1, source_target_pairs={{0,1},{1,0},{2,3},{3,2},{4,5},{5,4},{6,7},{7,6},{8,9},{9,8},{10,11... | collective-permute-start | bytes 6291464 | tf_op jit(solution)/shard_map/ppermute | solution.py:297
  163.2 27.5 %collective-permute-start.16 = (bf16[2,512,512]{2,1,0:T(8,128)(2,1)}, bf16[2,512,512]{2,1,0:T(8,128)(2,1)S(1)}, u32[]{:S(2)}, u32[]{:S(2)}) collective-permute-start(bf16[2,512,512]{2,1,0:T(8,128)(2,1)} %shard_map.97.refs_6_), channel_id=1, source_target_pairs={{0,48},{16,0},{32,16},{48,32},{64,112},{80,64},{96,80},{112,96},{1... | collective-permute-start | bytes 3145736 | tf_op jit(solution)/shard_map/ppermute | solution.py:353
  163.7 49.2 %collective-permute-start.15 = (bf16[2,512,512]{2,1,0:T(8,128)(2,1)}, bf16[2,512,512]{2,1,0:T(8,128)(2,1)S(1)}, u32[]{:S(2)}, u32[]{:S(2)}) collective-permute-start(bf16[2,512,512]{2,1,0:T(8,128)(2,1)} %shard_map.97.refs_6_), channel_id=1, source_target_pairs={{0,32},{16,48},{32,0},{48,16},{64,96},{80,112},{96,64},{112,80},{1... | collective-permute-start | bytes 3145736 | tf_op jit(solution)/shard_map/ppermute | solution.py:353
  168.0 65.0 %collective-permute-start.14 = (bf16[2,512,512]{2,1,0:T(8,128)(2,1)}, bf16[2,512,512]{2,1,0:T(8,128)(2,1)S(1)}, u32[]{:S(2)}, u32[]{:S(2)}) collective-permute-start(bf16[2,512,512]{2,1,0:T(8,128)(2,1)} %shard_map.97.refs_6_), channel_id=1, source_target_pairs={{0,16},{16,32},{32,48},{48,0},{64,80},{80,96},{96,112},{112,64},{1... | collective-permute-start | bytes 3145736 | tf_op jit(solution)/shard_map/ppermute | solution.py:353
  187.8 46.6 %collective-permute-start.25 = (bf16[16,32,512]{2,1,0:T(8,128)(2,1)S(1)}, bf16[16,32,512]{2,1,0:T(8,128)(2,1)S(1)}, u32[]{:S(2)}, u32[]{:S(2)}) collective-permute-start(bf16[16,32,512]{2,1,0:T(8,128)(2,1)S(1)} %shard_map.98.refs_0_), channel_id=1, source_target_pairs={{0,3},{1,2},{2,1},{3,0},{4,7},{5,6},{6,5},{7,4},{8,11},{9,10},{10,... | collective-permute-start | bytes 1572872 | tf_op jit(solution)/shard_map/ppermute | solution.py:297
  190.6 44.7 %collective-permute-start.24 = (bf16[16,32,512]{2,1,0:T(8,128)(2,1)S(1)}, bf16[16,32,512]{2,1,0:T(8,128)(2,1)S(1)}, u32[]{:S(2)}, u32[]{:S(2)}) collective-permute-start(bf16[16,32,512]{2,1,0:T(8,128)(2,1)S(1)} %shard_map.98.refs_0_), channel_id=1, source_target_pairs={{0,2},{1,3},{2,0},{3,1},{4,6},{5,7},{6,4},{7,5},{8,10},{9,11},{10,... | collective-permute-start | bytes 1572872 | tf_op jit(solution)/shard_map/ppermute | solution.py:297
  212.9 22.4 %collective-permute-start.23 = (bf16[16,32,512]{2,1,0:T(8,128)(2,1)S(1)}, bf16[16,32,512]{2,1,0:T(8,128)(2,1)S(1)}, u32[]{:S(2)}, u32[]{:S(2)}) collective-permute-start(bf16[16,32,512]{2,1,0:T(8,128)(2,1)S(1)} %shard_map.98.refs_0_), channel_id=1, source_target_pairs={{0,1},{1,0},{2,3},{3,2},{4,5},{5,4},{6,7},{7,6},{8,9},{9,8},{10,11... | collective-permute-start | bytes 1572872 | tf_op jit(solution)/shard_map/ppermute | solution.py:297
  234.2 23.3 %collective-permute-start.9 = (bf16[16,32,512]{2,1,0:T(8,128)(2,1)S(1)}, bf16[16,32,512]{2,1,0:T(8,128)(2,1)S(1)}, u32[]{:S(2)}, u32[]{:S(2)}) collective-permute-start(bf16[16,32,512]{2,1,0:T(8,128)(2,1)S(1)} %shard_map.96.refs_0_), channel_id=1, source_target_pairs={{0,2},{1,3},{2,0},{3,1},{4,6},{5,7},{6,4},{7,5},{8,10},{9,11},{10,... | collective-permute-start | bytes 1572872 | tf_op jit(solution)/shard_map/ppermute | solution.py:297
  234.5 23.0 %collective-permute-start.8 = (bf16[16,32,512]{2,1,0:T(8,128)(2,1)S(1)}, bf16[16,32,512]{2,1,0:T(8,128)(2,1)S(1)}, u32[]{:S(2)}, u32[]{:S(2)}) collective-permute-start(bf16[16,32,512]{2,1,0:T(8,128)(2,1)S(1)} %shard_map.96.refs_0_), channel_id=1, source_target_pairs={{0,1},{1,0},{2,3},{3,2},{4,5},{5,4},{6,7},{7,6},{8,9},{9,8},{10,11... | collective-permute-start | bytes 1572872 | tf_op jit(solution)/shard_map/ppermute | solution.py:297
  243.3 29.9 %collective-permute-start.26 = (bf16[128,2048]{1,0:T(8,128)(2,1)S(1)}, bf16[128,2048]{1,0:T(8,128)(2,1)S(1)}, u32[]{:S(2)}, u32[]{:S(2)}) collective-permute-start(bf16[128,2048]{1,0:T(8,128)(2,1)S(1)} %get-tuple-element.29), channel_id=1, source_target_pairs={{0,4},{1,5},{2,6},{3,7},{4,0},{5,1},{6,2},{7,3},{8,12},{9,13},{10,... | collective-permute-start | bytes 1572872 | tf_op jit(solution)/shard_map/ppermute | solution.py:297
  246.1 28.6 %collective-permute-start.27 = (bf16[128,2048]{1,0:T(8,128)(2,1)S(1)}, bf16[128,2048]{1,0:T(8,128)(2,1)S(1)}, u32[]{:S(2)}, u32[]{:S(2)}) collective-permute-start(bf16[128,2048]{1,0:T(8,128)(2,1)S(1)} %get-tuple-element.30), channel_id=1, source_target_pairs={{0,8},{1,9},{2,10},{3,11},{4,12},{5,13},{6,14},{7,15},{8,0},{9,1},... | collective-permute-start | bytes 1572872 | tf_op jit(solution)/shard_map/ppermute | solution.py:297
  249.7 35.7 %collective-permute-start.28 = (bf16[128,2048]{1,0:T(8,128)(2,1)S(1)}, bf16[128,2048]{1,0:T(8,128)(2,1)S(1)}, u32[]{:S(2)}, u32[]{:S(2)}) collective-permute-start(bf16[128,2048]{1,0:T(8,128)(2,1)S(1)} %get-tuple-element.31), channel_id=1, source_target_pairs={{0,12},{1,13},{2,14},{3,15},{4,8},{5,9},{6,10},{7,11},{8,4},{9,5},... | collective-permute-start | bytes 1572872 | tf_op jit(solution)/shard_map/ppermute | solution.py:297
  266.8 26.6 %collective-permute-start.17 = (bf16[128,2048]{1,0:T(8,128)(2,1)}, bf16[128,2048]{1,0:T(8,128)(2,1)S(1)}, u32[]{:S(2)}, u32[]{:S(2)}) collective-permute-start(bf16[128,2048]{1,0:T(8,128)(2,1)} %get-tuple-element.21), channel_id=1, source_target_pairs={{0,4},{1,5},{2,6},{3,7},{4,0},{5,1},{6,2},{7,3},{8,12},{9,13},{10,... | collective-permute-start | bytes 1572872 | tf_op jit(solution)/shard_map/ppermute | solution.py:297
  269.6 26.5 %collective-permute-start.18 = (bf16[128,2048]{1,0:T(8,128)(2,1)S(1)}, bf16[128,2048]{1,0:T(8,128)(2,1)S(1)}, u32[]{:S(2)}, u32[]{:S(2)}) collective-permute-start(bf16[128,2048]{1,0:T(8,128)(2,1)S(1)} %get-tuple-element.22), channel_id=1, source_target_pairs={{0,8},{1,9},{2,10},{3,11},{4,12},{5,13},{6,14},{7,15},{8,0},{9,1},... | collective-permute-start | bytes 1572872 | tf_op jit(solution)/shard_map/ppermute | solution.py:297
  273.2 34.8 %collective-permute-start.19 = (bf16[128,2048]{1,0:T(8,128)(2,1)S(1)}, bf16[128,2048]{1,0:T(8,128)(2,1)S(1)}, u32[]{:S(2)}, u32[]{:S(2)}) collective-permute-start(bf16[128,2048]{1,0:T(8,128)(2,1)S(1)} %get-tuple-element.23), channel_id=1, source_target_pairs={{0,12},{1,13},{2,14},{3,15},{4,8},{5,9},{6,10},{7,11},{8,4},{9,5},... | collective-permute-start | bytes 1572872 | tf_op jit(solution)/shard_map/ppermute | solution.py:297
  289.7 24.2 %collective-permute-start.29 = (bf16[32,2048]{1,0:T(8,128)(2,1)}, bf16[32,2048]{1,0:T(8,128)(2,1)S(1)}, u32[]{:S(2)}, u32[]{:S(2)}) collective-permute-start(bf16[32,2048]{1,0:T(8,128)(2,1)} %get-tuple-element.33), channel_id=1, source_target_pairs={{0,1},{1,0},{2,3},{3,2},{4,5},{5,4},{6,7},{7,6},{8,9},{9,8},{10,11... | collective-permute-start | bytes 393224 | tf_op jit(solution)/shard_map/ppermute | solution.py:297
  291.5 24.8 %collective-permute-start.30 = (bf16[32,2048]{1,0:T(8,128)(2,1)}, bf16[32,2048]{1,0:T(8,128)(2,1)S(1)}, u32[]{:S(2)}, u32[]{:S(2)}) collective-permute-start(bf16[32,2048]{1,0:T(8,128)(2,1)} %get-tuple-element.34), channel_id=1, source_target_pairs={{0,2},{1,3},{2,0},{3,1},{4,6},{5,7},{6,4},{7,5},{8,10},{9,11},{10,... | collective-permute-start | bytes 393224 | tf_op jit(solution)/shard_map/ppermute | solution.py:297
  293.4 22.9 %collective-permute-start.31 = (bf16[32,2048]{1,0:T(8,128)(2,1)}, bf16[32,2048]{1,0:T(8,128)(2,1)S(1)}, u32[]{:S(2)}, u32[]{:S(2)}) collective-permute-start(bf16[32,2048]{1,0:T(8,128)(2,1)} %get-tuple-element.35), channel_id=1, source_target_pairs={{0,3},{1,2},{2,1},{3,0},{4,7},{5,6},{6,5},{7,4},{8,11},{9,10},{10,... | collective-permute-start | bytes 393224 | tf_op jit(solution)/shard_map/ppermute | solution.py:297
  (34 other events, 398.8 us)

commit v2 on v1

--- a/solution.py
+++ b/solution.py
@@ -17,11 +17,12 @@
 PARTS = 2
 Y_COUNT = 4
 ANY = pl.ANY
+VMEM_SPEC = pl.BlockSpec(memory_space=pltpu.VMEM)
 
 
 def attend_kernel(
     own_ref, loc_ref, core_ref, q_ref, first_ref, second_ref, out_ref,
-    k_ref, v_ref, vt_ref, qt_ref, acc_ref, max_ref, sum_ref, top_ref, factor_ref, sems, *tile_refs,
+    k_ref, vt_ref, qt_ref, acc_ref, max_ref, sum_ref, top_ref, factor_ref, *tile_refs,
     rows, part, heads, run,
 ):
     span = pl.program_id(0)
@@ -33,27 +34,20 @@
 
     @pl.when(span == 0)
     def _():
-        def fetch(k_src, v_src):
-            copies = []
-            for s in range(slots):
-                dst = pl.ds(s * block_rows, block_rows)
-                copies.append(pltpu.make_async_copy(k_src.at[s, pl.ds(0, block_rows)], k_ref.at[dst], sems.at[s]))
-                copies.append(pltpu.make_async_copy(v_src.at[s, pl.ds(0, block_rows)], v_ref.at[dst], sems.at[slots + s]))
-            for c in copies:
-                c.start()
-            for c in copies:
-                c.wait()
+        def take(keys, values):
+            for i in range(slots):
+                at = i * block_rows
+                k_ref[at:at + block_rows, :] = keys[i, :block_rows, :]
+                for b in range(0, block_rows, SPAN):
+                    vt_ref[(at + b) // SPAN] = values[i, b:b + SPAN, :].T
 
         @pl.when(core_ref[0] == 0)
         def _():
-            fetch(first_ref, second_ref)
+            take(first_ref, second_ref)
 
         @pl.when(core_ref[0] != 0)
         def _():
-            fetch(second_ref, first_ref)
-
-        for b in range(k_ref.shape[0] // SPAN):
-            vt_ref[b] = v_ref[b * SPAN:(b + 1) * SPAN, :].T
+            take(second_ref, first_ref)
 
     own = own_ref[span]
     q_all = q_ref[...].reshape(nrow, heads * HD)
@@ -136,12 +130,11 @@
             grid=(spans,),
             in_specs=[
                 pl.BlockSpec((per, rows, width), lambda s, *_: (s, part, 0)),
-                pl.BlockSpec(memory_space=ANY),
-                pl.BlockSpec(memory_space=ANY),
+                VMEM_SPEC,
+                VMEM_SPEC,
             ],
             out_specs=pl.BlockSpec((per, rows, width), lambda s, *_: (s, 0, 0)),
             scratch_shapes=[
-                pltpu.VMEM((keys, HD), jnp.bfloat16),
                 pltpu.VMEM((keys, HD), jnp.bfloat16),
                 pltpu.VMEM((keys // SPAN, HD, SPAN), jnp.bfloat16),
                 pltpu.VMEM((HD, per * rows * heads), jnp.bfloat16),
@@ -150,33 +143,27 @@
                 pltpu.VMEM((groups, 8, GW), jnp.float32),
                 pltpu.VMEM((groups, 8, GW), jnp.float32),
                 pltpu.VMEM((groups, 8, GW), jnp.float32),
-                pltpu.SemaphoreType.DMA((2 * slots,)),
             ]
             + [pltpu.VMEM((SPAN, GW), jnp.float32)] * groups
             + [pltpu.VMEM((SPAN, GW), jnp.bfloat16)] * groups,
         ),
-        compiler_params=pltpu.CompilerParams(dimension_semantics=("arbitrary",), vmem_limit_bytes=40 * 2**20),
+        compiler_params=pltpu.CompilerParams(dimension_semantics=("arbitrary",), vmem_limit_bytes=20 * 2**20),
         cost_estimate=pl.CostEstimate(flops=8 * HD * pairs, bytes_accessed=4 * keys * HD, transcendentals=pairs),
     )(own, loc, core, queries.reshape(tp_count, run, width), first, second)
 
 
 def stack_kernel(*refs):
-    ins, out_ref, sems = refs[:-2], refs[-2], refs[-1]
-    copies = [pltpu.make_async_copy(x, out_ref.at[i], sems.at[i]) for i, x in enumerate(ins)]
-    for c in copies:
-        c.start()
-    for c in copies:
-        c.wait()
+    for i, x in enumerate(refs[:-1]):
+        refs[-1][i] = x[...]
 
 
 def stacked(pieces):
-    shape = (len(pieces), *pieces[0].shape)
     return pl.pallas_call(
         stack_kernel,
-        out_shape=jax.ShapeDtypeStruct(shape, pieces[0].dtype),
-        in_specs=[pl.BlockSpec(memory_space=ANY)] * len(pieces),
-        out_specs=pl.BlockSpec(memory_space=ANY),
-        scratch_shapes=[pltpu.SemaphoreType.DMA((len(pieces),))],
+        out_shape=jax.ShapeDtypeStruct((len(pieces), *pieces[0].shape), pieces[0].dtype),
+        in_specs=[VMEM_SPEC] * len(pieces),
+        out_specs=VMEM_SPEC,
+        compiler_params=pltpu.CompilerParams(vmem_limit_bytes=8 * 2**20),
     )(*pieces)
 
 
@@ -196,7 +183,7 @@
         o[...] = acc_ref[pl.ds(pl.multiple_of((place_ref[1] ^ i) * n, n), n), :].astype(jnp.bfloat16)
 
 
-def project(place, atts, weight, paired, far):
+def project(place, atts, kept, paired, far):
     tps, r, k = atts[0].shape
     rows, cut = tps * r, far[0].shape[-1]
     blocks = len(far)
@@ -207,46 +194,37 @@
         grid_spec=pltpu.PrefetchScalarGridSpec(
             num_scalar_prefetch=1,
             grid=(blocks,),
-            in_specs=[pl.BlockSpec((tps, r, k), lambda j, p: (0, 0, 0))] * 4
-            + [
-                pl.BlockSpec((k, cut), lambda j, p: (0, p[0] * blocks + col(j, p))),
-                pl.BlockSpec((k, cut), lambda j, p: (0, col(j, p))),
-            ]
-            + [pl.BlockSpec(far[0].shape, lambda j, p: (0, 0, 0))] * blocks,
+            in_specs=[VMEM_SPEC] * 4
+            + [pl.BlockSpec((k, cut), lambda j, p: (0, col(j, p)))] * 2
+            + [VMEM_SPEC] * blocks,
             out_specs=[pl.BlockSpec((rows // 4, cut), lambda j, p: (0, col(j, p)))] * 4,
             scratch_shapes=[pltpu.VMEM((rows, cut), jnp.float32)],
         ),
-        compiler_params=pltpu.CompilerParams(dimension_semantics=("arbitrary",), vmem_limit_bytes=40 * 2**20),
+        compiler_params=pltpu.CompilerParams(dimension_semantics=("arbitrary",), vmem_limit_bytes=20 * 2**20),
         cost_estimate=pl.CostEstimate(flops=8 * rows * k * cut * blocks, bytes_accessed=8 * k * cut * blocks, transcendentals=0),
         name="project",
-    )(place, *atts, weight, paired, *far)
-
-
-def gather_kernel(m_ref, *refs):
+    )(place, *atts, kept, paired, *far)
+
+
+def add_kernel(m_ref, *refs):
     ins, outs = refs[:4], refs[4:]
-    step = pl.program_id(0)
-    total = ins[0][...].astype(jnp.float32)
-    for i in ins[1:]:
-        total = total + i[...].astype(jnp.float32)
+    r = outs[0].shape[0]
     for i, o in enumerate(outs):
-        @pl.when(step == i)
-        def _(o=o):
-            o[...] = total.astype(jnp.bfloat16)
+        rows = pl.ds(pl.multiple_of((m_ref[0] ^ i) * r, r), r)
+        total = ins[0][rows, :].astype(jnp.float32)
+        for x in ins[1:]:
+            total = total + x[rows, :].astype(jnp.float32)
+        o[...] = total.astype(jnp.bfloat16)
 
 
 def add_parts(member, parts):
     rows, n = parts[0].shape
-    r = rows // 4
-    return pl.pallas_call(
-        gather_kernel,
-        out_shape=[jax.ShapeDtypeStruct((r, n), jnp.bfloat16)] * 4,
-        grid_spec=pltpu.PrefetchScalarGridSpec(
-            num_scalar_prefetch=1,
-            grid=(4,),
-            in_specs=[pl.BlockSpec((r, n), lambda i, m: (m[0] ^ i, 0))] * 4,
-            out_specs=[pl.BlockSpec((r, n), lambda i, m: (0, 0))] * 4,
-        ),
-        compiler_params=pltpu.CompilerParams(dimension_semantics=("arbitrary",)),
+    return pl.pallas_call(
+        add_kernel,
+        out_shape=[jax.ShapeDtypeStruct((rows // 4, n), jnp.bfloat16)] * 4,
+        in_specs=[pl.BlockSpec(memory_space=pltpu.SMEM)] + [VMEM_SPEC] * 4,
+        out_specs=[VMEM_SPEC] * 4,
+        compiler_params=pltpu.CompilerParams(vmem_limit_bytes=8 * 2**20),
         cost_estimate=pl.CostEstimate(flops=4 * rows * n, bytes_accessed=10 * rows * n, transcendentals=0),
         name="add_parts",
     )(member, *parts)
@@ -272,7 +250,6 @@
     rows, width = residual.shape
     r = rows // PARTS
     whole = pl.BlockSpec((r, width), lambda i, *_: (part, 0))
-    small = pl.BlockSpec(parts[0].shape, lambda i, *_: (0, 0))
     kernel = finish_kernel
     if before:
         kernel = lambda m, s, res, g, a, b, c, d, e, f, *rest: finish_kernel(m, s, res, g, a, b, c, d, *rest)
@@ -283,12 +260,13 @@
             num_scalar_prefetch=2,
             grid=(1,),
             in_specs=[whole, pl.BlockSpec((1, width), lambda i, *_: (0, 0))]
-            + [small] * 4
+            + [VMEM_SPEC] * 4
             + [pl.BlockSpec(memory_space=ANY)] * len(before),
             out_specs=[whole] * 2,
             scratch_shapes=[pltpu.VMEM((r, width), jnp.float32)],
         ),
         input_output_aliases={8 + i: i for i in range(len(before))},
+        compiler_params=pltpu.CompilerParams(vmem_limit_bytes=12 * 2**20),
         cost_estimate=pl.CostEstimate(flops=8 * r * width, bytes_accessed=10 * r * width, transcendentals=0),
     )(member, static_scale, residual, gain, *parts, *before)
 
@@ -351,7 +329,7 @@
     for dy in (1, 2, 3):
         pairs = [(c, c - c % Y_COUNT + (c + dy) % Y_COUNT) for c in range(ctx_count)]
         far.append(lax.ppermute(side, "ctx", pairs))
-    w = lax.dynamic_slice_in_dim(out_weight, (member ^ 1) * quarter, quarter, 1)
+    kept, w = (lax.dynamic_slice_in_dim(out_weight, (member ^ i) * quarter, quarter, 1) for i in (0, 1))
     paired = swapped(w, 1, tp_count)
     place = jnp.stack([member, group, y_rank])
 
@@ -361,7 +339,7 @@
         atts = [att]
         for i in (1, 2, 3):
             atts.append(swapped(att, i, tp_count))
-        sent = project(place, atts, out_weight, paired, far)
+        sent = project(place, atts, kept, paired, far)
         got = [sent[0]]
         for i in (1, 2, 3):
             got.append(swapped(sent[i], 4 * i, tp_count))

time: 326 us -> 220 us (0.67)
  Pallas kernels: 163 us -> 55.7 us
  local copies, waits for them, and re-layouts: 13.1 us -> 8.01 us
  waiting for transfers between devices: 98.3 us -> 103 us
    pallas_call x4, Pallas kernels: 105 us -> 0.72 us  [the longest x2 0.51 us: add_parts(): pl.pallas_call(add_kernel, out_shape=[jax.ShapeDtypeStruct((rows // 4, n)...]
    unnamed x52 -> x8, local copies, waits for them, and re-layouts: 6.8 us -> 0.02 us
    ppermute x22, waiting for transfers between devices: 50.6 us -> 55 us  [swapped(): return lax.ppermute(value, 'tp', [(i, i ^ mask) for i in range(count)])]
  transfers between devices with their start and end apart: 32 -> 32, of which waited for: 12 -> 13; matrix products, arithmetic and copies ran while one was open for 2% -> 3% of each run, Pallas kernels for 29% -> 25%
where the time goes in v2:
time: 220 us
  waiting for transfers between devices  103 us (47%)
  Pallas kernels  55.7 us (25%)
  starting transfers between devices  49.8 us (23%)
  local copies, waits for them, and re-layouts  8.01 us (4%)
    ppermute x22, waiting for transfers between devices, swapped(): return lax.ppermute(value, 'tp', [(i, i ^ mask) for i in range(count)])  55 us
    ppermute x22, starting transfers between devices, swapped(): return lax.ppermute(value, 'tp', [(i, i ^ mask) for i in range(count)])  38.3 us
    pallas_call x2, Pallas kernels, attend(): pl.pallas_call(functools.partial(attend_kernel, rows=rows, part=part, hea...  36.2 us
    ppermute x7, waiting for transfers between devices, shards(): pieces.append(lax.ppermute(mine, 'ctx', pairs))  25.8 us
    ppermute x3, waiting for transfers between devices, shards(): far.append(lax.ppermute(side, 'ctx', pairs))  22.6 us
    pallas_call x2, Pallas kernels, project(): pl.pallas_call(project_kernel, out_shape=[jax.ShapeDtypeStruct((rows // 4...  16 us
    ppermute x7, starting transfers between devices, shards(): pieces.append(lax.ppermute(mine, 'ctx', pairs))  5.87 us
    ppermute x3, starting transfers between devices, shards(): far.append(lax.ppermute(side, 'ctx', pairs))  5.65 us
  transfers between devices with their start and end apart: 32, of which 13 were waited for; matrix products, arithmetic and copies ran while one was open for 3% of the time, Pallas kernels for 25%

profile of v2, /device:TPU:25, one launch (start us, length us, event | category | flops | bytes accessed | tf_op | source)
XLA Modules:
  0.0 220.0 jit_solution(9142120168967962754)
XLA Ops:
  8.6 14.8 %collective-permute-done.6.refs_7_ = bf16[1040,128]{1,0:T(8,128)(2,1)S(1)} collective-permute-done((bf16[1040,128]{1,0:T(8,128)(2,1)S(1)}, bf16[1040,128]{1,0:T(8,128)(2,1)S(1)}, u32[]{:S(2)}, u32[]{:S(2)}) %collective-permute-start.6) | collective-permute-done | bytes 266272 | tf_op jit(solution)/shard_map/ppermute | solution.py:314
  23.5 6.9 %collective-permute-done.3.refs_4_ = bf16[1040,128]{1,0:T(8,128)(2,1)S(1)} collective-permute-done((bf16[1040,128]{1,0:T(8,128)(2,1)S(1)}, bf16[1040,128]{1,0:T(8,128)(2,1)S(1)}, u32[]{:S(2)}, u32[]{:S(2)}) %collective-permute-start.3) | collective-permute-done | bytes 266272 | tf_op jit(solution)/shard_map/ppermute | solution.py:314
  30.4 4.0 %collective-permute-done.2.refs_3_ = bf16[1040,128]{1,0:T(8,128)(2,1)S(1)} collective-permute-done((bf16[1040,128]{1,0:T(8,128)(2,1)S(1)}, bf16[1040,128]{1,0:T(8,128)(2,1)S(1)}, u32[]{:S(2)}, u32[]{:S(2)}) %collective-permute-start.2) | collective-permute-done | bytes 266272 | tf_op jit(solution)/shard_map/ppermute | solution.py:314
  39.8 4.9 %constant_dynamic-slice_fusion.2 = (bf16[512,2048]{1,0:T(8,128)(2,1)}, bf16[512,2048]{1,0:T(8,128)(2,1)}) fusion(bf16[512,8192]{1,0:T(8,128)(2,1)} %param.12, s32[]{:T(128)S(6)} %select_n.39, s32[]{:T(128)S(6)} %select_n.38), kind=kLoop, calls=%fused_computation.10 | loop fusion | bytes 8388616 | tf_op jit(solution)/shard_map/dynamic_slice | solution.py:332
  45.9 7.0 %collective-permute-done.13.refs_1_ = bf16[512,512]{1,0:T(8,128)(2,1)S(1)} collective-permute-done((bf16[512,512]{1,0:T(8,128)(2,1)}, bf16[512,512]{1,0:T(8,128)(2,1)S(1)}, u32[]{:S(2)}, u32[]{:S(2)}) %collective-permute-start.13) | collective-permute-done | bytes 524320 | tf_op jit(solution)/shard_map/ppermute | solution.py:275
  52.8 10.2 %collective-permute-done.12.refs_0_ = bf16[512,512]{1,0:T(8,128)(2,1)S(1)} collective-permute-done((bf16[512,512]{1,0:T(8,128)(2,1)}, bf16[512,512]{1,0:T(8,128)(2,1)S(1)}, u32[]{:S(2)}, u32[]{:S(2)}) %collective-permute-start.12) | collective-permute-done | bytes 524320 | tf_op jit(solution)/shard_map/ppermute | solution.py:275
  64.5 4.3 %collective-permute-start.15 = (bf16[2,512,512]{2,1,0:T(8,128)(2,1)S(1)}, bf16[2,512,512]{2,1,0:T(8,128)(2,1)S(1)}, u32[]{:S(2)}, u32[]{:S(2)}) collective-permute-start(bf16[2,512,512]{2,1,0:T(8,128)(2,1)S(1)} %shard_map.97.refs_6_), channel_id=1, source_target_pairs={{0,32},{16,48},{32,0},{48,16},{64,96},{80,112},{96,64},{112,80},{1... | collective-permute-start | bytes 3145736 | tf_op jit(solution)/shard_map/ppermute | solution.py:331
  68.8 18.1 %shard_map.98.refs_0_ = bf16[16,32,512]{2,1,0:T(8,128)(2,1)S(1)} custom-call(s32[2]{0:T(128)S(1)} %get-tuple-element.39.own_ref, s32[16]{0:T(128)S(1)} %select_reduce_fusion.loc_ref, s32[1]{0:T(128)} %bitcast.4.core_ref, bf16[16,64,512]{2,1,0:T(8,128)(2,1)S(1)} %bitcast.8, bf16[8,1040,128]{2,1,0:T(8,128)(2,1)S(1)} %shard_map.95.first_ref, ...), custom_call_target="tpu_custom_call" | custom-call | flops 17179869184 | bytes 4194304 | tf_op jit(solution)/shard_map/pallas_call | solution.py:125
  86.9 2.8 %collective-permute-start.25 = (bf16[16,32,512]{2,1,0:T(8,128)(2,1)S(1)}, bf16[16,32,512]{2,1,0:T(8,128)(2,1)S(1)}, u32[]{:S(2)}, u32[]{:S(2)}) collective-permute-start(bf16[16,32,512]{2,1,0:T(8,128)(2,1)S(1)} %shard_map.98.refs_0_), channel_id=1, source_target_pairs={{0,3},{1,2},{2,1},{3,0},{4,7},{5,6},{6,5},{7,4},{8,11},{9,10},{10,... | collective-permute-start | bytes 1572872 | tf_op jit(solution)/shard_map/ppermute | solution.py:275
  91.3 22.2 %collective-permute-done.15.refs_8_ = bf16[2,512,512]{2,1,0:T(8,128)(2,1)S(1)} collective-permute-done((bf16[2,512,512]{2,1,0:T(8,128)(2,1)S(1)}, bf16[2,512,512]{2,1,0:T(8,128)(2,1)S(1)}, u32[]{:S(2)}, u32[]{:S(2)}) %collective-permute-start.15) | collective-permute-done | bytes 1048608 | tf_op jit(solution)/shard_map/ppermute | solution.py:331
  115.4 18.1 %shard_map.96.refs_0_ = bf16[16,32,512]{2,1,0:T(8,128)(2,1)S(1)} custom-call(s32[2]{0:T(128)S(1)} %get-tuple-element.39.own_ref, s32[16]{0:T(128)S(1)} %select_reduce_fusion.loc_ref, s32[1]{0:T(128)} %bitcast.4.core_ref, bf16[16,64,512]{2,1,0:T(8,128)(2,1)S(1)} %bitcast.9, bf16[8,1040,128]{2,1,0:T(8,128)(2,1)S(1)} %shard_map.95.first_ref, ...), custom_call_target="tpu_custom_call" | custom-call | flops 17179869184 | bytes 4194304 | tf_op jit(solution)/shard_map/pallas_call | solution.py:125
  135.8 8.0 %project.3 = (bf16[128,2048]{1,0:T(8,128)(2,1)S(1)}, bf16[128,2048]{1,0:T(8,128)(2,1)S(1)}, bf16[128,2048]{1,0:T(8,128)(2,1)S(1)}, bf16[128,2048]{1,0:T(8,128)(2,1)S(1)}) custom-call(s32[3]{0:T(128)S(1)} %pad_add_fusion.place_ref, bf16[16,32,512]{2,1,0:T(8,128)(2,1)S(1)} %shard_map.98.refs_0_, bf16[16,32,512]{2,1,0:T(8,128)(2,1)S(1)} %collective-permute-done.23.refs_1_, ...), custom_call_target="tpu_custom_call" | custom-call | flops 4294967296 | bytes 8388608 | tf_op jit(solution)/shard_map/project/pallas_call | solution.py:191
  143.8 2.8 %collective-permute-start.26 = (bf16[128,2048]{1,0:T(8,128)(2,1)S(1)}, bf16[128,2048]{1,0:T(8,128)(2,1)S(1)}, u32[]{:S(2)}, u32[]{:S(2)}) collective-permute-start(bf16[128,2048]{1,0:T(8,128)(2,1)S(1)} %get-tuple-element.29), channel_id=1, source_target_pairs={{0,4},{1,5},{2,6},{3,7},{4,0},{5,1},{6,2},{7,3},{8,12},{9,13},{10,... | collective-permute-start | bytes 1572872 | tf_op jit(solution)/shard_map/ppermute | solution.py:275
  146.7 3.6 %collective-permute-start.27 = (bf16[128,2048]{1,0:T(8,128)(2,1)S(1)}, bf16[128,2048]{1,0:T(8,128)(2,1)S(1)}, u32[]{:S(2)}, u32[]{:S(2)}) collective-permute-start(bf16[128,2048]{1,0:T(8,128)(2,1)S(1)} %get-tuple-element.30), channel_id=1, source_target_pairs={{0,8},{1,9},{2,10},{3,11},{4,12},{5,13},{6,14},{7,15},{8,0},{9,1},... | collective-permute-start | bytes 1572872 | tf_op jit(solution)/shard_map/ppermute | solution.py:275
  150.3 3.6 %collective-permute-start.28 = (bf16[128,2048]{1,0:T(8,128)(2,1)S(1)}, bf16[128,2048]{1,0:T(8,128)(2,1)S(1)}, u32[]{:S(2)}, u32[]{:S(2)}) collective-permute-start(bf16[128,2048]{1,0:T(8,128)(2,1)S(1)} %get-tuple-element.31), channel_id=1, source_target_pairs={{0,12},{1,13},{2,14},{3,15},{4,8},{5,9},{6,10},{7,11},{8,4},{9,5},... | collective-permute-start | bytes 1572872 | tf_op jit(solution)/shard_map/ppermute | solution.py:275
  153.9 4.1 %collective-permute-done.9.refs_2_ = bf16[16,32,512]{2,1,0:T(8,128)(2,1)S(1)} collective-permute-done((bf16[16,32,512]{2,1,0:T(8,128)(2,1)S(1)}, bf16[16,32,512]{2,1,0:T(8,128)(2,1)S(1)}, u32[]{:S(2)}, u32[]{:S(2)}) %collective-permute-start.9) | collective-permute-done | bytes 524320 | tf_op jit(solution)/shard_map/ppermute | solution.py:275
  158.0 8.0 %project.2 = (bf16[128,2048]{1,0:T(8,128)(2,1)S(1)}, bf16[128,2048]{1,0:T(8,128)(2,1)S(1)}, bf16[128,2048]{1,0:T(8,128)(2,1)S(1)}, bf16[128,2048]{1,0:T(8,128)(2,1)S(1)}) custom-call(s32[3]{0:T(128)S(1)} %pad_add_fusion.place_ref, bf16[16,32,512]{2,1,0:T(8,128)(2,1)S(1)} %shard_map.96.refs_0_, bf16[16,32,512]{2,1,0:T(8,128)(2,1)S(1)} %collective-permute-done.8.refs_1_, ...), custom_call_target="tpu_custom_call" | custom-call | flops 4294967296 | bytes 8388608 | tf_op jit(solution)/shard_map/project/pallas_call | solution.py:191
  166.0 2.8 %collective-permute-start.17 = (bf16[128,2048]{1,0:T(8,128)(2,1)S(1)}, bf16[128,2048]{1,0:T(8,128)(2,1)S(1)}, u32[]{:S(2)}, u32[]{:S(2)}) collective-permute-start(bf16[128,2048]{1,0:T(8,128)(2,1)S(1)} %get-tuple-element.21), channel_id=1, source_target_pairs={{0,4},{1,5},{2,6},{3,7},{4,0},{5,1},{6,2},{7,3},{8,12},{9,13},{10,... | collective-permute-start | bytes 1572872 | tf_op jit(solution)/shard_map/ppermute | solution.py:275
  168.8 3.6 %collective-permute-start.18 = (bf16[128,2048]{1,0:T(8,128)(2,1)S(1)}, bf16[128,2048]{1,0:T(8,128)(2,1)S(1)}, u32[]{:S(2)}, u32[]{:S(2)}) collective-permute-start(bf16[128,2048]{1,0:T(8,128)(2,1)S(1)} %get-tuple-element.22), channel_id=1, source_target_pairs={{0,8},{1,9},{2,10},{3,11},{4,12},{5,13},{6,14},{7,15},{8,0},{9,1},... | collective-permute-start | bytes 1572872 | tf_op jit(solution)/shard_map/ppermute | solution.py:275
  172.4 2.9 %collective-permute-start.19 = (bf16[128,2048]{1,0:T(8,128)(2,1)S(1)}, bf16[128,2048]{1,0:T(8,128)(2,1)S(1)}, u32[]{:S(2)}, u32[]{:S(2)}) collective-permute-start(bf16[128,2048]{1,0:T(8,128)(2,1)S(1)} %get-tuple-element.23), channel_id=1, source_target_pairs={{0,12},{1,13},{2,14},{3,15},{4,8},{5,9},{6,10},{7,11},{8,4},{9,5},... | collective-permute-start | bytes 1572872 | tf_op jit(solution)/shard_map/ppermute | solution.py:275
  175.3 10.7 %collective-permute-done.28.refs_3_ = bf16[128,2048]{1,0:T(8,128)(2,1)S(1)} collective-permute-done((bf16[128,2048]{1,0:T(8,128)(2,1)S(1)}, bf16[128,2048]{1,0:T(8,128)(2,1)S(1)}, u32[]{:S(2)}, u32[]{:S(2)}) %collective-permute-start.28) | collective-permute-done | bytes 524320 | tf_op jit(solution)/shard_map/ppermute | solution.py:275
  188.1 5.8 %collective-permute-done.17.refs_1_ = bf16[128,2048]{1,0:T(8,128)(2,1)S(1)} collective-permute-done((bf16[128,2048]{1,0:T(8,128)(2,1)S(1)}, bf16[128,2048]{1,0:T(8,128)(2,1)S(1)}, u32[]{:S(2)}, u32[]{:S(2)}) %collective-permute-start.17) | collective-permute-done | bytes 524320 | tf_op jit(solution)/shard_map/ppermute | solution.py:275
  195.5 12.9 %collective-permute-done.19.refs_3_ = bf16[128,2048]{1,0:T(8,128)(2,1)S(1)} collective-permute-done((bf16[128,2048]{1,0:T(8,128)(2,1)S(1)}, bf16[128,2048]{1,0:T(8,128)(2,1)S(1)}, u32[]{:S(2)}, u32[]{:S(2)}) %collective-permute-start.19) | collective-permute-done | bytes 524320 | tf_op jit(solution)/shard_map/ppermute | solution.py:275
  215.5 3.1 %collective-permute-done.22.d = bf16[32,2048]{1,0:T(8,128)(2,1)S(1)} collective-permute-done((bf16[32,2048]{1,0:T(8,128)(2,1)S(1)}, bf16[32,2048]{1,0:T(8,128)(2,1)S(1)}, u32[]{:S(2)}, u32[]{:S(2)}) %collective-permute-start.22) | collective-permute-done | bytes 131104 | tf_op jit(solution)/shard_map/ppermute | solution.py:275
  (69 shorter events, 33.3 us)
Async XLA Ops:
  2.8 20.7 %collective-permute-start.6 = (bf16[1040,128]{1,0:T(8,128)(2,1)S(1)}, bf16[1040,128]{1,0:T(8,128)(2,1)S(1)}, u32[]{:S(2)}, u32[]{:S(2)}) collective-permute-start(bf16[1040,128]{1,0:T(8,128)(2,1)S(1)} %pad_maximum_fusion.refs_0_), channel_id=1, source_target_pairs={{0,112},{16,64},{32,80},{48,96},{64,48},{80,0},{96,16},{112,32},{1... | collective-permute-start | bytes 798728 | tf_op jit(solution)/shard_map/ppermute | solution.py:314
  4.6 18.8 %collective-permute-start.5 = (bf16[1040,128]{1,0:T(8,128)(2,1)S(1)}, bf16[1040,128]{1,0:T(8,128)(2,1)S(1)}, u32[]{:S(2)}, u32[]{:S(2)}) collective-permute-start(bf16[1040,128]{1,0:T(8,128)(2,1)S(1)} %pad_maximum_fusion.refs_0_), channel_id=1, source_target_pairs={{0,80},{16,96},{32,112},{48,64},{64,16},{80,32},{96,48},{112,0},{1... | collective-permute-start | bytes 798728 | tf_op jit(solution)/shard_map/ppermute | solution.py:314
  7.5 22.9 %collective-permute-start.3 = (bf16[1040,128]{1,0:T(8,128)(2,1)S(1)}, bf16[1040,128]{1,0:T(8,128)(2,1)S(1)}, u32[]{:S(2)}, u32[]{:S(2)}) collective-permute-start(bf16[1040,128]{1,0:T(8,128)(2,1)S(1)} %pad_maximum_fusion.refs_0_), channel_id=1, source_target_pairs={{0,64},{16,80},{32,96},{48,112},{64,0},{80,16},{96,32},{112,48},{1... | collective-permute-start | bytes 798728 | tf_op jit(solution)/shard_map/ppermute | solution.py:314
  8.0 26.4 %collective-permute-start.2 = (bf16[1040,128]{1,0:T(8,128)(2,1)S(1)}, bf16[1040,128]{1,0:T(8,128)(2,1)S(1)}, u32[]{:S(2)}, u32[]{:S(2)}) collective-permute-start(bf16[1040,128]{1,0:T(8,128)(2,1)S(1)} %pad_maximum_fusion.refs_0_), channel_id=1, source_target_pairs={{0,48},{16,0},{32,16},{48,32},{64,112},{80,64},{96,80},{112,96},{1... | collective-permute-start | bytes 798728 | tf_op jit(solution)/shard_map/ppermute | solution.py:314
  34.6 34.2 %collective-permute-start.7 = (bf16[8,1040,128]{2,1,0:T(8,128)(2,1)S(1)}, bf16[8,1040,128]{2,1,0:T(8,128)(2,1)}, u32[]{:S(2)}, u32[]{:S(2)}) collective-permute-start(bf16[8,1040,128]{2,1,0:T(8,128)(2,1)S(1)} %shard_map.95.first_ref), channel_id=1, source_target_pairs={{0,1},{1,0},{2,3},{3,2},{4,5},{5,4},{6,7},{7,6},{8,9},{9,8},{10,11... | collective-permute-start | bytes 6389768 | tf_op jit(solution)/shard_map/ppermute | solution.py:275
  39.5 23.5 %collective-permute-start.12 = (bf16[512,512]{1,0:T(8,128)(2,1)}, bf16[512,512]{1,0:T(8,128)(2,1)S(1)}, u32[]{:S(2)}, u32[]{:S(2)}) collective-permute-start(bf16[512,512]{1,0:T(8,128)(2,1)} %get-tuple-element.41), channel_id=1, source_target_pairs={{0,2},{1,3},{2,0},{3,1},{4,6},{5,7},{6,4},{7,5},{8,10},{9,11},{10,... | collective-permute-start | bytes 1572872 | tf_op jit(solution)/shard_map/ppermute | solution.py:275
  44.7 90.0 %collective-permute-start.11 = (bf16[512,2048]{1,0:T(8,128)(2,1)}, bf16[512,2048]{1,0:T(8,128)(2,1)}, u32[]{:S(2)}, u32[]{:S(2)}) collective-permute-start(bf16[512,2048]{1,0:T(8,128)(2,1)} %get-tuple-element.42), channel_id=1, source_target_pairs={{0,1},{1,0},{2,3},{3,2},{4,5},{5,4},{6,7},{7,6},{8,9},{9,8},{10,11... | collective-permute-start | bytes 6291464 | tf_op jit(solution)/shard_map/ppermute | solution.py:275
  63.1 27.0 %collective-permute-start.16 = (bf16[2,512,512]{2,1,0:T(8,128)(2,1)S(1)}, bf16[2,512,512]{2,1,0:T(8,128)(2,1)S(1)}, u32[]{:S(2)}, u32[]{:S(2)}) collective-permute-start(bf16[2,512,512]{2,1,0:T(8,128)(2,1)S(1)} %shard_map.97.refs_6_), channel_id=1, source_target_pairs={{0,48},{16,0},{32,16},{48,32},{64,112},{80,64},{96,80},{112,96},{1... | collective-permute-start | bytes 3145736 | tf_op jit(solution)/shard_map/ppermute | solution.py:331
  64.5 49.0 %collective-permute-start.15 = (bf16[2,512,512]{2,1,0:T(8,128)(2,1)S(1)}, bf16[2,512,512]{2,1,0:T(8,128)(2,1)S(1)}, u32[]{:S(2)}, u32[]{:S(2)}) collective-permute-start(bf16[2,512,512]{2,1,0:T(8,128)(2,1)S(1)} %shard_map.97.refs_6_), channel_id=1, source_target_pairs={{0,32},{16,48},{32,0},{48,16},{64,96},{80,112},{96,64},{112,80},{1... | collective-permute-start | bytes 3145736 | tf_op jit(solution)/shard_map/ppermute | solution.py:331
  68.8 64.7 %collective-permute-start.14 = (bf16[2,512,512]{2,1,0:T(8,128)(2,1)S(1)}, bf16[2,512,512]{2,1,0:T(8,128)(2,1)S(1)}, u32[]{:S(2)}, u32[]{:S(2)}) collective-permute-start(bf16[2,512,512]{2,1,0:T(8,128)(2,1)S(1)} %shard_map.97.refs_6_), channel_id=1, source_target_pairs={{0,16},{16,32},{32,48},{48,0},{64,80},{80,96},{96,112},{112,64},{1... | collective-permute-start | bytes 3145736 | tf_op jit(solution)/shard_map/ppermute | solution.py:331
  86.9 48.1 %collective-permute-start.25 = (bf16[16,32,512]{2,1,0:T(8,128)(2,1)S(1)}, bf16[16,32,512]{2,1,0:T(8,128)(2,1)S(1)}, u32[]{:S(2)}, u32[]{:S(2)}) collective-permute-start(bf16[16,32,512]{2,1,0:T(8,128)(2,1)S(1)} %shard_map.98.refs_0_), channel_id=1, source_target_pairs={{0,3},{1,2},{2,1},{3,0},{4,7},{5,6},{6,5},{7,4},{8,11},{9,10},{10,... | collective-permute-start | bytes 1572872 | tf_op jit(solution)/shard_map/ppermute | solution.py:275
  90.1 45.7 %collective-permute-start.24 = (bf16[16,32,512]{2,1,0:T(8,128)(2,1)S(1)}, bf16[16,32,512]{2,1,0:T(8,128)(2,1)S(1)}, u32[]{:S(2)}, u32[]{:S(2)}) collective-permute-start(bf16[16,32,512]{2,1,0:T(8,128)(2,1)S(1)} %shard_map.98.refs_0_), channel_id=1, source_target_pairs={{0,2},{1,3},{2,0},{3,1},{4,6},{5,7},{6,4},{7,5},{8,10},{9,11},{10,... | collective-permute-start | bytes 1572872 | tf_op jit(solution)/shard_map/ppermute | solution.py:275
  113.5 22.4 %collective-permute-start.23 = (bf16[16,32,512]{2,1,0:T(8,128)(2,1)S(1)}, bf16[16,32,512]{2,1,0:T(8,128)(2,1)S(1)}, u32[]{:S(2)}, u32[]{:S(2)}) collective-permute-start(bf16[16,32,512]{2,1,0:T(8,128)(2,1)S(1)} %shard_map.98.refs_0_), channel_id=1, source_target_pairs={{0,1},{1,0},{2,3},{3,2},{4,5},{5,4},{6,7},{7,6},{8,9},{9,8},{10,11... | collective-permute-start | bytes 1572872 | tf_op jit(solution)/shard_map/ppermute | solution.py:275
  134.7 23.3 %collective-permute-start.9 = (bf16[16,32,512]{2,1,0:T(8,128)(2,1)S(1)}, bf16[16,32,512]{2,1,0:T(8,128)(2,1)S(1)}, u32[]{:S(2)}, u32[]{:S(2)}) collective-permute-start(bf16[16,32,512]{2,1,0:T(8,128)(2,1)S(1)} %shard_map.96.refs_0_), channel_id=1, source_target_pairs={{0,2},{1,3},{2,0},{3,1},{4,6},{5,7},{6,4},{7,5},{8,10},{9,11},{10,... | collective-permute-start | bytes 1572872 | tf_op jit(solution)/shard_map/ppermute | solution.py:275
  135.0 23.0 %collective-permute-start.8 = (bf16[16,32,512]{2,1,0:T(8,128)(2,1)S(1)}, bf16[16,32,512]{2,1,0:T(8,128)(2,1)S(1)}, u32[]{:S(2)}, u32[]{:S(2)}) collective-permute-start(bf16[16,32,512]{2,1,0:T(8,128)(2,1)S(1)} %shard_map.96.refs_0_), channel_id=1, source_target_pairs={{0,1},{1,0},{2,3},{3,2},{4,5},{5,4},{6,7},{7,6},{8,9},{9,8},{10,11... | collective-permute-start | bytes 1572872 | tf_op jit(solution)/shard_map/ppermute | solution.py:275
  143.8 28.6 %collective-permute-start.26 = (bf16[128,2048]{1,0:T(8,128)(2,1)S(1)}, bf16[128,2048]{1,0:T(8,128)(2,1)S(1)}, u32[]{:S(2)}, u32[]{:S(2)}) collective-permute-start(bf16[128,2048]{1,0:T(8,128)(2,1)S(1)} %get-tuple-element.29), channel_id=1, source_target_pairs={{0,4},{1,5},{2,6},{3,7},{4,0},{5,1},{6,2},{7,3},{8,12},{9,13},{10,... | collective-permute-start | bytes 1572872 | tf_op jit(solution)/shard_map/ppermute | solution.py:275
  146.7 28.6 %collective-permute-start.27 = (bf16[128,2048]{1,0:T(8,128)(2,1)S(1)}, bf16[128,2048]{1,0:T(8,128)(2,1)S(1)}, u32[]{:S(2)}, u32[]{:S(2)}) collective-permute-start(bf16[128,2048]{1,0:T(8,128)(2,1)S(1)} %get-tuple-element.30), channel_id=1, source_target_pairs={{0,8},{1,9},{2,10},{3,11},{4,12},{5,13},{6,14},{7,15},{8,0},{9,1},... | collective-permute-start | bytes 1572872 | tf_op jit(solution)/shard_map/ppermute | solution.py:275
  150.3 35.7 %collective-permute-start.28 = (bf16[128,2048]{1,0:T(8,128)(2,1)S(1)}, bf16[128,2048]{1,0:T(8,128)(2,1)S(1)}, u32[]{:S(2)}, u32[]{:S(2)}) collective-permute-start(bf16[128,2048]{1,0:T(8,128)(2,1)S(1)} %get-tuple-element.31), channel_id=1, source_target_pairs={{0,12},{1,13},{2,14},{3,15},{4,8},{5,9},{6,10},{7,11},{8,4},{9,5},... | collective-permute-start | bytes 1572872 | tf_op jit(solution)/shard_map/ppermute | solution.py:275
  166.0 27.9 %collective-permute-start.17 = (bf16[128,2048]{1,0:T(8,128)(2,1)S(1)}, bf16[128,2048]{1,0:T(8,128)(2,1)S(1)}, u32[]{:S(2)}, u32[]{:S(2)}) collective-permute-start(bf16[128,2048]{1,0:T(8,128)(2,1)S(1)} %get-tuple-element.21), channel_id=1, source_target_pairs={{0,4},{1,5},{2,6},{3,7},{4,0},{5,1},{6,2},{7,3},{8,12},{9,13},{10,... | collective-permute-start | bytes 1572872 | tf_op jit(solution)/shard_map/ppermute | solution.py:275
  168.8 26.7 %collective-permute-start.18 = (bf16[128,2048]{1,0:T(8,128)(2,1)S(1)}, bf16[128,2048]{1,0:T(8,128)(2,1)S(1)}, u32[]{:S(2)}, u32[]{:S(2)}) collective-permute-start(bf16[128,2048]{1,0:T(8,128)(2,1)S(1)} %get-tuple-element.22), channel_id=1, source_target_pairs={{0,8},{1,9},{2,10},{3,11},{4,12},{5,13},{6,14},{7,15},{8,0},{9,1},... | collective-permute-start | bytes 1572872 | tf_op jit(solution)/shard_map/ppermute | solution.py:275
  172.4 36.0 %collective-permute-start.19 = (bf16[128,2048]{1,0:T(8,128)(2,1)S(1)}, bf16[128,2048]{1,0:T(8,128)(2,1)S(1)}, u32[]{:S(2)}, u32[]{:S(2)}) collective-permute-start(bf16[128,2048]{1,0:T(8,128)(2,1)S(1)} %get-tuple-element.23), channel_id=1, source_target_pairs={{0,12},{1,13},{2,14},{3,15},{4,8},{5,9},{6,10},{7,11},{8,4},{9,5},... | collective-permute-start | bytes 1572872 | tf_op jit(solution)/shard_map/ppermute | solution.py:275
  186.2 24.3 %collective-permute-start.29 = (bf16[32,2048]{1,0:T(8,128)(2,1)S(1)}, bf16[32,2048]{1,0:T(8,128)(2,1)S(1)}, u32[]{:S(2)}, u32[]{:S(2)}) collective-permute-start(bf16[32,2048]{1,0:T(8,128)(2,1)S(1)} %get-tuple-element.33), channel_id=1, source_target_pairs={{0,1},{1,0},{2,3},{3,2},{4,5},{5,4},{6,7},{7,6},{8,9},{9,8},{10,11... | collective-permute-start | bytes 393224 | tf_op jit(solution)/shard_map/ppermute | solution.py:275
  188.1 24.8 %collective-permute-start.30 = (bf16[32,2048]{1,0:T(8,128)(2,1)S(1)}, bf16[32,2048]{1,0:T(8,128)(2,1)S(1)}, u32[]{:S(2)}, u32[]{:S(2)}) collective-permute-start(bf16[32,2048]{1,0:T(8,128)(2,1)S(1)} %get-tuple-element.34), channel_id=1, source_target_pairs={{0,2},{1,3},{2,0},{3,1},{4,6},{5,7},{6,4},{7,5},{8,10},{9,11},{10,... | collective-permute-start | bytes 393224 | tf_op jit(solution)/shard_map/ppermute | solution.py:275
  193.9 19.0 %collective-permute-start.31 = (bf16[32,2048]{1,0:T(8,128)(2,1)S(1)}, bf16[32,2048]{1,0:T(8,128)(2,1)S(1)}, u32[]{:S(2)}, u32[]{:S(2)}) collective-permute-start(bf16[32,2048]{1,0:T(8,128)(2,1)S(1)} %get-tuple-element.35), channel_id=1, source_target_pairs={{0,3},{1,2},{2,1},{3,0},{4,7},{5,6},{6,5},{7,4},{8,11},{9,10},{10,... | collective-permute-start | bytes 393224 | tf_op jit(solution)/shard_map/ppermute | solution.py:275
  (12 other events, 214.8 us)

commit v3 on v2

--- a/solution.py
+++ b/solution.py
@@ -153,17 +153,22 @@
 
 
 def stack_kernel(*refs):
-    for i, x in enumerate(refs[:-1]):
-        refs[-1][i] = x[...]
+    ins, out_ref, sems = refs[:-2], refs[-2], refs[-1]
+    copies = [pltpu.make_async_copy(x, out_ref.at[i], sems.at[i]) for i, x in enumerate(ins)]
+    for c in copies:
+        c.start()
+    for c in copies:
+        c.wait()
 
 
 def stacked(pieces):
     return pl.pallas_call(
         stack_kernel,
         out_shape=jax.ShapeDtypeStruct((len(pieces), *pieces[0].shape), pieces[0].dtype),
-        in_specs=[VMEM_SPEC] * len(pieces),
+        in_specs=[pl.BlockSpec(memory_space=ANY)] * len(pieces),
         out_specs=VMEM_SPEC,
-        compiler_params=pltpu.CompilerParams(vmem_limit_bytes=8 * 2**20),
+        scratch_shapes=[pltpu.SemaphoreType.DMA((len(pieces),))],
+        compiler_params=pltpu.CompilerParams(vmem_limit_bytes=57 * 2**20),
     )(*pieces)
 
 
@@ -337,8 +342,9 @@
     for part in range(PARTS):
         att = attend(own, loc, core[None], queries, first, second, part, tp_count)
         atts = [att]
-        for i in (1, 2, 3):
-            atts.append(swapped(att, i, tp_count))
+        for source, mask in ((0, 2), (0, 1), (1, 1)):
+            atts.append(swapped(atts[source], mask, tp_count))
+        atts = [atts[i] for i in (0, 2, 1, 3)]
         sent = project(place, atts, kept, paired, far)
         got = [sent[0]]
         for i in (1, 2, 3):

time: 220 us -> 221 us (level)
  the two profiles are of different devices: /device:TPU:25 before, /device:TPU:17 now
where the time goes in v3:
time: 221 us; the launch traced here: 220 us
  Pallas kernels  76 us (34%)
  waiting for transfers between devices  69.8 us (32%)
  starting transfers between devices  54.7 us (25%)
  local copies, waits for them, and re-layouts  16.7 us (8%)
    ppermute x22, waiting for transfers between devices, swapped(): return lax.ppermute(value, 'tp', [(i, i ^ mask) for i in range(count)])  56.5 us
    pallas_call x2, Pallas kernels, attend(): pl.pallas_call(functools.partial(attend_kernel, rows=rows, part=part, hea...  50.1 us
    ppermute x22, starting transfers between devices, swapped(): return lax.ppermute(value, 'tp', [(i, i ^ mask) for i in range(count)])  31.1 us
    ppermute x7, starting transfers between devices, shards(): pieces.append(lax.ppermute(mine, 'ctx', pairs))  17.8 us
    pallas_call x2, Pallas kernels, project(): pl.pallas_call(project_kernel, out_shape=[jax.ShapeDtypeStruct((rows // 4...  17.5 us
    ppermute x7, waiting for transfers between devices, shards(): pieces.append(lax.ppermute(mine, 'ctx', pairs))  13.3 us
    unnamed x42, local copies, waits for them, and re-layouts  8.62 us
    ppermute x3, starting transfers between devices, shards(): far.append(lax.ppermute(side, 'ctx', pairs))  5.85 us
  transfers between devices with their start and end apart: 32, of which 13 were waited for; matrix products, arithmetic and copies ran while one was open for 3% of the time, Pallas kernels for 33%

profile of v3, /device:TPU:17, one launch (start us, length us, event | category | flops | bytes accessed | tf_op | source)
XLA Modules:
  0.0 220.4 jit_solution(1627257299347759483)
XLA Ops:
  10.0 3.9 %collective-permute-done.6.refs_7_ = bf16[1040,128]{1,0:T(8,128)(2,1)S(1)} collective-permute-done((bf16[1040,128]{1,0:T(8,128)(2,1)S(1)}, bf16[1040,128]{1,0:T(8,128)(2,1)S(1)}, u32[]{:S(2)}, u32[]{:S(2)}) %collective-permute-start.6) | collective-permute-done | bytes 266272 | tf_op jit(solution)/shard_map/ppermute | solution.py:319
  13.9 10.6 %collective-permute-start.1 = (bf16[1040,128]{1,0:T(8,128)(2,1)S(1)}, bf16[1040,128]{1,0:T(8,128)(2,1)S(1)}, u32[]{:S(2)}, u32[]{:S(2)}) collective-permute-start(bf16[1040,128]{1,0:T(8,128)(2,1)S(1)} %pad_maximum_fusion.refs_0_), channel_id=1, source_target_pairs={{0,16},{16,32},{32,48},{48,0},{64,80},{80,96},{96,112},{112,64},{1... | collective-permute-start | bytes 798728 | tf_op jit(solution)/shard_map/ppermute | solution.py:319
  24.5 4.7 %collective-permute-done.3.refs_4_ = bf16[1040,128]{1,0:T(8,128)(2,1)S(1)} collective-permute-done((bf16[1040,128]{1,0:T(8,128)(2,1)S(1)}, bf16[1040,128]{1,0:T(8,128)(2,1)S(1)}, u32[]{:S(2)}, u32[]{:S(2)}) %collective-permute-start.3) | collective-permute-done | bytes 266272 | tf_op jit(solution)/shard_map/ppermute | solution.py:319
  29.2 4.7 %collective-permute-done.refs_1_ = bf16[1040,128]{1,0:T(8,128)(2,1)S(1)} collective-permute-done((bf16[1040,128]{1,0:T(8,128)(2,1)S(1)}, bf16[1040,128]{1,0:T(8,128)(2,1)S(1)}, u32[]{:S(2)}, u32[]{:S(2)}) %collective-permute-start) | collective-permute-done | bytes 266272 | tf_op jit(solution)/shard_map/ppermute | solution.py:319
  34.6 2.9 %shard_map.95.first_ref = bf16[8,1040,128]{2,1,0:T(8,128)(2,1)} custom-call(bf16[1040,128]{1,0:T(8,128)(2,1)} %copy-done.13, bf16[1040,128]{1,0:T(8,128)(2,1)} %copy-done.20, bf16[1040,128]{1,0:T(8,128)(2,1)} %copy-done.19, bf16[1040,128]{1,0:T(8,128)(2,1)} %copy-done.18, bf16[1040,128]{1,0:T(8,128)(2,1)} %copy-done.17, bf16[1040,128]{1,0:T(8,128)(2,1)} %copy-done.16, ...), custom_call_target="tpu_custom_call" | custom-call | tf_op jit(solution)/shard_map/pallas_call | solution.py:165
  37.5 3.0 %collective-permute-start.7 = (bf16[8,1040,128]{2,1,0:T(8,128)(2,1)}, bf16[8,1040,128]{2,1,0:T(8,128)(2,1)}, u32[]{:S(2)}, u32[]{:S(2)}) collective-permute-start(bf16[8,1040,128]{2,1,0:T(8,128)(2,1)} %shard_map.95.first_ref), channel_id=1, source_target_pairs={{0,1},{1,0},{2,3},{3,2},{4,5},{5,4},{6,7},{7,6},{8,9},{9,8},{10,11... | collective-permute-start | bytes 6389768 | tf_op jit(solution)/shard_map/ppermute | solution.py:280
  44.2 5.0 %constant_dynamic-slice_fusion.2 = (bf16[512,2048]{1,0:T(8,128)(2,1)}, bf16[512,2048]{1,0:T(8,128)(2,1)}) fusion(bf16[512,8192]{1,0:T(8,128)(2,1)} %param.12, s32[]{:T(128)S(6)} %select_n.39, s32[]{:T(128)S(6)} %select_n.38), kind=kLoop, calls=%fused_computation.10 | loop fusion | bytes 8388616 | tf_op jit(solution)/shard_map/dynamic_slice | solution.py:337
  50.3 7.0 %collective-permute-done.13.refs_1_ = bf16[512,512]{1,0:T(8,128)(2,1)} collective-permute-done((bf16[512,512]{1,0:T(8,128)(2,1)}, bf16[512,512]{1,0:T(8,128)(2,1)}, u32[]{:S(2)}, u32[]{:S(2)}) %collective-permute-start.13) | collective-permute-done | bytes 524320 | tf_op jit(solution)/shard_map/ppermute | solution.py:280
  57.3 10.2 %collective-permute-done.12.refs_0_ = bf16[512,512]{1,0:T(8,128)(2,1)} collective-permute-done((bf16[512,512]{1,0:T(8,128)(2,1)}, bf16[512,512]{1,0:T(8,128)(2,1)}, u32[]{:S(2)}, u32[]{:S(2)}) %collective-permute-start.12) | collective-permute-done | bytes 524320 | tf_op jit(solution)/shard_map/ppermute | solution.py:280
  69.8 3.8 %collective-permute-start.15 = (bf16[2,512,512]{2,1,0:T(8,128)(2,1)}, bf16[2,512,512]{2,1,0:T(8,128)(2,1)S(1)}, u32[]{:S(2)}, u32[]{:S(2)}) collective-permute-start(bf16[2,512,512]{2,1,0:T(8,128)(2,1)} %shard_map.97.refs_6_), channel_id=1, source_target_pairs={{0,32},{16,48},{32,0},{48,16},{64,96},{80,112},{96,64},{112,80},{1... | collective-permute-start | bytes 3145736 | tf_op jit(solution)/shard_map/ppermute | solution.py:336
  75.6 25.0 %shard_map.98.refs_0_ = bf16[16,32,512]{2,1,0:T(8,128)(2,1)} custom-call(s32[2]{0:T(128)S(1)} %get-tuple-element.39.own_ref, s32[16]{0:T(128)S(1)} %select_reduce_fusion.loc_ref, s32[1]{0:T(128)} %bitcast.4.core_ref, bf16[16,64,512]{2,1,0:T(8,128)(2,1)S(1)} %bitcast.8, bf16[8,1040,128]{2,1,0:T(8,128)(2,1)S(1)} %copy-done.1, ...), custom_call_target="tpu_custom_call" | custom-call | flops 17179869184 | bytes 4194304 | tf_op jit(solution)/shard_map/pallas_call | solution.py:125
  101.8 25.0 %shard_map.96.refs_0_ = bf16[16,32,512]{2,1,0:T(8,128)(2,1)} custom-call(s32[2]{0:T(128)S(1)} %get-tuple-element.39.own_ref, s32[16]{0:T(128)S(1)} %select_reduce_fusion.loc_ref, s32[1]{0:T(128)} %bitcast.4.core_ref, bf16[16,64,512]{2,1,0:T(8,128)(2,1)S(1)} %bitcast.9, bf16[8,1040,128]{2,1,0:T(8,128)(2,1)S(1)} %copy-done.1, ...), custom_call_target="tpu_custom_call" | custom-call | flops 17179869184 | bytes 4194304 | tf_op jit(solution)/shard_map/pallas_call | solution.py:125
  132.2 7.2 %collective-permute-done.9.refs_2_ = bf16[16,32,512]{2,1,0:T(8,128)(2,1)S(1)} collective-permute-done((bf16[16,32,512]{2,1,0:T(8,128)(2,1)}, bf16[16,32,512]{2,1,0:T(8,128)(2,1)S(1)}, u32[]{:S(2)}, u32[]{:S(2)}) %collective-permute-start.9) | collective-permute-done | bytes 524320 | tf_op jit(solution)/shard_map/ppermute | solution.py:280
  139.4 3.0 %collective-permute-start.10 = (bf16[16,32,512]{2,1,0:T(8,128)(2,1)S(1)}, bf16[16,32,512]{2,1,0:T(8,128)(2,1)S(1)}, u32[]{:S(2)}, u32[]{:S(2)}) collective-permute-start(bf16[16,32,512]{2,1,0:T(8,128)(2,1)S(1)} %collective-permute-done.9.refs_2_), channel_id=1, source_target_pairs={{0,1},{1,0},{2,3},{3,2},{4,5},{5,4},{6,7},{7,6},{8,9},{9,8},{10,11... | collective-permute-start | bytes 1572872 | tf_op jit(solution)/shard_map/ppermute | solution.py:280
  148.4 8.9 %project.3 = (bf16[128,2048]{1,0:T(8,128)(2,1)S(1)}, bf16[128,2048]{1,0:T(8,128)(2,1)S(1)}, bf16[128,2048]{1,0:T(8,128)(2,1)S(1)}, bf16[128,2048]{1,0:T(8,128)(2,1)S(1)}) custom-call(s32[3]{0:T(128)S(1)} %pad_add_fusion.place_ref, bf16[16,32,512]{2,1,0:T(8,128)(2,1)} %shard_map.98.refs_0_, bf16[16,32,512]{2,1,0:T(8,128)(2,1)S(1)} %copy-done.12, ...), custom_call_target="tpu_custom_call" | custom-call | flops 4294967296 | bytes 8388608 | tf_op jit(solution)/shard_map/project/pallas_call | solution.py:196
  157.3 2.5 %collective-permute-start.26 = (bf16[128,2048]{1,0:T(8,128)(2,1)S(1)}, bf16[128,2048]{1,0:T(8,128)(2,1)S(1)}, u32[]{:S(2)}, u32[]{:S(2)}) collective-permute-start(bf16[128,2048]{1,0:T(8,128)(2,1)S(1)} %get-tuple-element.29), channel_id=1, source_target_pairs={{0,4},{1,5},{2,6},{3,7},{4,0},{5,1},{6,2},{7,3},{8,12},{9,13},{10,... | collective-permute-start | bytes 1572872 | tf_op jit(solution)/shard_map/ppermute | solution.py:280
  159.8 3.6 %collective-permute-start.27 = (bf16[128,2048]{1,0:T(8,128)(2,1)S(1)}, bf16[128,2048]{1,0:T(8,128)(2,1)S(1)}, u32[]{:S(2)}, u32[]{:S(2)}) collective-permute-start(bf16[128,2048]{1,0:T(8,128)(2,1)S(1)} %get-tuple-element.30), channel_id=1, source_target_pairs={{0,8},{1,9},{2,10},{3,11},{4,12},{5,13},{6,14},{7,15},{8,0},{9,1},... | collective-permute-start | bytes 1572872 | tf_op jit(solution)/shard_map/ppermute | solution.py:280
  163.7 8.6 %project.2 = (bf16[128,2048]{1,0:T(8,128)(2,1)S(1)}, bf16[128,2048]{1,0:T(8,128)(2,1)S(1)}, bf16[128,2048]{1,0:T(8,128)(2,1)S(1)}, bf16[128,2048]{1,0:T(8,128)(2,1)S(1)}) custom-call(s32[3]{0:T(128)S(1)} %pad_add_fusion.place_ref, bf16[16,32,512]{2,1,0:T(8,128)(2,1)} %shard_map.96.refs_0_, bf16[16,32,512]{2,1,0:T(8,128)(2,1)S(1)} %collective-permute-done.8.refs_1_, ...), custom_call_target="tpu_custom_call" | custom-call | flops 4294967296 | bytes 8388608 | tf_op jit(solution)/shard_map/project/pallas_call | solution.py:196
  172.2 2.5 %collective-permute-start.17 = (bf16[128,2048]{1,0:T(8,128)(2,1)S(1)}, bf16[128,2048]{1,0:T(8,128)(2,1)S(1)}, u32[]{:S(2)}, u32[]{:S(2)}) collective-permute-start(bf16[128,2048]{1,0:T(8,128)(2,1)S(1)} %get-tuple-element.21), channel_id=1, source_target_pairs={{0,4},{1,5},{2,6},{3,7},{4,0},{5,1},{6,2},{7,3},{8,12},{9,13},{10,... | collective-permute-start | bytes 1572872 | tf_op jit(solution)/shard_map/ppermute | solution.py:280
  174.8 3.0 %collective-permute-start.18 = (bf16[128,2048]{1,0:T(8,128)(2,1)S(1)}, bf16[128,2048]{1,0:T(8,128)(2,1)S(1)}, u32[]{:S(2)}, u32[]{:S(2)}) collective-permute-start(bf16[128,2048]{1,0:T(8,128)(2,1)S(1)} %get-tuple-element.22), channel_id=1, source_target_pairs={{0,8},{1,9},{2,10},{3,11},{4,12},{5,13},{6,14},{7,15},{8,0},{9,1},... | collective-permute-start | bytes 1572872 | tf_op jit(solution)/shard_map/ppermute | solution.py:280
  178.1 7.5 %collective-permute-done.27.refs_2_ = bf16[128,2048]{1,0:T(8,128)(2,1)S(1)} collective-permute-done((bf16[128,2048]{1,0:T(8,128)(2,1)S(1)}, bf16[128,2048]{1,0:T(8,128)(2,1)S(1)}, u32[]{:S(2)}, u32[]{:S(2)}) %collective-permute-start.27) | collective-permute-done | bytes 524320 | tf_op jit(solution)/shard_map/ppermute | solution.py:280
  188.9 6.0 %collective-permute-done.17.refs_1_ = bf16[128,2048]{1,0:T(8,128)(2,1)S(1)} collective-permute-done((bf16[128,2048]{1,0:T(8,128)(2,1)S(1)}, bf16[128,2048]{1,0:T(8,128)(2,1)S(1)}, u32[]{:S(2)}, u32[]{:S(2)}) %collective-permute-start.17) | collective-permute-done | bytes 524320 | tf_op jit(solution)/shard_map/ppermute | solution.py:280
  196.3 11.8 %collective-permute-done.18.refs_2_ = bf16[128,2048]{1,0:T(8,128)(2,1)S(1)} collective-permute-done((bf16[128,2048]{1,0:T(8,128)(2,1)S(1)}, bf16[128,2048]{1,0:T(8,128)(2,1)S(1)}, u32[]{:S(2)}, u32[]{:S(2)}) %collective-permute-start.18) | collective-permute-done | bytes 524320 | tf_op jit(solution)/shard_map/ppermute | solution.py:280
  216.0 3.1 %collective-permute-done.22.d = bf16[32,2048]{1,0:T(8,128)(2,1)S(1)} collective-permute-done((bf16[32,2048]{1,0:T(8,128)(2,1)S(1)}, bf16[32,2048]{1,0:T(8,128)(2,1)S(1)}, u32[]{:S(2)}, u32[]{:S(2)}) %collective-permute-start.22) | collective-permute-done | bytes 131104 | tf_op jit(solution)/shard_map/ppermute | solution.py:280
  (103 shorter events, 45.4 us)
Async XLA Ops:
  4.4 20.1 %collective-permute-start.5 = (bf16[1040,128]{1,0:T(8,128)(2,1)S(1)}, bf16[1040,128]{1,0:T(8,128)(2,1)S(1)}, u32[]{:S(2)}, u32[]{:S(2)}) collective-permute-start(bf16[1040,128]{1,0:T(8,128)(2,1)S(1)} %pad_maximum_fusion.refs_0_), channel_id=1, source_target_pairs={{0,80},{16,96},{32,112},{48,64},{64,16},{80,32},{96,48},{112,0},{1... | collective-permute-start | bytes 798728 | tf_op jit(solution)/shard_map/ppermute | solution.py:319
  5.3 19.2 %collective-permute-start.4 = (bf16[1040,128]{1,0:T(8,128)(2,1)S(1)}, bf16[1040,128]{1,0:T(8,128)(2,1)S(1)}, u32[]{:S(2)}, u32[]{:S(2)}) collective-permute-start(bf16[1040,128]{1,0:T(8,128)(2,1)S(1)} %pad_maximum_fusion.refs_0_), channel_id=1, source_target_pairs={{0,96},{16,112},{32,64},{48,80},{64,32},{80,48},{96,0},{112,16},{1... | collective-permute-start | bytes 798728 | tf_op jit(solution)/shard_map/ppermute | solution.py:319
  6.6 22.6 %collective-permute-start.3 = (bf16[1040,128]{1,0:T(8,128)(2,1)S(1)}, bf16[1040,128]{1,0:T(8,128)(2,1)S(1)}, u32[]{:S(2)}, u32[]{:S(2)}) collective-permute-start(bf16[1040,128]{1,0:T(8,128)(2,1)S(1)} %pad_maximum_fusion.refs_0_), channel_id=1, source_target_pairs={{0,64},{16,80},{32,96},{48,112},{64,0},{80,16},{96,32},{112,48},{1... | collective-permute-start | bytes 798728 | tf_op jit(solution)/shard_map/ppermute | solution.py:319
  8.2 21.0 %collective-permute-start.2 = (bf16[1040,128]{1,0:T(8,128)(2,1)S(1)}, bf16[1040,128]{1,0:T(8,128)(2,1)S(1)}, u32[]{:S(2)}, u32[]{:S(2)}) collective-permute-start(bf16[1040,128]{1,0:T(8,128)(2,1)S(1)} %pad_maximum_fusion.refs_0_), channel_id=1, source_target_pairs={{0,48},{16,0},{32,16},{48,32},{64,112},{80,64},{96,80},{112,96},{1... | collective-permute-start | bytes 798728 | tf_op jit(solution)/shard_map/ppermute | solution.py:319
  13.9 15.3 %collective-permute-start.1 = (bf16[1040,128]{1,0:T(8,128)(2,1)S(1)}, bf16[1040,128]{1,0:T(8,128)(2,1)S(1)}, u32[]{:S(2)}, u32[]{:S(2)}) collective-permute-start(bf16[1040,128]{1,0:T(8,128)(2,1)S(1)} %pad_maximum_fusion.refs_0_), channel_id=1, source_target_pairs={{0,16},{16,32},{32,48},{48,0},{64,80},{80,96},{96,112},{112,64},{1... | collective-permute-start | bytes 798728 | tf_op jit(solution)/shard_map/ppermute | solution.py:319
  37.5 38.1 %collective-permute-start.7 = (bf16[8,1040,128]{2,1,0:T(8,128)(2,1)}, bf16[8,1040,128]{2,1,0:T(8,128)(2,1)}, u32[]{:S(2)}, u32[]{:S(2)}) collective-permute-start(bf16[8,1040,128]{2,1,0:T(8,128)(2,1)} %shard_map.95.first_ref), channel_id=1, source_target_pairs={{0,1},{1,0},{2,3},{3,2},{4,5},{5,4},{6,7},{7,6},{8,9},{9,8},{10,11... | collective-permute-start | bytes 6389768 | tf_op jit(solution)/shard_map/ppermute | solution.py:280
  42.8 14.5 %collective-permute-start.13 = (bf16[512,512]{1,0:T(8,128)(2,1)}, bf16[512,512]{1,0:T(8,128)(2,1)}, u32[]{:S(2)}, u32[]{:S(2)}) collective-permute-start(bf16[512,512]{1,0:T(8,128)(2,1)} %get-tuple-element.40), channel_id=1, source_target_pairs={{0,3},{1,2},{2,1},{3,0},{4,7},{5,6},{6,5},{7,4},{8,11},{9,10},{10,... | collective-permute-start | bytes 1572872 | tf_op jit(solution)/shard_map/ppermute | solution.py:280
  43.9 23.6 %collective-permute-start.12 = (bf16[512,512]{1,0:T(8,128)(2,1)}, bf16[512,512]{1,0:T(8,128)(2,1)}, u32[]{:S(2)}, u32[]{:S(2)}) collective-permute-start(bf16[512,512]{1,0:T(8,128)(2,1)} %get-tuple-element.41), channel_id=1, source_target_pairs={{0,2},{1,3},{2,0},{3,1},{4,6},{5,7},{6,4},{7,5},{8,10},{9,11},{10,... | collective-permute-start | bytes 1572872 | tf_op jit(solution)/shard_map/ppermute | solution.py:280
  49.1 93.3 %collective-permute-start.11 = (bf16[512,2048]{1,0:T(8,128)(2,1)}, bf16[512,2048]{1,0:T(8,128)(2,1)}, u32[]{:S(2)}, u32[]{:S(2)}) collective-permute-start(bf16[512,2048]{1,0:T(8,128)(2,1)} %get-tuple-element.42), channel_id=1, source_target_pairs={{0,1},{1,0},{2,3},{3,2},{4,5},{5,4},{6,7},{7,6},{8,9},{9,8},{10,11... | collective-permute-start | bytes 6291464 | tf_op jit(solution)/shard_map/ppermute | solution.py:280
  69.7 57.1 %collective-permute-start.16 = (bf16[2,512,512]{2,1,0:T(8,128)(2,1)}, bf16[2,512,512]{2,1,0:T(8,128)(2,1)S(1)}, u32[]{:S(2)}, u32[]{:S(2)}) collective-permute-start(bf16[2,512,512]{2,1,0:T(8,128)(2,1)} %shard_map.97.refs_6_), channel_id=1, source_target_pairs={{0,48},{16,0},{32,16},{48,32},{64,112},{80,64},{96,80},{112,96},{1... | collective-permute-start | bytes 3145736 | tf_op jit(solution)/shard_map/ppermute | solution.py:336
  69.8 58.3 %collective-permute-start.15 = (bf16[2,512,512]{2,1,0:T(8,128)(2,1)}, bf16[2,512,512]{2,1,0:T(8,128)(2,1)S(1)}, u32[]{:S(2)}, u32[]{:S(2)}) collective-permute-start(bf16[2,512,512]{2,1,0:T(8,128)(2,1)} %shard_map.97.refs_6_), channel_id=1, source_target_pairs={{0,32},{16,48},{32,0},{48,16},{64,96},{80,112},{96,64},{112,80},{1... | collective-permute-start | bytes 3145736 | tf_op jit(solution)/shard_map/ppermute | solution.py:336
  73.6 58.0 %collective-permute-start.14 = (bf16[2,512,512]{2,1,0:T(8,128)(2,1)}, bf16[2,512,512]{2,1,0:T(8,128)(2,1)}, u32[]{:S(2)}, u32[]{:S(2)}) collective-permute-start(bf16[2,512,512]{2,1,0:T(8,128)(2,1)} %shard_map.97.refs_6_), channel_id=1, source_target_pairs={{0,16},{16,32},{32,48},{48,0},{64,80},{80,96},{96,112},{112,64},{1... | collective-permute-start | bytes 3145736 | tf_op jit(solution)/shard_map/ppermute | solution.py:336
  100.6 30.9 %collective-permute-start.24 = (bf16[16,32,512]{2,1,0:T(8,128)(2,1)}, bf16[16,32,512]{2,1,0:T(8,128)(2,1)}, u32[]{:S(2)}, u32[]{:S(2)}) collective-permute-start(bf16[16,32,512]{2,1,0:T(8,128)(2,1)} %shard_map.98.refs_0_), channel_id=1, source_target_pairs={{0,2},{1,3},{2,0},{3,1},{4,6},{5,7},{6,4},{7,5},{8,10},{9,11},{10,... | collective-permute-start | bytes 1572872 | tf_op jit(solution)/shard_map/ppermute | solution.py:280
  131.6 32.0 %collective-permute-start.8 = (bf16[16,32,512]{2,1,0:T(8,128)(2,1)}, bf16[16,32,512]{2,1,0:T(8,128)(2,1)S(1)}, u32[]{:S(2)}, u32[]{:S(2)}) collective-permute-start(bf16[16,32,512]{2,1,0:T(8,128)(2,1)} %shard_map.96.refs_0_), channel_id=1, source_target_pairs={{0,1},{1,0},{2,3},{3,2},{4,5},{5,4},{6,7},{7,6},{8,9},{9,8},{10,11... | collective-permute-start | bytes 1572872 | tf_op jit(solution)/shard_map/ppermute | solution.py:280
  139.4 24.3 %collective-permute-start.10 = (bf16[16,32,512]{2,1,0:T(8,128)(2,1)S(1)}, bf16[16,32,512]{2,1,0:T(8,128)(2,1)S(1)}, u32[]{:S(2)}, u32[]{:S(2)}) collective-permute-start(bf16[16,32,512]{2,1,0:T(8,128)(2,1)S(1)} %collective-permute-done.9.refs_2_), channel_id=1, source_target_pairs={{0,1},{1,0},{2,3},{3,2},{4,5},{5,4},{6,7},{7,6},{8,9},{9,8},{10,11... | collective-permute-start | bytes 1572872 | tf_op jit(solution)/shard_map/ppermute | solution.py:280
  157.3 20.5 %collective-permute-start.26 = (bf16[128,2048]{1,0:T(8,128)(2,1)S(1)}, bf16[128,2048]{1,0:T(8,128)(2,1)S(1)}, u32[]{:S(2)}, u32[]{:S(2)}) collective-permute-start(bf16[128,2048]{1,0:T(8,128)(2,1)S(1)} %get-tuple-element.29), channel_id=1, source_target_pairs={{0,4},{1,5},{2,6},{3,7},{4,0},{5,1},{6,2},{7,3},{8,12},{9,13},{10,... | collective-permute-start | bytes 1572872 | tf_op jit(solution)/shard_map/ppermute | solution.py:280
  159.8 25.8 %collective-permute-start.27 = (bf16[128,2048]{1,0:T(8,128)(2,1)S(1)}, bf16[128,2048]{1,0:T(8,128)(2,1)S(1)}, u32[]{:S(2)}, u32[]{:S(2)}) collective-permute-start(bf16[128,2048]{1,0:T(8,128)(2,1)S(1)} %get-tuple-element.30), channel_id=1, source_target_pairs={{0,8},{1,9},{2,10},{3,11},{4,12},{5,13},{6,14},{7,15},{8,0},{9,1},... | collective-permute-start | bytes 1572872 | tf_op jit(solution)/shard_map/ppermute | solution.py:280
  163.4 23.5 %collective-permute-start.28 = (bf16[128,2048]{1,0:T(8,128)(2,1)S(1)}, bf16[128,2048]{1,0:T(8,128)(2,1)S(1)}, u32[]{:S(2)}, u32[]{:S(2)}) collective-permute-start(bf16[128,2048]{1,0:T(8,128)(2,1)S(1)} %get-tuple-element.31), channel_id=1, source_target_pairs={{0,12},{1,13},{2,14},{3,15},{4,8},{5,9},{6,10},{7,11},{8,4},{9,5},... | collective-permute-start | bytes 1572872 | tf_op jit(solution)/shard_map/ppermute | solution.py:280
  172.2 22.6 %collective-permute-start.17 = (bf16[128,2048]{1,0:T(8,128)(2,1)S(1)}, bf16[128,2048]{1,0:T(8,128)(2,1)S(1)}, u32[]{:S(2)}, u32[]{:S(2)}) collective-permute-start(bf16[128,2048]{1,0:T(8,128)(2,1)S(1)} %get-tuple-element.21), channel_id=1, source_target_pairs={{0,4},{1,5},{2,6},{3,7},{4,0},{5,1},{6,2},{7,3},{8,12},{9,13},{10,... | collective-permute-start | bytes 1572872 | tf_op jit(solution)/shard_map/ppermute | solution.py:280
  174.8 33.3 %collective-permute-start.18 = (bf16[128,2048]{1,0:T(8,128)(2,1)S(1)}, bf16[128,2048]{1,0:T(8,128)(2,1)S(1)}, u32[]{:S(2)}, u32[]{:S(2)}) collective-permute-start(bf16[128,2048]{1,0:T(8,128)(2,1)S(1)} %get-tuple-element.22), channel_id=1, source_target_pairs={{0,8},{1,9},{2,10},{3,11},{4,12},{5,13},{6,14},{7,15},{8,0},{9,1},... | collective-permute-start | bytes 1572872 | tf_op jit(solution)/shard_map/ppermute | solution.py:280
  177.7 31.6 %collective-permute-start.19 = (bf16[128,2048]{1,0:T(8,128)(2,1)S(1)}, bf16[128,2048]{1,0:T(8,128)(2,1)S(1)}, u32[]{:S(2)}, u32[]{:S(2)}) collective-permute-start(bf16[128,2048]{1,0:T(8,128)(2,1)S(1)} %get-tuple-element.23), channel_id=1, source_target_pairs={{0,12},{1,13},{2,14},{3,15},{4,8},{5,9},{6,10},{7,11},{8,4},{9,5},... | collective-permute-start | bytes 1572872 | tf_op jit(solution)/shard_map/ppermute | solution.py:280
  187.2 24.1 %collective-permute-start.29 = (bf16[32,2048]{1,0:T(8,128)(2,1)S(1)}, bf16[32,2048]{1,0:T(8,128)(2,1)S(1)}, u32[]{:S(2)}, u32[]{:S(2)}) collective-permute-start(bf16[32,2048]{1,0:T(8,128)(2,1)S(1)} %get-tuple-element.33), channel_id=1, source_target_pairs={{0,1},{1,0},{2,3},{3,2},{4,5},{5,4},{6,7},{7,6},{8,9},{9,8},{10,11... | collective-permute-start | bytes 393224 | tf_op jit(solution)/shard_map/ppermute | solution.py:280
  188.6 24.8 %collective-permute-start.30 = (bf16[32,2048]{1,0:T(8,128)(2,1)S(1)}, bf16[32,2048]{1,0:T(8,128)(2,1)S(1)}, u32[]{:S(2)}, u32[]{:S(2)}) collective-permute-start(bf16[32,2048]{1,0:T(8,128)(2,1)S(1)} %get-tuple-element.34), channel_id=1, source_target_pairs={{0,2},{1,3},{2,0},{3,1},{4,6},{5,7},{6,4},{7,5},{8,10},{9,11},{10,... | collective-permute-start | bytes 393224 | tf_op jit(solution)/shard_map/ppermute | solution.py:280
  194.8 18.6 %collective-permute-start.31 = (bf16[32,2048]{1,0:T(8,128)(2,1)S(1)}, bf16[32,2048]{1,0:T(8,128)(2,1)S(1)}, u32[]{:S(2)}, u32[]{:S(2)}) collective-permute-start(bf16[32,2048]{1,0:T(8,128)(2,1)S(1)} %get-tuple-element.35), channel_id=1, source_target_pairs={{0,3},{1,2},{2,1},{3,0},{4,7},{5,6},{6,5},{7,4},{8,11},{9,10},{10,... | collective-permute-start | bytes 393224 | tf_op jit(solution)/shard_map/ppermute | solution.py:280
  (29 other events, 321.7 us)

commit v4 on v3

--- a/solution.py
+++ b/solution.py
@@ -173,40 +173,33 @@
 
 
 def project_kernel(place_ref, *refs):
-    atts, near, far, (acc_ref,), outs = refs[:4], refs[4:6], refs[6:10], refs[14:], refs[10:14]
-    step = pl.program_id(0)
-    rows, k = acc_ref.shape[0], atts[0].shape[-1]
-    near_term = jnp.dot(atts[0][...].reshape(rows, k), near[0][...], preferred_element_type=jnp.float32)
-    near_term += jnp.dot(atts[1][...].reshape(rows, k), near[1][...], preferred_element_type=jnp.float32)
+    atts, near, far, outs, acc_ref = refs[:4], refs[4:6], refs[6:10], refs[10:14], refs[14]
+    rows, cut = acc_ref.shape
+    n = outs[0].shape[0]
     for j, w in enumerate(far):
-        @pl.when(step == j)
-        def _(w=w):
-            total = near_term + jnp.dot(atts[2][...].reshape(rows, k), w[0], preferred_element_type=jnp.float32)
-            acc_ref[...] = total + jnp.dot(atts[3][...].reshape(rows, k), w[1], preferred_element_type=jnp.float32)
-    n = outs[0].shape[0]
-    for i, o in enumerate(outs):
-        o[...] = acc_ref[pl.ds(pl.multiple_of((place_ref[1] ^ i) * n, n), n), :].astype(jnp.bfloat16)
+        cols = pl.ds(pl.multiple_of(((place_ref[2] - j) & (len(far) - 1)) * cut, cut), cut)
+        total = None
+        for m, a in enumerate(atts):
+            weight = near[m][:, cols] if m < 2 else w[m - 2]
+            term = jnp.dot(a[...].reshape(rows, a.shape[-1]), weight, preferred_element_type=jnp.float32)
+            total = term if total is None else total + term
+        acc_ref[...] = total
+        for i, o in enumerate(outs):
+            o[:, cols] = acc_ref[pl.ds(pl.multiple_of((place_ref[1] ^ i) * n, n), n), :].astype(jnp.bfloat16)
 
 
 def project(place, atts, kept, paired, far):
     tps, r, k = atts[0].shape
     rows, cut = tps * r, far[0].shape[-1]
-    blocks = len(far)
-    col = lambda j, p: (p[2] - j) & (blocks - 1)
+    n = cut * len(far)
     return pl.pallas_call(
         project_kernel,
-        out_shape=[jax.ShapeDtypeStruct((rows // 4, cut * blocks), jnp.bfloat16)] * 4,
-        grid_spec=pltpu.PrefetchScalarGridSpec(
-            num_scalar_prefetch=1,
-            grid=(blocks,),
-            in_specs=[VMEM_SPEC] * 4
-            + [pl.BlockSpec((k, cut), lambda j, p: (0, col(j, p)))] * 2
-            + [VMEM_SPEC] * blocks,
-            out_specs=[pl.BlockSpec((rows // 4, cut), lambda j, p: (0, col(j, p)))] * 4,
-            scratch_shapes=[pltpu.VMEM((rows, cut), jnp.float32)],
-        ),
-        compiler_params=pltpu.CompilerParams(dimension_semantics=("arbitrary",), vmem_limit_bytes=20 * 2**20),
-        cost_estimate=pl.CostEstimate(flops=8 * rows * k * cut * blocks, bytes_accessed=8 * k * cut * blocks, transcendentals=0),
+        out_shape=[jax.ShapeDtypeStruct((rows // 4, n), jnp.bfloat16)] * 4,
+        in_specs=[pl.BlockSpec(memory_space=pltpu.SMEM)] + [VMEM_SPEC] * (6 + len(far)),
+        out_specs=[VMEM_SPEC] * 4,
+        scratch_shapes=[pltpu.VMEM((rows, cut), jnp.float32)],
+        compiler_params=pltpu.CompilerParams(vmem_limit_bytes=16 * 2**20),
+        cost_estimate=pl.CostEstimate(flops=8 * rows * k * n, bytes_accessed=8 * k * n, transcendentals=0),
         name="project",
     )(place, *atts, kept, paired, *far)
 

time: 221 us -> 219 us (level)
  Pallas kernels: 76 us -> 72.2 us
    pallas_call x2, Pallas kernels: 17.5 us -> 13.7 us  [project(): pl.pallas_call(project_kernel, out_shape=[jax.ShapeDtypeStruct((rows // 4...]
  transfers between devices with their start and end apart: 32 -> 32, of which waited for: 13 -> 13; matrix products, arithmetic and copies ran while one was open for 3% -> 4% of each run, Pallas kernels for 33% -> 31%
where the time goes in v4:
time: 219 us
  Pallas kernels  72.2 us (33%)
  waiting for transfers between devices  69.8 us (32%)
  starting transfers between devices  56.7 us (26%)
  local copies, waits for them, and re-layouts  16.7 us (8%)
    ppermute x22, waiting for transfers between devices, swapped(): return lax.ppermute(value, 'tp', [(i, i ^ mask) for i in range(count)])  56.5 us
    pallas_call x2, Pallas kernels, attend(): pl.pallas_call(functools.partial(attend_kernel, rows=rows, part=part, hea...  50.1 us
    ppermute x22, starting transfers between devices, swapped(): return lax.ppermute(value, 'tp', [(i, i ^ mask) for i in range(count)])  33 us
    ppermute x7, starting transfers between devices, shards(): pieces.append(lax.ppermute(mine, 'ctx', pairs))  17.8 us
    pallas_call x2, Pallas kernels, project(): pl.pallas_call(project_kernel, out_shape=[jax.ShapeDtypeStruct((rows // 4...  13.7 us
    ppermute x7, waiting for transfers between devices, shards(): pieces.append(lax.ppermute(mine, 'ctx', pairs))  13.3 us
    unnamed x42, local copies, waits for them, and re-layouts  8.62 us
    ppermute x3, starting transfers between devices, shards(): far.append(lax.ppermute(side, 'ctx', pairs))  5.85 us
  transfers between devices with their start and end apart: 32, of which 13 were waited for; matrix products, arithmetic and copies ran while one was open for 4% of the time, Pallas kernels for 31%

profile of v4, /device:TPU:17, one launch (start us, length us, event | category | flops | bytes accessed | tf_op | source)
XLA Modules:
  0.0 218.5 jit_solution(6195397792725889679)
XLA Ops:
  10.0 3.9 %collective-permute-done.6.refs_7_ = bf16[1040,128]{1,0:T(8,128)(2,1)S(1)} collective-permute-done((bf16[1040,128]{1,0:T(8,128)(2,1)S(1)}, bf16[1040,128]{1,0:T(8,128)(2,1)S(1)}, u32[]{:S(2)}, u32[]{:S(2)}) %collective-permute-start.6) | collective-permute-done | bytes 266272 | tf_op jit(solution)/shard_map/ppermute | solution.py:312
  13.9 10.6 %collective-permute-start.1 = (bf16[1040,128]{1,0:T(8,128)(2,1)S(1)}, bf16[1040,128]{1,0:T(8,128)(2,1)S(1)}, u32[]{:S(2)}, u32[]{:S(2)}) collective-permute-start(bf16[1040,128]{1,0:T(8,128)(2,1)S(1)} %pad_maximum_fusion.refs_0_), channel_id=1, source_target_pairs={{0,16},{16,32},{32,48},{48,0},{64,80},{80,96},{96,112},{112,64},{1... | collective-permute-start | bytes 798728 | tf_op jit(solution)/shard_map/ppermute | solution.py:312
  24.5 4.7 %collective-permute-done.3.refs_4_ = bf16[1040,128]{1,0:T(8,128)(2,1)S(1)} collective-permute-done((bf16[1040,128]{1,0:T(8,128)(2,1)S(1)}, bf16[1040,128]{1,0:T(8,128)(2,1)S(1)}, u32[]{:S(2)}, u32[]{:S(2)}) %collective-permute-start.3) | collective-permute-done | bytes 266272 | tf_op jit(solution)/shard_map/ppermute | solution.py:312
  29.2 4.7 %collective-permute-done.refs_1_ = bf16[1040,128]{1,0:T(8,128)(2,1)S(1)} collective-permute-done((bf16[1040,128]{1,0:T(8,128)(2,1)S(1)}, bf16[1040,128]{1,0:T(8,128)(2,1)S(1)}, u32[]{:S(2)}, u32[]{:S(2)}) %collective-permute-start) | collective-permute-done | bytes 266272 | tf_op jit(solution)/shard_map/ppermute | solution.py:312
  34.6 2.9 %shard_map.95.first_ref = bf16[8,1040,128]{2,1,0:T(8,128)(2,1)} custom-call(bf16[1040,128]{1,0:T(8,128)(2,1)} %copy-done.13, bf16[1040,128]{1,0:T(8,128)(2,1)} %copy-done.20, bf16[1040,128]{1,0:T(8,128)(2,1)} %copy-done.19, bf16[1040,128]{1,0:T(8,128)(2,1)} %copy-done.18, bf16[1040,128]{1,0:T(8,128)(2,1)} %copy-done.17, bf16[1040,128]{1,0:T(8,128)(2,1)} %copy-done.16, ...), custom_call_target="tpu_custom_call" | custom-call | tf_op jit(solution)/shard_map/pallas_call | solution.py:165
  37.5 3.0 %collective-permute-start.7 = (bf16[8,1040,128]{2,1,0:T(8,128)(2,1)}, bf16[8,1040,128]{2,1,0:T(8,128)(2,1)}, u32[]{:S(2)}, u32[]{:S(2)}) collective-permute-start(bf16[8,1040,128]{2,1,0:T(8,128)(2,1)} %shard_map.95.first_ref), channel_id=1, source_target_pairs={{0,1},{1,0},{2,3},{3,2},{4,5},{5,4},{6,7},{7,6},{8,9},{9,8},{10,11... | collective-permute-start | bytes 6389768 | tf_op jit(solution)/shard_map/ppermute | solution.py:273
  44.2 5.0 %constant_dynamic-slice_fusion.2 = (bf16[512,2048]{1,0:T(8,128)(2,1)}, bf16[512,2048]{1,0:T(8,128)(2,1)}) fusion(bf16[512,8192]{1,0:T(8,128)(2,1)} %param.12, s32[]{:T(128)S(6)} %select_n.39, s32[]{:T(128)S(6)} %select_n.38), kind=kLoop, calls=%fused_computation.10 | loop fusion | bytes 8388616 | tf_op jit(solution)/shard_map/dynamic_slice | solution.py:330
  50.3 7.0 %collective-permute-done.13.refs_1_ = bf16[512,512]{1,0:T(8,128)(2,1)} collective-permute-done((bf16[512,512]{1,0:T(8,128)(2,1)}, bf16[512,512]{1,0:T(8,128)(2,1)}, u32[]{:S(2)}, u32[]{:S(2)}) %collective-permute-start.13) | collective-permute-done | bytes 524320 | tf_op jit(solution)/shard_map/ppermute | solution.py:273
  57.3 10.2 %collective-permute-done.12.refs_0_ = bf16[512,512]{1,0:T(8,128)(2,1)} collective-permute-done((bf16[512,512]{1,0:T(8,128)(2,1)}, bf16[512,512]{1,0:T(8,128)(2,1)}, u32[]{:S(2)}, u32[]{:S(2)}) %collective-permute-start.12) | collective-permute-done | bytes 524320 | tf_op jit(solution)/shard_map/ppermute | solution.py:273
  69.8 3.8 %collective-permute-start.15 = (bf16[2,512,512]{2,1,0:T(8,128)(2,1)}, bf16[2,512,512]{2,1,0:T(8,128)(2,1)S(1)}, u32[]{:S(2)}, u32[]{:S(2)}) collective-permute-start(bf16[2,512,512]{2,1,0:T(8,128)(2,1)} %shard_map.97.refs_6_), channel_id=1, source_target_pairs={{0,32},{16,48},{32,0},{48,16},{64,96},{80,112},{96,64},{112,80},{1... | collective-permute-start | bytes 3145736 | tf_op jit(solution)/shard_map/ppermute | solution.py:329
  75.6 25.0 %shard_map.98.refs_0_ = bf16[16,32,512]{2,1,0:T(8,128)(2,1)} custom-call(s32[2]{0:T(128)S(1)} %get-tuple-element.39.own_ref, s32[16]{0:T(128)S(1)} %select_reduce_fusion.loc_ref, s32[1]{0:T(128)} %bitcast.4.core_ref, bf16[16,64,512]{2,1,0:T(8,128)(2,1)S(1)} %bitcast.8, bf16[8,1040,128]{2,1,0:T(8,128)(2,1)S(1)} %copy-done.1, ...), custom_call_target="tpu_custom_call" | custom-call | flops 17179869184 | bytes 4194304 | tf_op jit(solution)/shard_map/pallas_call | solution.py:125
  101.8 25.0 %shard_map.96.refs_0_ = bf16[16,32,512]{2,1,0:T(8,128)(2,1)} custom-call(s32[2]{0:T(128)S(1)} %get-tuple-element.39.own_ref, s32[16]{0:T(128)S(1)} %select_reduce_fusion.loc_ref, s32[1]{0:T(128)} %bitcast.4.core_ref, bf16[16,64,512]{2,1,0:T(8,128)(2,1)S(1)} %bitcast.9, bf16[8,1040,128]{2,1,0:T(8,128)(2,1)S(1)} %copy-done.1, ...), custom_call_target="tpu_custom_call" | custom-call | flops 17179869184 | bytes 4194304 | tf_op jit(solution)/shard_map/pallas_call | solution.py:125
  132.2 7.2 %collective-permute-done.9.refs_2_ = bf16[16,32,512]{2,1,0:T(8,128)(2,1)S(1)} collective-permute-done((bf16[16,32,512]{2,1,0:T(8,128)(2,1)}, bf16[16,32,512]{2,1,0:T(8,128)(2,1)S(1)}, u32[]{:S(2)}, u32[]{:S(2)}) %collective-permute-start.9) | collective-permute-done | bytes 524320 | tf_op jit(solution)/shard_map/ppermute | solution.py:273
  139.4 3.0 %collective-permute-start.10 = (bf16[16,32,512]{2,1,0:T(8,128)(2,1)S(1)}, bf16[16,32,512]{2,1,0:T(8,128)(2,1)S(1)}, u32[]{:S(2)}, u32[]{:S(2)}) collective-permute-start(bf16[16,32,512]{2,1,0:T(8,128)(2,1)S(1)} %collective-permute-done.9.refs_2_), channel_id=1, source_target_pairs={{0,1},{1,0},{2,3},{3,2},{4,5},{5,4},{6,7},{7,6},{8,9},{9,8},{10,11... | collective-permute-start | bytes 1572872 | tf_op jit(solution)/shard_map/ppermute | solution.py:273
  148.4 7.0 %project.3 = (bf16[128,2048]{1,0:T(8,128)(2,1)S(1)}, bf16[128,2048]{1,0:T(8,128)(2,1)S(1)}, bf16[128,2048]{1,0:T(8,128)(2,1)S(1)}, bf16[128,2048]{1,0:T(8,128)(2,1)S(1)}) custom-call(s32[3]{0:T(128)S(1)} %pad_add_fusion.place_ref, bf16[16,32,512]{2,1,0:T(8,128)(2,1)} %shard_map.98.refs_0_, bf16[16,32,512]{2,1,0:T(8,128)(2,1)S(1)} %copy-done.12, ...), custom_call_target="tpu_custom_call" | custom-call | flops 4294967296 | bytes 8388608 | tf_op jit(solution)/shard_map/project/pallas_call | solution.py:195
  155.4 2.5 %collective-permute-start.26 = (bf16[128,2048]{1,0:T(8,128)(2,1)S(1)}, bf16[128,2048]{1,0:T(8,128)(2,1)S(1)}, u32[]{:S(2)}, u32[]{:S(2)}) collective-permute-start(bf16[128,2048]{1,0:T(8,128)(2,1)S(1)} %get-tuple-element.29), channel_id=1, source_target_pairs={{0,4},{1,5},{2,6},{3,7},{4,0},{5,1},{6,2},{7,3},{8,12},{9,13},{10,... | collective-permute-start | bytes 1572872 | tf_op jit(solution)/shard_map/ppermute | solution.py:273
  157.9 3.6 %collective-permute-start.27 = (bf16[128,2048]{1,0:T(8,128)(2,1)S(1)}, bf16[128,2048]{1,0:T(8,128)(2,1)S(1)}, u32[]{:S(2)}, u32[]{:S(2)}) collective-permute-start(bf16[128,2048]{1,0:T(8,128)(2,1)S(1)} %get-tuple-element.30), channel_id=1, source_target_pairs={{0,8},{1,9},{2,10},{3,11},{4,12},{5,13},{6,14},{7,15},{8,0},{9,1},... | collective-permute-start | bytes 1572872 | tf_op jit(solution)/shard_map/ppermute | solution.py:273
  161.7 6.7 %project.2 = (bf16[128,2048]{1,0:T(8,128)(2,1)S(1)}, bf16[128,2048]{1,0:T(8,128)(2,1)S(1)}, bf16[128,2048]{1,0:T(8,128)(2,1)S(1)}, bf16[128,2048]{1,0:T(8,128)(2,1)S(1)}) custom-call(s32[3]{0:T(128)S(1)} %pad_add_fusion.place_ref, bf16[16,32,512]{2,1,0:T(8,128)(2,1)} %shard_map.96.refs_0_, bf16[16,32,512]{2,1,0:T(8,128)(2,1)S(1)} %collective-permute-done.8.refs_1_, ...), custom_call_target="tpu_custom_call" | custom-call | flops 4294967296 | bytes 8388608 | tf_op jit(solution)/shard_map/project/pallas_call | solution.py:195
  168.4 2.5 %collective-permute-start.17 = (bf16[128,2048]{1,0:T(8,128)(2,1)S(1)}, bf16[128,2048]{1,0:T(8,128)(2,1)S(1)}, u32[]{:S(2)}, u32[]{:S(2)}) collective-permute-start(bf16[128,2048]{1,0:T(8,128)(2,1)S(1)} %get-tuple-element.21), channel_id=1, source_target_pairs={{0,4},{1,5},{2,6},{3,7},{4,0},{5,1},{6,2},{7,3},{8,12},{9,13},{10,... | collective-permute-start | bytes 1572872 | tf_op jit(solution)/shard_map/ppermute | solution.py:273
  171.0 3.0 %collective-permute-start.18 = (bf16[128,2048]{1,0:T(8,128)(2,1)S(1)}, bf16[128,2048]{1,0:T(8,128)(2,1)S(1)}, u32[]{:S(2)}, u32[]{:S(2)}) collective-permute-start(bf16[128,2048]{1,0:T(8,128)(2,1)S(1)} %get-tuple-element.22), channel_id=1, source_target_pairs={{0,8},{1,9},{2,10},{3,11},{4,12},{5,13},{6,14},{7,15},{8,0},{9,1},... | collective-permute-start | bytes 1572872 | tf_op jit(solution)/shard_map/ppermute | solution.py:273
  176.2 7.5 %collective-permute-done.27.refs_2_ = bf16[128,2048]{1,0:T(8,128)(2,1)S(1)} collective-permute-done((bf16[128,2048]{1,0:T(8,128)(2,1)S(1)}, bf16[128,2048]{1,0:T(8,128)(2,1)S(1)}, u32[]{:S(2)}, u32[]{:S(2)}) %collective-permute-start.27) | collective-permute-done | bytes 524320 | tf_op jit(solution)/shard_map/ppermute | solution.py:273
  186.9 5.9 %collective-permute-done.17.refs_1_ = bf16[128,2048]{1,0:T(8,128)(2,1)S(1)} collective-permute-done((bf16[128,2048]{1,0:T(8,128)(2,1)S(1)}, bf16[128,2048]{1,0:T(8,128)(2,1)S(1)}, u32[]{:S(2)}, u32[]{:S(2)}) %collective-permute-start.17) | collective-permute-done | bytes 524320 | tf_op jit(solution)/shard_map/ppermute | solution.py:273
  194.4 11.8 %collective-permute-done.18.refs_2_ = bf16[128,2048]{1,0:T(8,128)(2,1)S(1)} collective-permute-done((bf16[128,2048]{1,0:T(8,128)(2,1)S(1)}, bf16[128,2048]{1,0:T(8,128)(2,1)S(1)}, u32[]{:S(2)}, u32[]{:S(2)}) %collective-permute-start.18) | collective-permute-done | bytes 524320 | tf_op jit(solution)/shard_map/ppermute | solution.py:273
  214.1 3.1 %collective-permute-done.22.d = bf16[32,2048]{1,0:T(8,128)(2,1)S(1)} collective-permute-done((bf16[32,2048]{1,0:T(8,128)(2,1)S(1)}, bf16[32,2048]{1,0:T(8,128)(2,1)S(1)}, u32[]{:S(2)}, u32[]{:S(2)}) %collective-permute-start.22) | collective-permute-done | bytes 131104 | tf_op jit(solution)/shard_map/ppermute | solution.py:273
  (103 shorter events, 47.3 us)
Async XLA Ops:
  4.4 20.1 %collective-permute-start.5 = (bf16[1040,128]{1,0:T(8,128)(2,1)S(1)}, bf16[1040,128]{1,0:T(8,128)(2,1)S(1)}, u32[]{:S(2)}, u32[]{:S(2)}) collective-permute-start(bf16[1040,128]{1,0:T(8,128)(2,1)S(1)} %pad_maximum_fusion.refs_0_), channel_id=1, source_target_pairs={{0,80},{16,96},{32,112},{48,64},{64,16},{80,32},{96,48},{112,0},{1... | collective-permute-start | bytes 798728 | tf_op jit(solution)/shard_map/ppermute | solution.py:312
  5.3 19.2 %collective-permute-start.4 = (bf16[1040,128]{1,0:T(8,128)(2,1)S(1)}, bf16[1040,128]{1,0:T(8,128)(2,1)S(1)}, u32[]{:S(2)}, u32[]{:S(2)}) collective-permute-start(bf16[1040,128]{1,0:T(8,128)(2,1)S(1)} %pad_maximum_fusion.refs_0_), channel_id=1, source_target_pairs={{0,96},{16,112},{32,64},{48,80},{64,32},{80,48},{96,0},{112,16},{1... | collective-permute-start | bytes 798728 | tf_op jit(solution)/shard_map/ppermute | solution.py:312
  6.6 22.6 %collective-permute-start.3 = (bf16[1040,128]{1,0:T(8,128)(2,1)S(1)}, bf16[1040,128]{1,0:T(8,128)(2,1)S(1)}, u32[]{:S(2)}, u32[]{:S(2)}) collective-permute-start(bf16[1040,128]{1,0:T(8,128)(2,1)S(1)} %pad_maximum_fusion.refs_0_), channel_id=1, source_target_pairs={{0,64},{16,80},{32,96},{48,112},{64,0},{80,16},{96,32},{112,48},{1... | collective-permute-start | bytes 798728 | tf_op jit(solution)/shard_map/ppermute | solution.py:312
  8.2 21.0 %collective-permute-start.2 = (bf16[1040,128]{1,0:T(8,128)(2,1)S(1)}, bf16[1040,128]{1,0:T(8,128)(2,1)S(1)}, u32[]{:S(2)}, u32[]{:S(2)}) collective-permute-start(bf16[1040,128]{1,0:T(8,128)(2,1)S(1)} %pad_maximum_fusion.refs_0_), channel_id=1, source_target_pairs={{0,48},{16,0},{32,16},{48,32},{64,112},{80,64},{96,80},{112,96},{1... | collective-permute-start | bytes 798728 | tf_op jit(solution)/shard_map/ppermute | solution.py:312
  13.9 15.3 %collective-permute-start.1 = (bf16[1040,128]{1,0:T(8,128)(2,1)S(1)}, bf16[1040,128]{1,0:T(8,128)(2,1)S(1)}, u32[]{:S(2)}, u32[]{:S(2)}) collective-permute-start(bf16[1040,128]{1,0:T(8,128)(2,1)S(1)} %pad_maximum_fusion.refs_0_), channel_id=1, source_target_pairs={{0,16},{16,32},{32,48},{48,0},{64,80},{80,96},{96,112},{112,64},{1... | collective-permute-start | bytes 798728 | tf_op jit(solution)/shard_map/ppermute | solution.py:312
  37.5 38.1 %collective-permute-start.7 = (bf16[8,1040,128]{2,1,0:T(8,128)(2,1)}, bf16[8,1040,128]{2,1,0:T(8,128)(2,1)}, u32[]{:S(2)}, u32[]{:S(2)}) collective-permute-start(bf16[8,1040,128]{2,1,0:T(8,128)(2,1)} %shard_map.95.first_ref), channel_id=1, source_target_pairs={{0,1},{1,0},{2,3},{3,2},{4,5},{5,4},{6,7},{7,6},{8,9},{9,8},{10,11... | collective-permute-start | bytes 6389768 | tf_op jit(solution)/shard_map/ppermute | solution.py:273
  42.8 14.5 %collective-permute-start.13 = (bf16[512,512]{1,0:T(8,128)(2,1)}, bf16[512,512]{1,0:T(8,128)(2,1)}, u32[]{:S(2)}, u32[]{:S(2)}) collective-permute-start(bf16[512,512]{1,0:T(8,128)(2,1)} %get-tuple-element.40), channel_id=1, source_target_pairs={{0,3},{1,2},{2,1},{3,0},{4,7},{5,6},{6,5},{7,4},{8,11},{9,10},{10,... | collective-permute-start | bytes 1572872 | tf_op jit(solution)/shard_map/ppermute | solution.py:273
  43.9 23.6 %collective-permute-start.12 = (bf16[512,512]{1,0:T(8,128)(2,1)}, bf16[512,512]{1,0:T(8,128)(2,1)}, u32[]{:S(2)}, u32[]{:S(2)}) collective-permute-start(bf16[512,512]{1,0:T(8,128)(2,1)} %get-tuple-element.41), channel_id=1, source_target_pairs={{0,2},{1,3},{2,0},{3,1},{4,6},{5,7},{6,4},{7,5},{8,10},{9,11},{10,... | collective-permute-start | bytes 1572872 | tf_op jit(solution)/shard_map/ppermute | solution.py:273
  49.1 93.3 %collective-permute-start.11 = (bf16[512,2048]{1,0:T(8,128)(2,1)}, bf16[512,2048]{1,0:T(8,128)(2,1)}, u32[]{:S(2)}, u32[]{:S(2)}) collective-permute-start(bf16[512,2048]{1,0:T(8,128)(2,1)} %get-tuple-element.42), channel_id=1, source_target_pairs={{0,1},{1,0},{2,3},{3,2},{4,5},{5,4},{6,7},{7,6},{8,9},{9,8},{10,11... | collective-permute-start | bytes 6291464 | tf_op jit(solution)/shard_map/ppermute | solution.py:273
  69.7 57.1 %collective-permute-start.16 = (bf16[2,512,512]{2,1,0:T(8,128)(2,1)}, bf16[2,512,512]{2,1,0:T(8,128)(2,1)S(1)}, u32[]{:S(2)}, u32[]{:S(2)}) collective-permute-start(bf16[2,512,512]{2,1,0:T(8,128)(2,1)} %shard_map.97.refs_6_), channel_id=1, source_target_pairs={{0,48},{16,0},{32,16},{48,32},{64,112},{80,64},{96,80},{112,96},{1... | collective-permute-start | bytes 3145736 | tf_op jit(solution)/shard_map/ppermute | solution.py:329
  69.8 58.3 %collective-permute-start.15 = (bf16[2,512,512]{2,1,0:T(8,128)(2,1)}, bf16[2,512,512]{2,1,0:T(8,128)(2,1)S(1)}, u32[]{:S(2)}, u32[]{:S(2)}) collective-permute-start(bf16[2,512,512]{2,1,0:T(8,128)(2,1)} %shard_map.97.refs_6_), channel_id=1, source_target_pairs={{0,32},{16,48},{32,0},{48,16},{64,96},{80,112},{96,64},{112,80},{1... | collective-permute-start | bytes 3145736 | tf_op jit(solution)/shard_map/ppermute | solution.py:329
  73.6 58.0 %collective-permute-start.14 = (bf16[2,512,512]{2,1,0:T(8,128)(2,1)}, bf16[2,512,512]{2,1,0:T(8,128)(2,1)}, u32[]{:S(2)}, u32[]{:S(2)}) collective-permute-start(bf16[2,512,512]{2,1,0:T(8,128)(2,1)} %shard_map.97.refs_6_), channel_id=1, source_target_pairs={{0,16},{16,32},{32,48},{48,0},{64,80},{80,96},{96,112},{112,64},{1... | collective-permute-start | bytes 3145736 | tf_op jit(solution)/shard_map/ppermute | solution.py:329
  100.6 30.9 %collective-permute-start.24 = (bf16[16,32,512]{2,1,0:T(8,128)(2,1)}, bf16[16,32,512]{2,1,0:T(8,128)(2,1)}, u32[]{:S(2)}, u32[]{:S(2)}) collective-permute-start(bf16[16,32,512]{2,1,0:T(8,128)(2,1)} %shard_map.98.refs_0_), channel_id=1, source_target_pairs={{0,2},{1,3},{2,0},{3,1},{4,6},{5,7},{6,4},{7,5},{8,10},{9,11},{10,... | collective-permute-start | bytes 1572872 | tf_op jit(solution)/shard_map/ppermute | solution.py:273
  131.6 30.1 %collective-permute-start.8 = (bf16[16,32,512]{2,1,0:T(8,128)(2,1)}, bf16[16,32,512]{2,1,0:T(8,128)(2,1)S(1)}, u32[]{:S(2)}, u32[]{:S(2)}) collective-permute-start(bf16[16,32,512]{2,1,0:T(8,128)(2,1)} %shard_map.96.refs_0_), channel_id=1, source_target_pairs={{0,1},{1,0},{2,3},{3,2},{4,5},{5,4},{6,7},{7,6},{8,9},{9,8},{10,11... | collective-permute-start | bytes 1572872 | tf_op jit(solution)/shard_map/ppermute | solution.py:273
  139.4 22.4 %collective-permute-start.10 = (bf16[16,32,512]{2,1,0:T(8,128)(2,1)S(1)}, bf16[16,32,512]{2,1,0:T(8,128)(2,1)S(1)}, u32[]{:S(2)}, u32[]{:S(2)}) collective-permute-start(bf16[16,32,512]{2,1,0:T(8,128)(2,1)S(1)} %collective-permute-done.9.refs_2_), channel_id=1, source_target_pairs={{0,1},{1,0},{2,3},{3,2},{4,5},{5,4},{6,7},{7,6},{8,9},{9,8},{10,11... | collective-permute-start | bytes 1572872 | tf_op jit(solution)/shard_map/ppermute | solution.py:273
  155.4 18.6 %collective-permute-start.26 = (bf16[128,2048]{1,0:T(8,128)(2,1)S(1)}, bf16[128,2048]{1,0:T(8,128)(2,1)S(1)}, u32[]{:S(2)}, u32[]{:S(2)}) collective-permute-start(bf16[128,2048]{1,0:T(8,128)(2,1)S(1)} %get-tuple-element.29), channel_id=1, source_target_pairs={{0,4},{1,5},{2,6},{3,7},{4,0},{5,1},{6,2},{7,3},{8,12},{9,13},{10,... | collective-permute-start | bytes 1572872 | tf_op jit(solution)/shard_map/ppermute | solution.py:273
  157.9 25.8 %collective-permute-start.27 = (bf16[128,2048]{1,0:T(8,128)(2,1)S(1)}, bf16[128,2048]{1,0:T(8,128)(2,1)S(1)}, u32[]{:S(2)}, u32[]{:S(2)}) collective-permute-start(bf16[128,2048]{1,0:T(8,128)(2,1)S(1)} %get-tuple-element.30), channel_id=1, source_target_pairs={{0,8},{1,9},{2,10},{3,11},{4,12},{5,13},{6,14},{7,15},{8,0},{9,1},... | collective-permute-start | bytes 1572872 | tf_op jit(solution)/shard_map/ppermute | solution.py:273
  161.5 23.5 %collective-permute-start.28 = (bf16[128,2048]{1,0:T(8,128)(2,1)S(1)}, bf16[128,2048]{1,0:T(8,128)(2,1)S(1)}, u32[]{:S(2)}, u32[]{:S(2)}) collective-permute-start(bf16[128,2048]{1,0:T(8,128)(2,1)S(1)} %get-tuple-element.31), channel_id=1, source_target_pairs={{0,12},{1,13},{2,14},{3,15},{4,8},{5,9},{6,10},{7,11},{8,4},{9,5},... | collective-permute-start | bytes 1572872 | tf_op jit(solution)/shard_map/ppermute | solution.py:273
  168.4 24.5 %collective-permute-start.17 = (bf16[128,2048]{1,0:T(8,128)(2,1)S(1)}, bf16[128,2048]{1,0:T(8,128)(2,1)S(1)}, u32[]{:S(2)}, u32[]{:S(2)}) collective-permute-start(bf16[128,2048]{1,0:T(8,128)(2,1)S(1)} %get-tuple-element.21), channel_id=1, source_target_pairs={{0,4},{1,5},{2,6},{3,7},{4,0},{5,1},{6,2},{7,3},{8,12},{9,13},{10,... | collective-permute-start | bytes 1572872 | tf_op jit(solution)/shard_map/ppermute | solution.py:273
  171.0 35.2 %collective-permute-start.18 = (bf16[128,2048]{1,0:T(8,128)(2,1)S(1)}, bf16[128,2048]{1,0:T(8,128)(2,1)S(1)}, u32[]{:S(2)}, u32[]{:S(2)}) collective-permute-start(bf16[128,2048]{1,0:T(8,128)(2,1)S(1)} %get-tuple-element.22), channel_id=1, source_target_pairs={{0,8},{1,9},{2,10},{3,11},{4,12},{5,13},{6,14},{7,15},{8,0},{9,1},... | collective-permute-start | bytes 1572872 | tf_op jit(solution)/shard_map/ppermute | solution.py:273
  173.9 33.5 %collective-permute-start.19 = (bf16[128,2048]{1,0:T(8,128)(2,1)S(1)}, bf16[128,2048]{1,0:T(8,128)(2,1)S(1)}, u32[]{:S(2)}, u32[]{:S(2)}) collective-permute-start(bf16[128,2048]{1,0:T(8,128)(2,1)S(1)} %get-tuple-element.23), channel_id=1, source_target_pairs={{0,12},{1,13},{2,14},{3,15},{4,8},{5,9},{6,10},{7,11},{8,4},{9,5},... | collective-permute-start | bytes 1572872 | tf_op jit(solution)/shard_map/ppermute | solution.py:273
  185.2 24.1 %collective-permute-start.29 = (bf16[32,2048]{1,0:T(8,128)(2,1)S(1)}, bf16[32,2048]{1,0:T(8,128)(2,1)S(1)}, u32[]{:S(2)}, u32[]{:S(2)}) collective-permute-start(bf16[32,2048]{1,0:T(8,128)(2,1)S(1)} %get-tuple-element.33), channel_id=1, source_target_pairs={{0,1},{1,0},{2,3},{3,2},{4,5},{5,4},{6,7},{7,6},{8,9},{9,8},{10,11... | collective-permute-start | bytes 393224 | tf_op jit(solution)/shard_map/ppermute | solution.py:273
  186.7 24.8 %collective-permute-start.30 = (bf16[32,2048]{1,0:T(8,128)(2,1)S(1)}, bf16[32,2048]{1,0:T(8,128)(2,1)S(1)}, u32[]{:S(2)}, u32[]{:S(2)}) collective-permute-start(bf16[32,2048]{1,0:T(8,128)(2,1)S(1)} %get-tuple-element.34), channel_id=1, source_target_pairs={{0,2},{1,3},{2,0},{3,1},{4,6},{5,7},{6,4},{7,5},{8,10},{9,11},{10,... | collective-permute-start | bytes 393224 | tf_op jit(solution)/shard_map/ppermute | solution.py:273
  192.9 18.6 %collective-permute-start.31 = (bf16[32,2048]{1,0:T(8,128)(2,1)S(1)}, bf16[32,2048]{1,0:T(8,128)(2,1)S(1)}, u32[]{:S(2)}, u32[]{:S(2)}) collective-permute-start(bf16[32,2048]{1,0:T(8,128)(2,1)S(1)} %get-tuple-element.35), channel_id=1, source_target_pairs={{0,3},{1,2},{2,1},{3,0},{4,7},{5,6},{6,5},{7,4},{8,11},{9,10},{10,... | collective-permute-start | bytes 393224 | tf_op jit(solution)/shard_map/ppermute | solution.py:273
  (29 other events, 321.8 us)

commit v5 on v4

--- a/solution.py
+++ b/solution.py
@@ -12,6 +12,7 @@
 HD = 128
 SPAN = 512
 GW = 256
+UNROLL = 2
 MASKED = -1e30
 LOG2_SCALE = math.log2(math.e) / math.sqrt(HD)
 PARTS = 2
@@ -28,7 +29,9 @@
     span = pl.program_id(0)
     slots = first_ref.shape[0]
     block_rows = k_ref.shape[0] // slots
-    nrow = q_ref.shape[0] * rows
+    per = q_ref.shape[0] // pl.num_programs(0)
+    mine = pl.ds(span * per, per)
+    nrow = per * rows
     groups = nrow * heads // GW
     score_refs, weight_refs = tile_refs[:groups], tile_refs[groups:]
 
@@ -37,7 +40,8 @@
         def take(keys, values):
             for i in range(slots):
                 at = i * block_rows
-                k_ref[at:at + block_rows, :] = keys[i, :block_rows, :]
+                k_ref[at:at + block_rows, :HD] = keys[i, :block_rows, :]
+                k_ref[at:at + block_rows, HD:] = keys[i, :block_rows, :]
                 for b in range(0, block_rows, SPAN):
                     vt_ref[(at + b) // SPAN] = values[i, b:b + SPAN, :].T
 
@@ -50,9 +54,12 @@
             take(second_ref, first_ref)
 
     own = own_ref[span]
-    q_all = q_ref[...].reshape(nrow, heads * HD)
+    q_all = q_ref[mine, part * rows:(part + 1) * rows, :].reshape(nrow, heads * HD).astype(jnp.float32) * LOG2_SCALE
     for h in range(heads):
-        qt_ref[:, h * nrow:(h + 1) * nrow] = q_all[:, h * HD:(h + 1) * HD].T
+        q_t = q_all[:, h * HD:(h + 1) * HD].T
+        high = q_t.astype(jnp.bfloat16)
+        qt_ref[:HD, h * nrow:(h + 1) * nrow] = high
+        qt_ref[HD:, h * nrow:(h + 1) * nrow] = (q_t - high.astype(jnp.float32)).astype(jnp.bfloat16)
 
     def score(blk, g):
         keys = k_ref[pl.ds(pl.multiple_of(blk * SPAN, SPAN), SPAN), :]
@@ -64,8 +71,8 @@
         old = max_ref[g]
         new = jnp.maximum(old, jnp.broadcast_to(jnp.max(top, axis=0, keepdims=True), old.shape))
         max_ref[g] = new
-        p = jnp.exp2(s.reshape(SPAN // 8, 8, GW) * LOG2_SCALE - (new * LOG2_SCALE)[None])
-        factor = jnp.exp2((old - new) * LOG2_SCALE)
+        p = jnp.exp2(s.reshape(SPAN // 8, 8, GW) - new[None])
+        factor = jnp.exp2(old - new)
         factor_ref[g] = factor
         sum_ref[g] = sum_ref[g] * factor + jnp.sum(p, axis=0)
         weight_refs[g][...] = p.reshape(SPAN, GW).astype(jnp.bfloat16)
@@ -82,15 +89,25 @@
         weight_refs[g][...] = jnp.zeros_like(weight_refs[g])
         score(loc_ref[0], g)
 
-    def body(t, carry):
+    def turn(t):
         prev = loc_ref[jnp.maximum(t - 1, 0)]
         for g in range(groups):
             apply(prev, g)
             weigh(score_refs[g][...], top_ref[g], g)
             score(loc_ref[t + 1], g)
+
+    def turns(i, carry):
+        for u in range(UNROLL):
+            turn(i * UNROLL + u)
         return carry
 
-    lax.fori_loop(0, own, body, 0)
+    def single(t, carry):
+        turn(t)
+        return carry
+
+    whole = lax.div(own, jnp.int32(UNROLL))
+    lax.fori_loop(0, whole, turns, 0)
+    lax.fori_loop(whole * UNROLL, own, single, 0)
     prev = loc_ref[jnp.maximum(own - 1, 0)]
     key_i = lax.broadcasted_iota(jnp.int32, (SPAN, GW), 0)
     col_i = lax.broadcasted_iota(jnp.int32, (SPAN, GW), 1)
@@ -108,7 +125,8 @@
         n = min(nrow, GW)
         for c in range(0, GW, n):
             h, r0 = divmod(g * GW + c, nrow)
-            out_ref[r0 // rows:(r0 + n) // rows, :, h * HD:(h + 1) * HD] = done[c:c + n].reshape(n // rows, rows, HD)
+            at = pl.ds(span * per + r0 // rows, n // rows)
+            out_ref[at, :, h * HD:(h + 1) * HD] = done[c:c + n].reshape(n // rows, rows, HD)
 
 
 def attend(own, loc, core, queries, first, second, part, tp_count):
@@ -129,15 +147,15 @@
             num_scalar_prefetch=3,
             grid=(spans,),
             in_specs=[
-                pl.BlockSpec((per, rows, width), lambda s, *_: (s, part, 0)),
+                VMEM_SPEC,
                 VMEM_SPEC,
                 VMEM_SPEC,
             ],
-            out_specs=pl.BlockSpec((per, rows, width), lambda s, *_: (s, 0, 0)),
+            out_specs=VMEM_SPEC,
             scratch_shapes=[
-                pltpu.VMEM((keys, HD), jnp.bfloat16),
+                pltpu.VMEM((keys, 2 * HD), jnp.bfloat16),
                 pltpu.VMEM((keys // SPAN, HD, SPAN), jnp.bfloat16),
-                pltpu.VMEM((HD, per * rows * heads), jnp.bfloat16),
+                pltpu.VMEM((2 * HD, per * rows * heads), jnp.bfloat16),
                 pltpu.VMEM((groups, HD // 8, 8, GW), jnp.float32),
                 pltpu.VMEM((groups, 8, GW), jnp.float32),
                 pltpu.VMEM((groups, 8, GW), jnp.float32),
@@ -335,7 +353,8 @@
     for part in range(PARTS):
         att = attend(own, loc, core[None], queries, first, second, part, tp_count)
         atts = [att]
-        for source, mask in ((0, 2), (0, 1), (1, 1)):
+        routes = ((0, 2), (0, 1), (0, 3) if part == 0 else (1, 1))
+        for source, mask in routes:
             atts.append(swapped(atts[source], mask, tp_count))
         atts = [atts[i] for i in (0, 2, 1, 3)]
         sent = project(place, atts, kept, paired, far)

time: 219 us -> 227 us (1.037)
  the two profiles are of different devices: /device:TPU:17 before, /device:TPU:19 now
where the time goes in v5:
time: 227 us; the launch traced here: 226 us
  waiting for transfers between devices  83.9 us (37%)
  Pallas kernels  68.3 us (30%)
  starting transfers between devices  54 us (24%)
  local copies, waits for them, and re-layouts  16.9 us (7%)
    ppermute x22, waiting for transfers between devices, swapped(): return lax.ppermute(value, 'tp', [(i, i ^ mask) for i in range(count)])  70.6 us
    pallas_call x2, Pallas kernels, attend(): pl.pallas_call(functools.partial(attend_kernel, rows=rows, part=part, hea...  46.8 us
    ppermute x22, starting transfers between devices, swapped(): return lax.ppermute(value, 'tp', [(i, i ^ mask) for i in range(count)])  30.4 us
    ppermute x7, starting transfers between devices, shards(): pieces.append(lax.ppermute(mine, 'ctx', pairs))  17.8 us
    ppermute x7, waiting for transfers between devices, shards(): pieces.append(lax.ppermute(mine, 'ctx', pairs))  13.3 us
    pallas_call x2, Pallas kernels, project(): pl.pallas_call(project_kernel, out_shape=[jax.ShapeDtypeStruct((rows // 4...  13.1 us
    unnamed x42, local copies, waits for them, and re-layouts  8.91 us
    ppermute x3, starting transfers between devices, shards(): far.append(lax.ppermute(side, 'ctx', pairs))  5.85 us
  transfers between devices with their start and end apart: 32, of which 14 were waited for; matrix products, arithmetic and copies ran while one was open for 3% of the time, Pallas kernels for 28%

profile of v5, /device:TPU:19, one launch (start us, length us, event | category | flops | bytes accessed | tf_op | source)
XLA Modules:
  0.0 226.4 jit_solution(17104471672090182160)
XLA Ops:
  10.0 3.9 %collective-permute-done.6.refs_7_ = bf16[1040,128]{1,0:T(8,128)(2,1)S(1)} collective-permute-done((bf16[1040,128]{1,0:T(8,128)(2,1)S(1)}, bf16[1040,128]{1,0:T(8,128)(2,1)S(1)}, u32[]{:S(2)}, u32[]{:S(2)}) %collective-permute-start.6) | collective-permute-done | bytes 266272 | tf_op jit(solution)/shard_map/ppermute | solution.py:330
  13.9 10.6 %collective-permute-start.1 = (bf16[1040,128]{1,0:T(8,128)(2,1)S(1)}, bf16[1040,128]{1,0:T(8,128)(2,1)S(1)}, u32[]{:S(2)}, u32[]{:S(2)}) collective-permute-start(bf16[1040,128]{1,0:T(8,128)(2,1)S(1)} %pad_maximum_fusion.refs_0_), channel_id=1, source_target_pairs={{0,16},{16,32},{32,48},{48,0},{64,80},{80,96},{96,112},{112,64},{1... | collective-permute-start | bytes 798728 | tf_op jit(solution)/shard_map/ppermute | solution.py:330
  24.5 4.7 %collective-permute-done.3.refs_4_ = bf16[1040,128]{1,0:T(8,128)(2,1)S(1)} collective-permute-done((bf16[1040,128]{1,0:T(8,128)(2,1)S(1)}, bf16[1040,128]{1,0:T(8,128)(2,1)S(1)}, u32[]{:S(2)}, u32[]{:S(2)}) %collective-permute-start.3) | collective-permute-done | bytes 266272 | tf_op jit(solution)/shard_map/ppermute | solution.py:330
  29.2 4.7 %collective-permute-done.refs_1_ = bf16[1040,128]{1,0:T(8,128)(2,1)S(1)} collective-permute-done((bf16[1040,128]{1,0:T(8,128)(2,1)S(1)}, bf16[1040,128]{1,0:T(8,128)(2,1)S(1)}, u32[]{:S(2)}, u32[]{:S(2)}) %collective-permute-start) | collective-permute-done | bytes 266272 | tf_op jit(solution)/shard_map/ppermute | solution.py:330
  34.6 2.9 %shard_map.95.first_ref = bf16[8,1040,128]{2,1,0:T(8,128)(2,1)} custom-call(bf16[1040,128]{1,0:T(8,128)(2,1)} %copy-done.13, bf16[1040,128]{1,0:T(8,128)(2,1)} %copy-done.20, bf16[1040,128]{1,0:T(8,128)(2,1)} %copy-done.19, bf16[1040,128]{1,0:T(8,128)(2,1)} %copy-done.18, bf16[1040,128]{1,0:T(8,128)(2,1)} %copy-done.17, bf16[1040,128]{1,0:T(8,128)(2,1)} %copy-done.16, ...), custom_call_target="tpu_custom_call" | custom-call | tf_op jit(solution)/shard_map/pallas_call | solution.py:183
  37.6 3.0 %collective-permute-start.7 = (bf16[8,1040,128]{2,1,0:T(8,128)(2,1)}, bf16[8,1040,128]{2,1,0:T(8,128)(2,1)}, u32[]{:S(2)}, u32[]{:S(2)}) collective-permute-start(bf16[8,1040,128]{2,1,0:T(8,128)(2,1)} %shard_map.95.first_ref), channel_id=1, source_target_pairs={{0,1},{1,0},{2,3},{3,2},{4,5},{5,4},{6,7},{7,6},{8,9},{9,8},{10,11... | collective-permute-start | bytes 6389768 | tf_op jit(solution)/shard_map/ppermute | solution.py:291
  44.2 5.0 %constant_dynamic-slice_fusion.2 = (bf16[512,2048]{1,0:T(8,128)(2,1)}, bf16[512,2048]{1,0:T(8,128)(2,1)}) fusion(bf16[512,8192]{1,0:T(8,128)(2,1)} %param.12, s32[]{:T(128)S(6)} %select_n.39, s32[]{:T(128)S(6)} %select_n.38), kind=kLoop, calls=%fused_computation.10 | loop fusion | bytes 8388616 | tf_op jit(solution)/shard_map/dynamic_slice | solution.py:348
  50.3 7.0 %collective-permute-done.13.refs_1_ = bf16[512,512]{1,0:T(8,128)(2,1)} collective-permute-done((bf16[512,512]{1,0:T(8,128)(2,1)}, bf16[512,512]{1,0:T(8,128)(2,1)}, u32[]{:S(2)}, u32[]{:S(2)}) %collective-permute-start.13) | collective-permute-done | bytes 524320 | tf_op jit(solution)/shard_map/ppermute | solution.py:291
  57.3 10.2 %collective-permute-done.12.refs_0_ = bf16[512,512]{1,0:T(8,128)(2,1)} collective-permute-done((bf16[512,512]{1,0:T(8,128)(2,1)}, bf16[512,512]{1,0:T(8,128)(2,1)}, u32[]{:S(2)}, u32[]{:S(2)}) %collective-permute-start.12) | collective-permute-done | bytes 524320 | tf_op jit(solution)/shard_map/ppermute | solution.py:291
  69.8 3.8 %collective-permute-start.15 = (bf16[2,512,512]{2,1,0:T(8,128)(2,1)}, bf16[2,512,512]{2,1,0:T(8,128)(2,1)S(1)}, u32[]{:S(2)}, u32[]{:S(2)}) collective-permute-start(bf16[2,512,512]{2,1,0:T(8,128)(2,1)} %shard_map.97.refs_6_), channel_id=1, source_target_pairs={{0,32},{16,48},{32,0},{48,16},{64,96},{80,112},{96,64},{112,80},{1... | collective-permute-start | bytes 3145736 | tf_op jit(solution)/shard_map/ppermute | solution.py:347
  75.6 23.4 %shard_map.96.refs_0_ = bf16[16,32,512]{2,1,0:T(8,128)(2,1)} custom-call(s32[2]{0:T(128)S(1)} %get-tuple-element.39.own_ref, s32[16]{0:T(128)S(1)} %select_reduce_fusion.loc_ref, s32[1]{0:T(128)} %bitcast.4.core_ref, bf16[16,64,512]{2,1,0:T(8,128)(2,1)S(1)} %bitcast.8, bf16[8,1040,128]{2,1,0:T(8,128)(2,1)S(1)} %copy-done.1, ...), custom_call_target="tpu_custom_call" | custom-call | flops 17179869184 | bytes 4194304 | tf_op jit(solution)/shard_map/pallas_call | solution.py:143
  99.3 23.4 %shard_map.98.refs_0_ = bf16[16,32,512]{2,1,0:T(8,128)(2,1)} custom-call(s32[2]{0:T(128)S(1)} %get-tuple-element.39.own_ref, s32[16]{0:T(128)S(1)} %select_reduce_fusion.loc_ref, s32[1]{0:T(128)} %bitcast.4.core_ref, bf16[16,64,512]{2,1,0:T(8,128)(2,1)S(1)} %bitcast.9, bf16[8,1040,128]{2,1,0:T(8,128)(2,1)S(1)} %copy-done.1, ...), custom_call_target="tpu_custom_call" | custom-call | flops 17179869184 | bytes 4194304 | tf_op jit(solution)/shard_map/pallas_call | solution.py:143
  123.7 3.2 %collective-permute-start.25 = (bf16[16,32,512]{2,1,0:T(8,128)(2,1)}, bf16[16,32,512]{2,1,0:T(8,128)(2,1)S(1)}, u32[]{:S(2)}, u32[]{:S(2)}) collective-permute-start(bf16[16,32,512]{2,1,0:T(8,128)(2,1)} %shard_map.98.refs_0_), channel_id=1, source_target_pairs={{0,3},{1,2},{2,1},{3,0},{4,7},{5,6},{6,5},{7,4},{8,11},{9,10},{10,... | collective-permute-start | bytes 1572872 | tf_op jit(solution)/shard_map/ppermute | solution.py:291
  129.9 10.0 %collective-permute-done.25.refs_3_ = bf16[16,32,512]{2,1,0:T(8,128)(2,1)S(1)} collective-permute-done((bf16[16,32,512]{2,1,0:T(8,128)(2,1)}, bf16[16,32,512]{2,1,0:T(8,128)(2,1)S(1)}, u32[]{:S(2)}, u32[]{:S(2)}) %collective-permute-start.25) | collective-permute-done | bytes 524320 | tf_op jit(solution)/shard_map/ppermute | solution.py:291
  139.8 11.2 %collective-permute-done.24.refs_2_ = bf16[16,32,512]{2,1,0:T(8,128)(2,1)S(1)} collective-permute-done((bf16[16,32,512]{2,1,0:T(8,128)(2,1)}, bf16[16,32,512]{2,1,0:T(8,128)(2,1)S(1)}, u32[]{:S(2)}, u32[]{:S(2)}) %collective-permute-start.24) | collective-permute-done | bytes 524320 | tf_op jit(solution)/shard_map/ppermute | solution.py:291
  156.3 6.4 %project.3 = (bf16[128,2048]{1,0:T(8,128)(2,1)S(1)}, bf16[128,2048]{1,0:T(8,128)(2,1)S(1)}, bf16[128,2048]{1,0:T(8,128)(2,1)S(1)}, bf16[128,2048]{1,0:T(8,128)(2,1)S(1)}) custom-call(s32[3]{0:T(128)S(1)} %pad_add_fusion.place_ref, bf16[16,32,512]{2,1,0:T(8,128)(2,1)} %shard_map.98.refs_0_, bf16[16,32,512]{2,1,0:T(8,128)(2,1)S(1)} %collective-permute-done.23.refs_1_, ...), custom_call_target="tpu_custom_call" | custom-call | flops 4294967296 | bytes 8388608 | tf_op jit(solution)/shard_map/project/pallas_call | solution.py:213
  164.5 3.6 %collective-permute-start.27 = (bf16[128,2048]{1,0:T(8,128)(2,1)S(1)}, bf16[128,2048]{1,0:T(8,128)(2,1)S(1)}, u32[]{:S(2)}, u32[]{:S(2)}) collective-permute-start(bf16[128,2048]{1,0:T(8,128)(2,1)S(1)} %get-tuple-element.30), channel_id=1, source_target_pairs={{0,8},{1,9},{2,10},{3,11},{4,12},{5,13},{6,14},{7,15},{8,0},{9,1},... | collective-permute-start | bytes 1572872 | tf_op jit(solution)/shard_map/ppermute | solution.py:291
  169.2 6.6 %project.2 = (bf16[128,2048]{1,0:T(8,128)(2,1)S(1)}, bf16[128,2048]{1,0:T(8,128)(2,1)S(1)}, bf16[128,2048]{1,0:T(8,128)(2,1)S(1)}, bf16[128,2048]{1,0:T(8,128)(2,1)S(1)}) custom-call(s32[3]{0:T(128)S(1)} %pad_add_fusion.place_ref, bf16[16,32,512]{2,1,0:T(8,128)(2,1)} %shard_map.96.refs_0_, bf16[16,32,512]{2,1,0:T(8,128)(2,1)S(1)} %collective-permute-done.8.refs_1_, ...), custom_call_target="tpu_custom_call" | custom-call | flops 4294967296 | bytes 8388608 | tf_op jit(solution)/shard_map/project/pallas_call | solution.py:213
  177.5 3.0 %collective-permute-start.18 = (bf16[128,2048]{1,0:T(8,128)(2,1)S(1)}, bf16[128,2048]{1,0:T(8,128)(2,1)S(1)}, u32[]{:S(2)}, u32[]{:S(2)}) collective-permute-start(bf16[128,2048]{1,0:T(8,128)(2,1)S(1)} %get-tuple-element.22), channel_id=1, source_target_pairs={{0,8},{1,9},{2,10},{3,11},{4,12},{5,13},{6,14},{7,15},{8,0},{9,1},... | collective-permute-start | bytes 1572872 | tf_op jit(solution)/shard_map/ppermute | solution.py:291
  182.4 7.4 %collective-permute-done.27.refs_2_ = bf16[128,2048]{1,0:T(8,128)(2,1)S(1)} collective-permute-done((bf16[128,2048]{1,0:T(8,128)(2,1)S(1)}, bf16[128,2048]{1,0:T(8,128)(2,1)S(1)}, u32[]{:S(2)}, u32[]{:S(2)}) %collective-permute-start.27) | collective-permute-done | bytes 524320 | tf_op jit(solution)/shard_map/ppermute | solution.py:291
  192.2 2.3 %collective-permute-start.29 = (bf16[32,2048]{1,0:T(8,128)(2,1)S(1)}, bf16[32,2048]{1,0:T(8,128)(2,1)S(1)}, u32[]{:S(2)}, u32[]{:S(2)}) collective-permute-start(bf16[32,2048]{1,0:T(8,128)(2,1)S(1)} %get-tuple-element.33), channel_id=1, source_target_pairs={{0,1},{1,0},{2,3},{3,2},{4,5},{5,4},{6,7},{7,6},{8,9},{9,8},{10,11... | collective-permute-start | bytes 393224 | tf_op jit(solution)/shard_map/ppermute | solution.py:291
  194.6 5.3 %collective-permute-done.17.refs_1_ = bf16[128,2048]{1,0:T(8,128)(2,1)S(1)} collective-permute-done((bf16[128,2048]{1,0:T(8,128)(2,1)S(1)}, bf16[128,2048]{1,0:T(8,128)(2,1)S(1)}, u32[]{:S(2)}, u32[]{:S(2)}) %collective-permute-start.17) | collective-permute-done | bytes 524320 | tf_op jit(solution)/shard_map/ppermute | solution.py:291
  201.4 10.9 %collective-permute-done.18.refs_2_ = bf16[128,2048]{1,0:T(8,128)(2,1)S(1)} collective-permute-done((bf16[128,2048]{1,0:T(8,128)(2,1)S(1)}, bf16[128,2048]{1,0:T(8,128)(2,1)S(1)}, u32[]{:S(2)}, u32[]{:S(2)}) %collective-permute-start.18) | collective-permute-done | bytes 524320 | tf_op jit(solution)/shard_map/ppermute | solution.py:291
  221.9 3.1 %collective-permute-done.22.d = bf16[32,2048]{1,0:T(8,128)(2,1)S(1)} collective-permute-done((bf16[32,2048]{1,0:T(8,128)(2,1)S(1)}, bf16[32,2048]{1,0:T(8,128)(2,1)S(1)}, u32[]{:S(2)}, u32[]{:S(2)}) %collective-permute-start.22) | collective-permute-done | bytes 131104 | tf_op jit(solution)/shard_map/ppermute | solution.py:291
  (103 shorter events, 49.2 us)
Async XLA Ops:
  4.4 20.1 %collective-permute-start.5 = (bf16[1040,128]{1,0:T(8,128)(2,1)S(1)}, bf16[1040,128]{1,0:T(8,128)(2,1)S(1)}, u32[]{:S(2)}, u32[]{:S(2)}) collective-permute-start(bf16[1040,128]{1,0:T(8,128)(2,1)S(1)} %pad_maximum_fusion.refs_0_), channel_id=1, source_target_pairs={{0,80},{16,96},{32,112},{48,64},{64,16},{80,32},{96,48},{112,0},{1... | collective-permute-start | bytes 798728 | tf_op jit(solution)/shard_map/ppermute | solution.py:330
  5.3 19.2 %collective-permute-start.4 = (bf16[1040,128]{1,0:T(8,128)(2,1)S(1)}, bf16[1040,128]{1,0:T(8,128)(2,1)S(1)}, u32[]{:S(2)}, u32[]{:S(2)}) collective-permute-start(bf16[1040,128]{1,0:T(8,128)(2,1)S(1)} %pad_maximum_fusion.refs_0_), channel_id=1, source_target_pairs={{0,96},{16,112},{32,64},{48,80},{64,32},{80,48},{96,0},{112,16},{1... | collective-permute-start | bytes 798728 | tf_op jit(solution)/shard_map/ppermute | solution.py:330
  6.6 22.6 %collective-permute-start.3 = (bf16[1040,128]{1,0:T(8,128)(2,1)S(1)}, bf16[1040,128]{1,0:T(8,128)(2,1)S(1)}, u32[]{:S(2)}, u32[]{:S(2)}) collective-permute-start(bf16[1040,128]{1,0:T(8,128)(2,1)S(1)} %pad_maximum_fusion.refs_0_), channel_id=1, source_target_pairs={{0,64},{16,80},{32,96},{48,112},{64,0},{80,16},{96,32},{112,48},{1... | collective-permute-start | bytes 798728 | tf_op jit(solution)/shard_map/ppermute | solution.py:330
  8.2 21.0 %collective-permute-start.2 = (bf16[1040,128]{1,0:T(8,128)(2,1)S(1)}, bf16[1040,128]{1,0:T(8,128)(2,1)S(1)}, u32[]{:S(2)}, u32[]{:S(2)}) collective-permute-start(bf16[1040,128]{1,0:T(8,128)(2,1)S(1)} %pad_maximum_fusion.refs_0_), channel_id=1, source_target_pairs={{0,48},{16,0},{32,16},{48,32},{64,112},{80,64},{96,80},{112,96},{1... | collective-permute-start | bytes 798728 | tf_op jit(solution)/shard_map/ppermute | solution.py:330
  37.6 38.1 %collective-permute-start.7 = (bf16[8,1040,128]{2,1,0:T(8,128)(2,1)}, bf16[8,1040,128]{2,1,0:T(8,128)(2,1)}, u32[]{:S(2)}, u32[]{:S(2)}) collective-permute-start(bf16[8,1040,128]{2,1,0:T(8,128)(2,1)} %shard_map.95.first_ref), channel_id=1, source_target_pairs={{0,1},{1,0},{2,3},{3,2},{4,5},{5,4},{6,7},{7,6},{8,9},{9,8},{10,11... | collective-permute-start | bytes 6389768 | tf_op jit(solution)/shard_map/ppermute | solution.py:291
  43.0 24.6 %collective-permute-start.12 = (bf16[512,512]{1,0:T(8,128)(2,1)}, bf16[512,512]{1,0:T(8,128)(2,1)}, u32[]{:S(2)}, u32[]{:S(2)}) collective-permute-start(bf16[512,512]{1,0:T(8,128)(2,1)} %get-tuple-element.41), channel_id=1, source_target_pairs={{0,2},{1,3},{2,0},{3,1},{4,6},{5,7},{6,4},{7,5},{8,10},{9,11},{10,... | collective-permute-start | bytes 1572872 | tf_op jit(solution)/shard_map/ppermute | solution.py:291
  49.1 80.2 %collective-permute-start.11 = (bf16[512,2048]{1,0:T(8,128)(2,1)}, bf16[512,2048]{1,0:T(8,128)(2,1)}, u32[]{:S(2)}, u32[]{:S(2)}) collective-permute-start(bf16[512,2048]{1,0:T(8,128)(2,1)} %get-tuple-element.42), channel_id=1, source_target_pairs={{0,1},{1,0},{2,3},{3,2},{4,5},{5,4},{6,7},{7,6},{8,9},{9,8},{10,11... | collective-permute-start | bytes 6291464 | tf_op jit(solution)/shard_map/ppermute | solution.py:291
  69.8 52.9 %collective-permute-start.16 = (bf16[2,512,512]{2,1,0:T(8,128)(2,1)}, bf16[2,512,512]{2,1,0:T(8,128)(2,1)S(1)}, u32[]{:S(2)}, u32[]{:S(2)}) collective-permute-start(bf16[2,512,512]{2,1,0:T(8,128)(2,1)} %shard_map.97.refs_6_), channel_id=1, source_target_pairs={{0,48},{16,0},{32,16},{48,32},{64,112},{80,64},{96,80},{112,96},{1... | collective-permute-start | bytes 3145736 | tf_op jit(solution)/shard_map/ppermute | solution.py:347
  69.8 57.1 %collective-permute-start.15 = (bf16[2,512,512]{2,1,0:T(8,128)(2,1)}, bf16[2,512,512]{2,1,0:T(8,128)(2,1)S(1)}, u32[]{:S(2)}, u32[]{:S(2)}) collective-permute-start(bf16[2,512,512]{2,1,0:T(8,128)(2,1)} %shard_map.97.refs_6_), channel_id=1, source_target_pairs={{0,32},{16,48},{32,0},{48,16},{64,96},{80,112},{96,64},{112,80},{1... | collective-permute-start | bytes 3145736 | tf_op jit(solution)/shard_map/ppermute | solution.py:347
  73.6 54.5 %collective-permute-start.14 = (bf16[2,512,512]{2,1,0:T(8,128)(2,1)}, bf16[2,512,512]{2,1,0:T(8,128)(2,1)S(1)}, u32[]{:S(2)}, u32[]{:S(2)}) collective-permute-start(bf16[2,512,512]{2,1,0:T(8,128)(2,1)} %shard_map.97.refs_6_), channel_id=1, source_target_pairs={{0,16},{16,32},{32,48},{48,0},{64,80},{80,96},{96,112},{112,64},{1... | collective-permute-start | bytes 3145736 | tf_op jit(solution)/shard_map/ppermute | solution.py:347
  99.0 30.7 %collective-permute-start.9 = (bf16[16,32,512]{2,1,0:T(8,128)(2,1)}, bf16[16,32,512]{2,1,0:T(8,128)(2,1)}, u32[]{:S(2)}, u32[]{:S(2)}) collective-permute-start(bf16[16,32,512]{2,1,0:T(8,128)(2,1)} %shard_map.96.refs_0_), channel_id=1, source_target_pairs={{0,2},{1,3},{2,0},{3,1},{4,6},{5,7},{6,4},{7,5},{8,10},{9,11},{10,... | collective-permute-start | bytes 1572872 | tf_op jit(solution)/shard_map/ppermute | solution.py:291
  127.9 23.2 %collective-permute-start.24 = (bf16[16,32,512]{2,1,0:T(8,128)(2,1)}, bf16[16,32,512]{2,1,0:T(8,128)(2,1)S(1)}, u32[]{:S(2)}, u32[]{:S(2)}) collective-permute-start(bf16[16,32,512]{2,1,0:T(8,128)(2,1)} %shard_map.98.refs_0_), channel_id=1, source_target_pairs={{0,2},{1,3},{2,0},{3,1},{4,6},{5,7},{6,4},{7,5},{8,10},{9,11},{10,... | collective-permute-start | bytes 1572872 | tf_op jit(solution)/shard_map/ppermute | solution.py:291
  129.1 22.0 %collective-permute-start.23 = (bf16[16,32,512]{2,1,0:T(8,128)(2,1)}, bf16[16,32,512]{2,1,0:T(8,128)(2,1)S(1)}, u32[]{:S(2)}, u32[]{:S(2)}) collective-permute-start(bf16[16,32,512]{2,1,0:T(8,128)(2,1)} %shard_map.98.refs_0_), channel_id=1, source_target_pairs={{0,1},{1,0},{2,3},{3,2},{4,5},{5,4},{6,7},{7,6},{8,9},{9,8},{10,11... | collective-permute-start | bytes 1572872 | tf_op jit(solution)/shard_map/ppermute | solution.py:291
  129.3 39.8 %collective-permute-start.8 = (bf16[16,32,512]{2,1,0:T(8,128)(2,1)}, bf16[16,32,512]{2,1,0:T(8,128)(2,1)S(1)}, u32[]{:S(2)}, u32[]{:S(2)}) collective-permute-start(bf16[16,32,512]{2,1,0:T(8,128)(2,1)} %shard_map.96.refs_0_), channel_id=1, source_target_pairs={{0,1},{1,0},{2,3},{3,2},{4,5},{5,4},{6,7},{7,6},{8,9},{9,8},{10,11... | collective-permute-start | bytes 1572872 | tf_op jit(solution)/shard_map/ppermute | solution.py:291
  129.7 39.4 %collective-permute-start.10 = (bf16[16,32,512]{2,1,0:T(8,128)(2,1)}, bf16[16,32,512]{2,1,0:T(8,128)(2,1)S(1)}, u32[]{:S(2)}, u32[]{:S(2)}) collective-permute-start(bf16[16,32,512]{2,1,0:T(8,128)(2,1)} %collective-permute-done.9.refs_2_), channel_id=1, source_target_pairs={{0,1},{1,0},{2,3},{3,2},{4,5},{5,4},{6,7},{7,6},{8,9},{9,8},{10,11... | collective-permute-start | bytes 1572872 | tf_op jit(solution)/shard_map/ppermute | solution.py:291
  162.8 17.7 %collective-permute-start.26 = (bf16[128,2048]{1,0:T(8,128)(2,1)S(1)}, bf16[128,2048]{1,0:T(8,128)(2,1)S(1)}, u32[]{:S(2)}, u32[]{:S(2)}) collective-permute-start(bf16[128,2048]{1,0:T(8,128)(2,1)S(1)} %get-tuple-element.29), channel_id=1, source_target_pairs={{0,4},{1,5},{2,6},{3,7},{4,0},{5,1},{6,2},{7,3},{8,12},{9,13},{10,... | collective-permute-start | bytes 1572872 | tf_op jit(solution)/shard_map/ppermute | solution.py:291
  164.5 25.3 %collective-permute-start.27 = (bf16[128,2048]{1,0:T(8,128)(2,1)S(1)}, bf16[128,2048]{1,0:T(8,128)(2,1)S(1)}, u32[]{:S(2)}, u32[]{:S(2)}) collective-permute-start(bf16[128,2048]{1,0:T(8,128)(2,1)S(1)} %get-tuple-element.30), channel_id=1, source_target_pairs={{0,8},{1,9},{2,10},{3,11},{4,12},{5,13},{6,14},{7,15},{8,0},{9,1},... | collective-permute-start | bytes 1572872 | tf_op jit(solution)/shard_map/ppermute | solution.py:291
  168.1 23.8 %collective-permute-start.28 = (bf16[128,2048]{1,0:T(8,128)(2,1)S(1)}, bf16[128,2048]{1,0:T(8,128)(2,1)S(1)}, u32[]{:S(2)}, u32[]{:S(2)}) collective-permute-start(bf16[128,2048]{1,0:T(8,128)(2,1)S(1)} %get-tuple-element.31), channel_id=1, source_target_pairs={{0,12},{1,13},{2,14},{3,15},{4,8},{5,9},{6,10},{7,11},{8,4},{9,5},... | collective-permute-start | bytes 1572872 | tf_op jit(solution)/shard_map/ppermute | solution.py:291
  175.8 24.1 %collective-permute-start.17 = (bf16[128,2048]{1,0:T(8,128)(2,1)S(1)}, bf16[128,2048]{1,0:T(8,128)(2,1)S(1)}, u32[]{:S(2)}, u32[]{:S(2)}) collective-permute-start(bf16[128,2048]{1,0:T(8,128)(2,1)S(1)} %get-tuple-element.21), channel_id=1, source_target_pairs={{0,4},{1,5},{2,6},{3,7},{4,0},{5,1},{6,2},{7,3},{8,12},{9,13},{10,... | collective-permute-start | bytes 1572872 | tf_op jit(solution)/shard_map/ppermute | solution.py:291
  177.5 34.8 %collective-permute-start.18 = (bf16[128,2048]{1,0:T(8,128)(2,1)S(1)}, bf16[128,2048]{1,0:T(8,128)(2,1)S(1)}, u32[]{:S(2)}, u32[]{:S(2)}) collective-permute-start(bf16[128,2048]{1,0:T(8,128)(2,1)S(1)} %get-tuple-element.22), channel_id=1, source_target_pairs={{0,8},{1,9},{2,10},{3,11},{4,12},{5,13},{6,14},{7,15},{8,0},{9,1},... | collective-permute-start | bytes 1572872 | tf_op jit(solution)/shard_map/ppermute | solution.py:291
  180.5 33.9 %collective-permute-start.19 = (bf16[128,2048]{1,0:T(8,128)(2,1)S(1)}, bf16[128,2048]{1,0:T(8,128)(2,1)S(1)}, u32[]{:S(2)}, u32[]{:S(2)}) collective-permute-start(bf16[128,2048]{1,0:T(8,128)(2,1)S(1)} %get-tuple-element.23), channel_id=1, source_target_pairs={{0,12},{1,13},{2,14},{3,15},{4,8},{5,9},{6,10},{7,11},{8,4},{9,5},... | collective-permute-start | bytes 1572872 | tf_op jit(solution)/shard_map/ppermute | solution.py:291
  192.2 24.8 %collective-permute-start.29 = (bf16[32,2048]{1,0:T(8,128)(2,1)S(1)}, bf16[32,2048]{1,0:T(8,128)(2,1)S(1)}, u32[]{:S(2)}, u32[]{:S(2)}) collective-permute-start(bf16[32,2048]{1,0:T(8,128)(2,1)S(1)} %get-tuple-element.33), channel_id=1, source_target_pairs={{0,1},{1,0},{2,3},{3,2},{4,5},{5,4},{6,7},{7,6},{8,9},{9,8},{10,11... | collective-permute-start | bytes 393224 | tf_op jit(solution)/shard_map/ppermute | solution.py:291
  194.6 24.8 %collective-permute-start.30 = (bf16[32,2048]{1,0:T(8,128)(2,1)S(1)}, bf16[32,2048]{1,0:T(8,128)(2,1)S(1)}, u32[]{:S(2)}, u32[]{:S(2)}) collective-permute-start(bf16[32,2048]{1,0:T(8,128)(2,1)S(1)} %get-tuple-element.34), channel_id=1, source_target_pairs={{0,2},{1,3},{2,0},{3,1},{4,6},{5,7},{6,4},{7,5},{8,10},{9,11},{10,... | collective-permute-start | bytes 393224 | tf_op jit(solution)/shard_map/ppermute | solution.py:291
  199.9 19.5 %collective-permute-start.31 = (bf16[32,2048]{1,0:T(8,128)(2,1)S(1)}, bf16[32,2048]{1,0:T(8,128)(2,1)S(1)}, u32[]{:S(2)}, u32[]{:S(2)}) collective-permute-start(bf16[32,2048]{1,0:T(8,128)(2,1)S(1)} %get-tuple-element.35), channel_id=1, source_target_pairs={{0,3},{1,2},{2,1},{3,0},{4,7},{5,6},{6,5},{7,4},{8,11},{9,10},{10,... | collective-permute-start | bytes 393224 | tf_op jit(solution)/shard_map/ppermute | solution.py:291
  (29 other events, 341.2 us)

commit v6 on v5

--- a/solution.py
+++ b/solution.py
@@ -191,35 +191,42 @@
 
 
 def project_kernel(place_ref, *refs):
-    atts, near, far, outs, acc_ref = refs[:4], refs[4:6], refs[6:10], refs[10:14], refs[14]
-    rows, cut = acc_ref.shape
+    atts, near, across, far, outs, acc_ref = refs[:4], refs[4:6], refs[6:8], refs[8:12], refs[12:16], refs[16]
+    rows = acc_ref.shape[0]
     n = outs[0].shape[0]
-    for j, w in enumerate(far):
-        cols = pl.ds(pl.multiple_of(((place_ref[2] - j) & (len(far) - 1)) * cut, cut), cut)
+    direct, cut = across[0].shape[1], far[0].shape[2]
+
+    def multiply(cols, width, others):
         total = None
-        for m, a in enumerate(atts):
-            weight = near[m][:, cols] if m < 2 else w[m - 2]
+        for a, weight in zip(atts, [w[:, cols] for w in near] + others):
             term = jnp.dot(a[...].reshape(rows, a.shape[-1]), weight, preferred_element_type=jnp.float32)
             total = term if total is None else total + term
-        acc_ref[...] = total
+        acc_ref[:, :width] = total
         for i, o in enumerate(outs):
-            o[:, cols] = acc_ref[pl.ds(pl.multiple_of((place_ref[1] ^ i) * n, n), n), :].astype(jnp.bfloat16)
-
-
-def project(place, atts, kept, paired, far):
+            group = pl.ds(pl.multiple_of((place_ref[1] ^ i) * n, n), n)
+            o[:, cols] = acc_ref[group, :width].astype(jnp.bfloat16)
+
+    wide = acc_ref.shape[1]
+    for c in range(0, direct, wide):
+        multiply(slice(c, c + wide), wide, [w[:, c:c + wide] for w in across])
+    for j, w in enumerate(far):
+        at = direct + ((place_ref[2] - j) & (len(far) - 1)) * cut
+        multiply(pl.ds(pl.multiple_of(at, cut), cut), cut, [w[0], w[1]])
+
+
+def project(place, atts, near, across, far):
     tps, r, k = atts[0].shape
-    rows, cut = tps * r, far[0].shape[-1]
-    n = cut * len(far)
+    rows, n = tps * r, near[0].shape[1]
     return pl.pallas_call(
         project_kernel,
         out_shape=[jax.ShapeDtypeStruct((rows // 4, n), jnp.bfloat16)] * 4,
-        in_specs=[pl.BlockSpec(memory_space=pltpu.SMEM)] + [VMEM_SPEC] * (6 + len(far)),
+        in_specs=[pl.BlockSpec(memory_space=pltpu.SMEM)] + [VMEM_SPEC] * (8 + len(far)),
         out_specs=[VMEM_SPEC] * 4,
-        scratch_shapes=[pltpu.VMEM((rows, cut), jnp.float32)],
+        scratch_shapes=[pltpu.VMEM((rows, across[0].shape[1] // 2), jnp.float32)],
         compiler_params=pltpu.CompilerParams(vmem_limit_bytes=16 * 2**20),
         cost_estimate=pl.CostEstimate(flops=8 * rows * k * n, bytes_accessed=8 * k * n, transcendentals=0),
         name="project",
-    )(place, *atts, kept, paired, *far)
+    )(place, *atts, *near, *across, *far)
 
 
 def add_kernel(m_ref, *refs):
@@ -335,16 +342,21 @@
     loc = jnp.sum(jnp.where(order[None, :] == blocks[:, None], blocks[None, :], 0), axis=1)
 
     quarter = out_weight.shape[1] // 4
-    cut = quarter // Y_COUNT
+    direct = quarter // 2
+    cut = (quarter - direct) // Y_COUNT
     sides = []
     for i in (2, 3):
-        w = lax.dynamic_slice_in_dim(out_weight, (member ^ i) * quarter + y_rank * cut, cut, 1)
+        w = lax.dynamic_slice_in_dim(out_weight, (member ^ i) * quarter + direct + y_rank * cut, cut, 1)
         sides.append(swapped(w, i, tp_count))
     side = stacked(sides)
     far = [side]
     for dy in (1, 2, 3):
         pairs = [(c, c - c % Y_COUNT + (c + dy) % Y_COUNT) for c in range(ctx_count)]
         far.append(lax.ppermute(side, "ctx", pairs))
+    across = []
+    for i in (2, 3):
+        w = lax.dynamic_slice_in_dim(out_weight, (member ^ i) * quarter, direct, 1)
+        across.append(swapped(w, i, tp_count))
     kept, w = (lax.dynamic_slice_in_dim(out_weight, (member ^ i) * quarter, quarter, 1) for i in (0, 1))
     paired = swapped(w, 1, tp_count)
     place = jnp.stack([member, group, y_rank])
@@ -353,11 +365,11 @@
     for part in range(PARTS):
         att = attend(own, loc, core[None], queries, first, second, part, tp_count)
         atts = [att]
-        routes = ((0, 2), (0, 1), (0, 3) if part == 0 else (1, 1))
+        routes = ((0, 2), (0, 1), (1, 1))
         for source, mask in routes:
             atts.append(swapped(atts[source], mask, tp_count))
         atts = [atts[i] for i in (0, 2, 1, 3)]
-        sent = project(place, atts, kept, paired, far)
+        sent = project(place, atts, (kept, paired), across, far)
         got = [sent[0]]
         for i in (1, 2, 3):
             got.append(swapped(sent[i], 4 * i, tp_count))

time: 227 us -> 203 us (0.89)
  the two profiles are of different devices: /device:TPU:19 before, /device:TPU:0 now
where the time goes in v6:
time: 203 us; the launch traced here: 201 us
  waiting for transfers between devices  84.3 us (42%)
  Pallas kernels  55.3 us (27%)
  starting transfers between devices  40.7 us (20%)
  local copies, waits for them, and re-layouts  17.1 us (8%)
    ppermute x24, waiting for transfers between devices, swapped(): return lax.ppermute(value, 'tp', [(i, i ^ mask) for i in range(count)])  61.5 us
    pallas_call x2, Pallas kernels, attend(): pl.pallas_call(functools.partial(attend_kernel, rows=rows, part=part, hea...  32.7 us
    ppermute x24, starting transfers between devices, swapped(): return lax.ppermute(value, 'tp', [(i, i ^ mask) for i in range(count)])  26.3 us
    ppermute x7, waiting for transfers between devices, shards(): pieces.append(lax.ppermute(mine, 'ctx', pairs))  22.8 us
    pallas_call x2, Pallas kernels, project(): pl.pallas_call(project_kernel, out_shape=[jax.ShapeDtypeStruct((rows // 4...  14.5 us
    ppermute x7, starting transfers between devices, shards(): pieces.append(lax.ppermute(mine, 'ctx', pairs))  14.2 us
    unnamed x44, local copies, waits for them, and re-layouts  7.14 us
    dynamic_slice x1, local copies, waits for them, and re-layouts, shards(): lax.dynamic_slice_in_dim(out_weight, (member ^ i) * quarter, quarter, 1)  5.05 us
  transfers between devices with their start and end apart: 34, of which 13 were waited for; matrix products, arithmetic and copies ran while one was open for 5% of the time, Pallas kernels for 25%

profile of v6, /device:TPU:0, one launch (start us, length us, event | category | flops | bytes accessed | tf_op | source)
XLA Modules:
  0.0 200.9 jit_solution(4322152662600963183)
XLA Ops:
  2.8 4.5 %collective-permute-start.6 = (bf16[1040,128]{1,0:T(8,128)(2,1)S(1)}, bf16[1040,128]{1,0:T(8,128)(2,1)S(1)}, u32[]{:S(2)}, u32[]{:S(2)}) collective-permute-start(bf16[1040,128]{1,0:T(8,128)(2,1)S(1)} %pad_maximum_fusion.refs_0_), channel_id=1, source_target_pairs={{0,112},{16,64},{32,80},{48,96},{64,48},{80,0},{96,16},{112,32},{1... | collective-permute-start | bytes 798728 | tf_op jit(solution)/shard_map/ppermute | solution.py:337
  7.3 3.1 %collective-permute-start.4 = (bf16[1040,128]{1,0:T(8,128)(2,1)S(1)}, bf16[1040,128]{1,0:T(8,128)(2,1)S(1)}, u32[]{:S(2)}, u32[]{:S(2)}) collective-permute-start(bf16[1040,128]{1,0:T(8,128)(2,1)S(1)} %pad_maximum_fusion.refs_0_), channel_id=1, source_target_pairs={{0,96},{16,112},{32,64},{48,80},{64,32},{80,48},{96,0},{112,16},{1... | collective-permute-start | bytes 798728 | tf_op jit(solution)/shard_map/ppermute | solution.py:337
  12.0 12.4 %collective-permute-done.6.refs_7_ = bf16[1040,128]{1,0:T(8,128)(2,1)S(1)} collective-permute-done((bf16[1040,128]{1,0:T(8,128)(2,1)S(1)}, bf16[1040,128]{1,0:T(8,128)(2,1)S(1)}, u32[]{:S(2)}, u32[]{:S(2)}) %collective-permute-start.6) | collective-permute-done | bytes 266272 | tf_op jit(solution)/shard_map/ppermute | solution.py:337
  24.4 5.0 %collective-permute-start = (bf16[1040,128]{1,0:T(8,128)(2,1)S(1)}, bf16[1040,128]{1,0:T(8,128)(2,1)S(1)}, u32[]{:S(2)}, u32[]{:S(2)}) collective-permute-start(bf16[1040,128]{1,0:T(8,128)(2,1)S(1)} %pad_maximum_fusion.refs_0_), channel_id=1, source_target_pairs={{0,32},{16,48},{32,0},{48,16},{64,96},{80,112},{96,64},{112,80},{1... | collective-permute-start | bytes 798728 | tf_op jit(solution)/shard_map/ppermute | solution.py:337
  29.4 5.3 %collective-permute-done.2.refs_3_ = bf16[1040,128]{1,0:T(8,128)(2,1)S(1)} collective-permute-done((bf16[1040,128]{1,0:T(8,128)(2,1)S(1)}, bf16[1040,128]{1,0:T(8,128)(2,1)S(1)}, u32[]{:S(2)}, u32[]{:S(2)}) %collective-permute-start.2) | collective-permute-done | bytes 266272 | tf_op jit(solution)/shard_map/ppermute | solution.py:337
  34.7 5.1 %collective-permute-done.refs_1_ = bf16[1040,128]{1,0:T(8,128)(2,1)S(1)} collective-permute-done((bf16[1040,128]{1,0:T(8,128)(2,1)S(1)}, bf16[1040,128]{1,0:T(8,128)(2,1)S(1)}, u32[]{:S(2)}, u32[]{:S(2)}) %collective-permute-start) | collective-permute-done | bytes 266272 | tf_op jit(solution)/shard_map/ppermute | solution.py:337
  40.6 3.0 %shard_map.95.first_ref = bf16[8,1040,128]{2,1,0:T(8,128)(2,1)} custom-call(bf16[1040,128]{1,0:T(8,128)(2,1)} %copy-done.12, bf16[1040,128]{1,0:T(8,128)(2,1)} %copy-done.19, bf16[1040,128]{1,0:T(8,128)(2,1)} %copy-done.18, bf16[1040,128]{1,0:T(8,128)(2,1)} %copy-done.17, bf16[1040,128]{1,0:T(8,128)(2,1)} %copy-done.16, bf16[1040,128]{1,0:T(8,128)(2,1)} %copy-done.15, ...), custom_call_target="tpu_custom_call" | custom-call | tf_op jit(solution)/shard_map/pallas_call | solution.py:183
  46.9 3.0 %constant_dynamic-slice_fusion.2 = (bf16[512,1024]{1,0:T(8,128)(2,1)}, bf16[512,1024]{1,0:T(8,128)(2,1)}) fusion(bf16[512,8192]{1,0:T(8,128)(2,1)} %param.12, s32[]{:T(128)S(6)} %select_n.47, s32[]{:T(128)S(6)} %select_n.46), kind=kLoop, calls=%fused_computation.9 | loop fusion | bytes 4194312 | tf_op jit(solution)/shard_map/dynamic_slice | solution.py:358
  51.5 5.0 %constant_dynamic-slice_fusion.4 = (bf16[512,2048]{1,0:T(8,128)(2,1)}, bf16[512,2048]{1,0:T(8,128)(2,1)}) fusion(bf16[512,8192]{1,0:T(8,128)(2,1)} %param.12, s32[]{:T(128)S(6)} %select_n.45, s32[]{:T(128)S(6)} %select_n.44), kind=kLoop, calls=%fused_computation.11 | loop fusion | bytes 8388616 | tf_op jit(solution)/shard_map/dynamic_slice | solution.py:360
  56.9 2.8 %collective-permute-done.14.refs_0_ = bf16[512,256]{1,0:T(8,128)(2,1)S(1)} collective-permute-done((bf16[512,256]{1,0:T(8,128)(2,1)S(1)}, bf16[512,256]{1,0:T(8,128)(2,1)S(1)}, u32[]{:S(2)}, u32[]{:S(2)}) %collective-permute-start.14) | collective-permute-done | bytes 262176 | tf_op jit(solution)/shard_map/ppermute | solution.py:298
  64.1 16.3 %shard_map.98.refs_0_ = bf16[16,32,512]{2,1,0:T(8,128)(2,1)} custom-call(s32[2]{0:T(128)S(1)} %get-tuple-element.39.own_ref, s32[16]{0:T(128)S(1)} %select_reduce_fusion.loc_ref, s32[1]{0:T(128)} %bitcast.4.core_ref, bf16[16,64,512]{2,1,0:T(8,128)(2,1)S(1)} %bitcast.8, bf16[8,1040,128]{2,1,0:T(8,128)(2,1)S(1)} %copy-done.1, ...), custom_call_target="tpu_custom_call" | custom-call | flops 17179869184 | bytes 4194304 | tf_op jit(solution)/shard_map/pallas_call | solution.py:143
  82.2 16.3 %shard_map.96.refs_0_ = bf16[16,32,512]{2,1,0:T(8,128)(2,1)} custom-call(s32[2]{0:T(128)S(1)} %get-tuple-element.39.own_ref, s32[16]{0:T(128)S(1)} %select_reduce_fusion.loc_ref, s32[1]{0:T(128)} %bitcast.4.core_ref, bf16[16,64,512]{2,1,0:T(8,128)(2,1)S(1)} %bitcast.9, bf16[8,1040,128]{2,1,0:T(8,128)(2,1)S(1)} %copy-done.1, ...), custom_call_target="tpu_custom_call" | custom-call | flops 17179869184 | bytes 4194304 | tf_op jit(solution)/shard_map/pallas_call | solution.py:143
  99.9 16.1 %collective-permute-done.26.refs_2_ = bf16[16,32,512]{2,1,0:T(8,128)(2,1)} collective-permute-done((bf16[16,32,512]{2,1,0:T(8,128)(2,1)}, bf16[16,32,512]{2,1,0:T(8,128)(2,1)}, u32[]{:S(2)}, u32[]{:S(2)}) %collective-permute-start.26) | collective-permute-done | bytes 524320 | tf_op jit(solution)/shard_map/ppermute | solution.py:298
  116.6 9.9 %collective-permute-done.9.refs_2_ = bf16[16,32,512]{2,1,0:T(8,128)(2,1)S(1)} collective-permute-done((bf16[16,32,512]{2,1,0:T(8,128)(2,1)}, bf16[16,32,512]{2,1,0:T(8,128)(2,1)S(1)}, u32[]{:S(2)}, u32[]{:S(2)}) %collective-permute-start.9) | collective-permute-done | bytes 524320 | tf_op jit(solution)/shard_map/ppermute | solution.py:298
  130.2 7.4 %project.3 = (bf16[128,2048]{1,0:T(8,128)(2,1)S(1)}, bf16[128,2048]{1,0:T(8,128)(2,1)S(1)}, bf16[128,2048]{1,0:T(8,128)(2,1)S(1)}, bf16[128,2048]{1,0:T(8,128)(2,1)S(1)}) custom-call(s32[3]{0:T(128)S(1)} %pad_add_fusion.place_ref, bf16[16,32,512]{2,1,0:T(8,128)(2,1)} %shard_map.98.refs_0_, bf16[16,32,512]{2,1,0:T(8,128)(2,1)S(1)} %collective-permute-done.25.refs_1_, ...), custom_call_target="tpu_custom_call" | custom-call | flops 4294967296 | bytes 8388608 | tf_op jit(solution)/shard_map/project/pallas_call | solution.py:220
  137.6 3.1 %collective-permute-start.28 = (bf16[128,2048]{1,0:T(8,128)(2,1)S(1)}, bf16[128,2048]{1,0:T(8,128)(2,1)S(1)}, u32[]{:S(2)}, u32[]{:S(2)}) collective-permute-start(bf16[128,2048]{1,0:T(8,128)(2,1)S(1)} %get-tuple-element.29), channel_id=1, source_target_pairs={{0,4},{1,5},{2,6},{3,7},{4,0},{5,1},{6,2},{7,3},{8,12},{9,13},{10,... | collective-permute-start | bytes 1572872 | tf_op jit(solution)/shard_map/ppermute | solution.py:298
  140.7 3.9 %collective-permute-start.29 = (bf16[128,2048]{1,0:T(8,128)(2,1)S(1)}, bf16[128,2048]{1,0:T(8,128)(2,1)S(1)}, u32[]{:S(2)}, u32[]{:S(2)}) collective-permute-start(bf16[128,2048]{1,0:T(8,128)(2,1)S(1)} %get-tuple-element.30), channel_id=1, source_target_pairs={{0,8},{1,9},{2,10},{3,11},{4,12},{5,13},{6,14},{7,15},{8,0},{9,1},... | collective-permute-start | bytes 1572872 | tf_op jit(solution)/shard_map/ppermute | solution.py:298
  144.6 7.2 %project.2 = (bf16[128,2048]{1,0:T(8,128)(2,1)S(1)}, bf16[128,2048]{1,0:T(8,128)(2,1)S(1)}, bf16[128,2048]{1,0:T(8,128)(2,1)S(1)}, bf16[128,2048]{1,0:T(8,128)(2,1)S(1)}) custom-call(s32[3]{0:T(128)S(1)} %pad_add_fusion.place_ref, bf16[16,32,512]{2,1,0:T(8,128)(2,1)} %shard_map.96.refs_0_, bf16[16,32,512]{2,1,0:T(8,128)(2,1)S(1)} %collective-permute-done.8.refs_1_, ...), custom_call_target="tpu_custom_call" | custom-call | flops 4294967296 | bytes 8388608 | tf_op jit(solution)/shard_map/project/pallas_call | solution.py:220
  151.7 3.0 %collective-permute-start.19 = (bf16[128,2048]{1,0:T(8,128)(2,1)S(1)}, bf16[128,2048]{1,0:T(8,128)(2,1)S(1)}, u32[]{:S(2)}, u32[]{:S(2)}) collective-permute-start(bf16[128,2048]{1,0:T(8,128)(2,1)S(1)} %get-tuple-element.21), channel_id=1, source_target_pairs={{0,4},{1,5},{2,6},{3,7},{4,0},{5,1},{6,2},{7,3},{8,12},{9,13},{10,... | collective-permute-start | bytes 1572872 | tf_op jit(solution)/shard_map/ppermute | solution.py:298
  154.8 3.5 %collective-permute-start.20 = (bf16[128,2048]{1,0:T(8,128)(2,1)S(1)}, bf16[128,2048]{1,0:T(8,128)(2,1)S(1)}, u32[]{:S(2)}, u32[]{:S(2)}) collective-permute-start(bf16[128,2048]{1,0:T(8,128)(2,1)S(1)} %get-tuple-element.22), channel_id=1, source_target_pairs={{0,8},{1,9},{2,10},{3,11},{4,12},{5,13},{6,14},{7,15},{8,0},{9,1},... | collective-permute-start | bytes 1572872 | tf_op jit(solution)/shard_map/ppermute | solution.py:298
  160.3 7.8 %collective-permute-done.29.refs_2_ = bf16[128,2048]{1,0:T(8,128)(2,1)S(1)} collective-permute-done((bf16[128,2048]{1,0:T(8,128)(2,1)S(1)}, bf16[128,2048]{1,0:T(8,128)(2,1)S(1)}, u32[]{:S(2)}, u32[]{:S(2)}) %collective-permute-start.29) | collective-permute-done | bytes 524320 | tf_op jit(solution)/shard_map/ppermute | solution.py:298
  170.5 6.0 %collective-permute-done.19.refs_1_ = bf16[128,2048]{1,0:T(8,128)(2,1)S(1)} collective-permute-done((bf16[128,2048]{1,0:T(8,128)(2,1)S(1)}, bf16[128,2048]{1,0:T(8,128)(2,1)S(1)}, u32[]{:S(2)}, u32[]{:S(2)}) %collective-permute-start.19) | collective-permute-done | bytes 524320 | tf_op jit(solution)/shard_map/ppermute | solution.py:298
  176.7 13.1 %collective-permute-done.20.refs_2_ = bf16[128,2048]{1,0:T(8,128)(2,1)S(1)} collective-permute-done((bf16[128,2048]{1,0:T(8,128)(2,1)S(1)}, bf16[128,2048]{1,0:T(8,128)(2,1)S(1)}, u32[]{:S(2)}, u32[]{:S(2)}) %collective-permute-start.20) | collective-permute-done | bytes 524320 | tf_op jit(solution)/shard_map/ppermute | solution.py:298
  195.3 2.5 %collective-permute-done.23.c = bf16[32,2048]{1,0:T(8,128)(2,1)S(1)} collective-permute-done((bf16[32,2048]{1,0:T(8,128)(2,1)S(1)}, bf16[32,2048]{1,0:T(8,128)(2,1)S(1)}, u32[]{:S(2)}, u32[]{:S(2)}) %collective-permute-start.23) | collective-permute-done | bytes 131104 | tf_op jit(solution)/shard_map/ppermute | solution.py:298
  (110 shorter events, 33.8 us)
Async XLA Ops:
  2.8 21.7 %collective-permute-start.6 = (bf16[1040,128]{1,0:T(8,128)(2,1)S(1)}, bf16[1040,128]{1,0:T(8,128)(2,1)S(1)}, u32[]{:S(2)}, u32[]{:S(2)}) collective-permute-start(bf16[1040,128]{1,0:T(8,128)(2,1)S(1)} %pad_maximum_fusion.refs_0_), channel_id=1, source_target_pairs={{0,112},{16,64},{32,80},{48,96},{64,48},{80,0},{96,16},{112,32},{1... | collective-permute-start | bytes 798728 | tf_op jit(solution)/shard_map/ppermute | solution.py:337
  7.3 22.1 %collective-permute-start.4 = (bf16[1040,128]{1,0:T(8,128)(2,1)S(1)}, bf16[1040,128]{1,0:T(8,128)(2,1)S(1)}, u32[]{:S(2)}, u32[]{:S(2)}) collective-permute-start(bf16[1040,128]{1,0:T(8,128)(2,1)S(1)} %pad_maximum_fusion.refs_0_), channel_id=1, source_target_pairs={{0,96},{16,112},{32,64},{48,80},{64,32},{80,48},{96,0},{112,16},{1... | collective-permute-start | bytes 798728 | tf_op jit(solution)/shard_map/ppermute | solution.py:337
  10.4 19.0 %collective-permute-start.3 = (bf16[1040,128]{1,0:T(8,128)(2,1)S(1)}, bf16[1040,128]{1,0:T(8,128)(2,1)S(1)}, u32[]{:S(2)}, u32[]{:S(2)}) collective-permute-start(bf16[1040,128]{1,0:T(8,128)(2,1)S(1)} %pad_maximum_fusion.refs_0_), channel_id=1, source_target_pairs={{0,64},{16,80},{32,96},{48,112},{64,0},{80,16},{96,32},{112,48},{1... | collective-permute-start | bytes 798728 | tf_op jit(solution)/shard_map/ppermute | solution.py:337
  10.5 24.2 %collective-permute-start.2 = (bf16[1040,128]{1,0:T(8,128)(2,1)S(1)}, bf16[1040,128]{1,0:T(8,128)(2,1)S(1)}, u32[]{:S(2)}, u32[]{:S(2)}) collective-permute-start(bf16[1040,128]{1,0:T(8,128)(2,1)S(1)} %pad_maximum_fusion.refs_0_), channel_id=1, source_target_pairs={{0,48},{16,0},{32,16},{48,32},{64,112},{80,64},{96,80},{112,96},{1... | collective-permute-start | bytes 798728 | tf_op jit(solution)/shard_map/ppermute | solution.py:337
  43.6 19.2 %collective-permute-start.7 = (bf16[8,1040,128]{2,1,0:T(8,128)(2,1)}, bf16[8,1040,128]{2,1,0:T(8,128)(2,1)}, u32[]{:S(2)}, u32[]{:S(2)}) collective-permute-start(bf16[8,1040,128]{2,1,0:T(8,128)(2,1)} %shard_map.95.first_ref), channel_id=1, source_target_pairs={{0,1},{1,0},{2,3},{3,2},{4,5},{5,4},{6,7},{7,6},{8,9},{9,8},{10,11... | collective-permute-start | bytes 6389768 | tf_op jit(solution)/shard_map/ppermute | solution.py:298
  50.0 49.9 %collective-permute-start.13 = (bf16[512,1024]{1,0:T(8,128)(2,1)}, bf16[512,1024]{1,0:T(8,128)(2,1)}, u32[]{:S(2)}, u32[]{:S(2)}) collective-permute-start(bf16[512,1024]{1,0:T(8,128)(2,1)} %get-tuple-element.42), channel_id=1, source_target_pairs={{0,3},{1,2},{2,1},{3,0},{4,7},{5,6},{6,5},{7,4},{8,11},{9,10},{10,... | collective-permute-start | bytes 3145736 | tf_op jit(solution)/shard_map/ppermute | solution.py:298
  50.8 65.2 %collective-permute-start.12 = (bf16[512,1024]{1,0:T(8,128)(2,1)}, bf16[512,1024]{1,0:T(8,128)(2,1)}, u32[]{:S(2)}, u32[]{:S(2)}) collective-permute-start(bf16[512,1024]{1,0:T(8,128)(2,1)} %get-tuple-element.43), channel_id=1, source_target_pairs={{0,2},{1,3},{2,0},{3,1},{4,6},{5,7},{6,4},{7,5},{8,10},{9,11},{10,... | collective-permute-start | bytes 3145736 | tf_op jit(solution)/shard_map/ppermute | solution.py:298
  56.5 70.0 %collective-permute-start.11 = (bf16[512,2048]{1,0:T(8,128)(2,1)}, bf16[512,2048]{1,0:T(8,128)(2,1)}, u32[]{:S(2)}, u32[]{:S(2)}) collective-permute-start(bf16[512,2048]{1,0:T(8,128)(2,1)} %get-tuple-element.44), channel_id=1, source_target_pairs={{0,1},{1,0},{2,3},{3,2},{4,5},{5,4},{6,7},{7,6},{8,9},{9,8},{10,11... | collective-permute-start | bytes 6291464 | tf_op jit(solution)/shard_map/ppermute | solution.py:298
  62.3 18.2 %collective-permute-start.18 = (bf16[2,512,256]{2,1,0:T(8,128)(2,1)}, bf16[2,512,256]{2,1,0:T(8,128)(2,1)S(1)}, u32[]{:S(2)}, u32[]{:S(2)}) collective-permute-start(bf16[2,512,256]{2,1,0:T(8,128)(2,1)} %shard_map.97.refs_8_), channel_id=1, source_target_pairs={{0,48},{16,0},{32,16},{48,32},{64,112},{80,64},{96,80},{112,96},{1... | collective-permute-start | bytes 1572872 | tf_op jit(solution)/shard_map/ppermute | solution.py:355
  62.8 17.7 %collective-permute-start.17 = (bf16[2,512,256]{2,1,0:T(8,128)(2,1)}, bf16[2,512,256]{2,1,0:T(8,128)(2,1)S(1)}, u32[]{:S(2)}, u32[]{:S(2)}) collective-permute-start(bf16[2,512,256]{2,1,0:T(8,128)(2,1)} %shard_map.97.refs_8_), channel_id=1, source_target_pairs={{0,32},{16,48},{32,0},{48,16},{64,96},{80,112},{96,64},{112,80},{1... | collective-permute-start | bytes 1572872 | tf_op jit(solution)/shard_map/ppermute | solution.py:355
  80.5 18.1 %collective-permute-start.16 = (bf16[2,512,256]{2,1,0:T(8,128)(2,1)S(1)}, bf16[2,512,256]{2,1,0:T(8,128)(2,1)S(1)}, u32[]{:S(2)}, u32[]{:S(2)}) collective-permute-start(bf16[2,512,256]{2,1,0:T(8,128)(2,1)S(1)} %copy-done.3), channel_id=1, source_target_pairs={{0,16},{16,32},{32,48},{48,0},{64,80},{80,96},{96,112},{112,64},{1... | collective-permute-start | bytes 1572872 | tf_op jit(solution)/shard_map/ppermute | solution.py:355
  80.5 35.5 %collective-permute-start.26 = (bf16[16,32,512]{2,1,0:T(8,128)(2,1)}, bf16[16,32,512]{2,1,0:T(8,128)(2,1)}, u32[]{:S(2)}, u32[]{:S(2)}) collective-permute-start(bf16[16,32,512]{2,1,0:T(8,128)(2,1)} %shard_map.98.refs_0_), channel_id=1, source_target_pairs={{0,2},{1,3},{2,0},{3,1},{4,6},{5,7},{6,4},{7,5},{8,10},{9,11},{10,... | collective-permute-start | bytes 1572872 | tf_op jit(solution)/shard_map/ppermute | solution.py:298
  99.4 27.1 %collective-permute-start.9 = (bf16[16,32,512]{2,1,0:T(8,128)(2,1)}, bf16[16,32,512]{2,1,0:T(8,128)(2,1)S(1)}, u32[]{:S(2)}, u32[]{:S(2)}) collective-permute-start(bf16[16,32,512]{2,1,0:T(8,128)(2,1)} %shard_map.96.refs_0_), channel_id=1, source_target_pairs={{0,2},{1,3},{2,0},{3,1},{4,6},{5,7},{6,4},{7,5},{8,10},{9,11},{10,... | collective-permute-start | bytes 1572872 | tf_op jit(solution)/shard_map/ppermute | solution.py:298
  99.9 26.6 %collective-permute-start.25 = (bf16[16,32,512]{2,1,0:T(8,128)(2,1)}, bf16[16,32,512]{2,1,0:T(8,128)(2,1)S(1)}, u32[]{:S(2)}, u32[]{:S(2)}) collective-permute-start(bf16[16,32,512]{2,1,0:T(8,128)(2,1)} %shard_map.98.refs_0_), channel_id=1, source_target_pairs={{0,1},{1,0},{2,3},{3,2},{4,5},{5,4},{6,7},{7,6},{8,9},{9,8},{10,11... | collective-permute-start | bytes 1572872 | tf_op jit(solution)/shard_map/ppermute | solution.py:298
  116.1 28.5 %collective-permute-start.8 = (bf16[16,32,512]{2,1,0:T(8,128)(2,1)}, bf16[16,32,512]{2,1,0:T(8,128)(2,1)S(1)}, u32[]{:S(2)}, u32[]{:S(2)}) collective-permute-start(bf16[16,32,512]{2,1,0:T(8,128)(2,1)} %shard_map.96.refs_0_), channel_id=1, source_target_pairs={{0,1},{1,0},{2,3},{3,2},{4,5},{5,4},{6,7},{7,6},{8,9},{9,8},{10,11... | collective-permute-start | bytes 1572872 | tf_op jit(solution)/shard_map/ppermute | solution.py:298
  126.5 18.1 %collective-permute-start.10 = (bf16[16,32,512]{2,1,0:T(8,128)(2,1)S(1)}, bf16[16,32,512]{2,1,0:T(8,128)(2,1)S(1)}, u32[]{:S(2)}, u32[]{:S(2)}) collective-permute-start(bf16[16,32,512]{2,1,0:T(8,128)(2,1)S(1)} %collective-permute-done.9.refs_2_), channel_id=1, source_target_pairs={{0,1},{1,0},{2,3},{3,2},{4,5},{5,4},{6,7},{7,6},{8,9},{9,8},{10,11... | collective-permute-start | bytes 1572872 | tf_op jit(solution)/shard_map/ppermute | solution.py:298
  137.6 20.7 %collective-permute-start.28 = (bf16[128,2048]{1,0:T(8,128)(2,1)S(1)}, bf16[128,2048]{1,0:T(8,128)(2,1)S(1)}, u32[]{:S(2)}, u32[]{:S(2)}) collective-permute-start(bf16[128,2048]{1,0:T(8,128)(2,1)S(1)} %get-tuple-element.29), channel_id=1, source_target_pairs={{0,4},{1,5},{2,6},{3,7},{4,0},{5,1},{6,2},{7,3},{8,12},{9,13},{10,... | collective-permute-start | bytes 1572872 | tf_op jit(solution)/shard_map/ppermute | solution.py:298
  140.7 27.4 %collective-permute-start.29 = (bf16[128,2048]{1,0:T(8,128)(2,1)S(1)}, bf16[128,2048]{1,0:T(8,128)(2,1)S(1)}, u32[]{:S(2)}, u32[]{:S(2)}) collective-permute-start(bf16[128,2048]{1,0:T(8,128)(2,1)S(1)} %get-tuple-element.30), channel_id=1, source_target_pairs={{0,8},{1,9},{2,10},{3,11},{4,12},{5,13},{6,14},{7,15},{8,0},{9,1},... | collective-permute-start | bytes 1572872 | tf_op jit(solution)/shard_map/ppermute | solution.py:298
  144.5 24.0 %collective-permute-start.30 = (bf16[128,2048]{1,0:T(8,128)(2,1)S(1)}, bf16[128,2048]{1,0:T(8,128)(2,1)S(1)}, u32[]{:S(2)}, u32[]{:S(2)}) collective-permute-start(bf16[128,2048]{1,0:T(8,128)(2,1)S(1)} %get-tuple-element.31), channel_id=1, source_target_pairs={{0,12},{1,13},{2,14},{3,15},{4,8},{5,9},{6,10},{7,11},{8,4},{9,5},... | collective-permute-start | bytes 1572872 | tf_op jit(solution)/shard_map/ppermute | solution.py:298
  151.7 24.7 %collective-permute-start.19 = (bf16[128,2048]{1,0:T(8,128)(2,1)S(1)}, bf16[128,2048]{1,0:T(8,128)(2,1)S(1)}, u32[]{:S(2)}, u32[]{:S(2)}) collective-permute-start(bf16[128,2048]{1,0:T(8,128)(2,1)S(1)} %get-tuple-element.21), channel_id=1, source_target_pairs={{0,4},{1,5},{2,6},{3,7},{4,0},{5,1},{6,2},{7,3},{8,12},{9,13},{10,... | collective-permute-start | bytes 1572872 | tf_op jit(solution)/shard_map/ppermute | solution.py:298
  154.8 35.1 %collective-permute-start.20 = (bf16[128,2048]{1,0:T(8,128)(2,1)S(1)}, bf16[128,2048]{1,0:T(8,128)(2,1)S(1)}, u32[]{:S(2)}, u32[]{:S(2)}) collective-permute-start(bf16[128,2048]{1,0:T(8,128)(2,1)S(1)} %get-tuple-element.22), channel_id=1, source_target_pairs={{0,8},{1,9},{2,10},{3,11},{4,12},{5,13},{6,14},{7,15},{8,0},{9,1},... | collective-permute-start | bytes 1572872 | tf_op jit(solution)/shard_map/ppermute | solution.py:298
  158.3 32.7 %collective-permute-start.21 = (bf16[128,2048]{1,0:T(8,128)(2,1)S(1)}, bf16[128,2048]{1,0:T(8,128)(2,1)S(1)}, u32[]{:S(2)}, u32[]{:S(2)}) collective-permute-start(bf16[128,2048]{1,0:T(8,128)(2,1)S(1)} %get-tuple-element.23), channel_id=1, source_target_pairs={{0,12},{1,13},{2,14},{3,15},{4,8},{5,9},{6,10},{7,11},{8,4},{9,5},... | collective-permute-start | bytes 1572872 | tf_op jit(solution)/shard_map/ppermute | solution.py:298
  168.8 24.1 %collective-permute-start.31 = (bf16[32,2048]{1,0:T(8,128)(2,1)S(1)}, bf16[32,2048]{1,0:T(8,128)(2,1)S(1)}, u32[]{:S(2)}, u32[]{:S(2)}) collective-permute-start(bf16[32,2048]{1,0:T(8,128)(2,1)S(1)} %get-tuple-element.33), channel_id=1, source_target_pairs={{0,1},{1,0},{2,3},{3,2},{4,5},{5,4},{6,7},{7,6},{8,9},{9,8},{10,11... | collective-permute-start | bytes 393224 | tf_op jit(solution)/shard_map/ppermute | solution.py:298
  168.9 24.9 %collective-permute-start.32 = (bf16[32,2048]{1,0:T(8,128)(2,1)S(1)}, bf16[32,2048]{1,0:T(8,128)(2,1)S(1)}, u32[]{:S(2)}, u32[]{:S(2)}) collective-permute-start(bf16[32,2048]{1,0:T(8,128)(2,1)S(1)} %get-tuple-element.34), channel_id=1, source_target_pairs={{0,2},{1,3},{2,0},{3,1},{4,6},{5,7},{6,4},{7,5},{8,10},{9,11},{10,... | collective-permute-start | bytes 393224 | tf_op jit(solution)/shard_map/ppermute | solution.py:298
  (32 other events, 347.0 us)
